TPU v7x, 32 devices: a whole 2x2x4 slice. The times are simulated.
32 devices in a mesh: seq: 8 (over z, x), tp: 4 (over y, core).
Axes of the slice: x: 2, y: 2, z: 4, core: 2. Of those that a mesh axis runs over, the one named last changes fastest.
Arguments:
- query_rows: bfloat16 [1536, 4096], P('seq', 'tp'), may hold values from -120 to 120
- key_rows: bfloat16 [1536, 1024], P('seq', 'tp'), may hold values from -6 to 6
- value_rows: bfloat16 [1536, 1024], P('seq', 'tp'), may hold values from -6 to 6
- document_ids: int32 [1536], replicated, may hold values from 0 to 3, never falling along the last dimension, each value on 1 to 768 neighbouring positions
- output_weight: bfloat16 [4096, 8192], P('tp'), may hold values from -0.09375 to 0.09375
Outputs:
- attended: bfloat16 [1536, 8192], P(('seq', 'tp'))
Inputs may be any that keep to these rules, and one draw needn't show every extreme that they name: `document_ids`: never falling along the sequence; every document holds at most 768 tokens, and one holds exactly 768.
All inputs are finite; a program needn't handle non-finite values.
Results may differ from a plain program's by a relative error of at most 0.014.
Values may be sent and summed in bfloat16 or wider, within the bound.
No kernel may reach another device: no remote copies, remote signals or barrier semaphores. Data moves between devices by JAX's collectives and lax.ppermute only.
A program may use at most 64 MiB of HBM per device.

v0:
```python
import functools

import jax
import jax.numpy as jnp
from jax import lax
from jax.experimental import pallas as pl
from jax.experimental.pallas import tpu as pltpu
from jax.sharding import PartitionSpec as P


HEADS = 32
KV = 8
HD = 128
AXES = ("seq", "tp")
LOG2E = 1.4426950408889634
SCALE = LOG2E / HD**0.5
VMEM = pl.BlockSpec(memory_space=pltpu.VMEM)
ANY = pl.BlockSpec(memory_space=pl.ANY)
MIB = 1 << 20


def routes(seq, tp):
    rows = seq // 2

    def flat(rule):
        pairs = []
        for s in range(seq):
            for t in range(tp):
                s2, t2 = rule(s, t)
                pairs.append((s * tp + t, s2 * tp + t2))
        return pairs

    def by_row(parity):
        def rule(s, t):
            row, col = divmod(s, 2)
            other = row + 1 if row % 2 == parity else row - 1
            if 0 <= other < rows:
                return other * 2 + col, t
            return s, t ^ 1

        return flat(rule)

    return {
        "even": by_row(0),
        "odd": by_row(1),
        "col": flat(lambda s, t: (s ^ 1, t)),
        "core": flat(lambda s, t: (s, t ^ 1)),
    }


def y_route(seq, tp, distance):
    pairs = []
    for s in range(seq):
        for t in range(tp):
            pairs.append((s * tp + t, s * tp + (t + 2 * distance) % tp))
    return pairs


def join_kernel(k_ref, v_ref, out_ref, sems):
    width = k_ref.shape[1]
    copies = [
        pltpu.make_async_copy(k_ref, out_ref.at[:, pl.ds(0, width)], sems.at[0]),
        pltpu.make_async_copy(v_ref, out_ref.at[:, pl.ds(width, width)], sems.at[1]),
    ]
    for copy in copies:
        copy.start()
    for copy in copies:
        copy.wait()


def query_doc(docs_t_ref, me):
    docs = docs_t_ref[...]
    lane = lax.broadcasted_iota(jnp.int32, docs.shape, 1)
    return jnp.sum(jnp.where(lane == me, docs, 0.0), axis=1, keepdims=True)


def key_doc(docs_ref, block, me):
    row = docs_ref[pl.ds(jnp.maximum(block, 0), 1), :]
    return jnp.where((block >= 0) & (block <= me), row, -1.0)


def stack(q_ref, h, group):
    return jnp.concatenate(
        [q_ref[:, pl.ds((h * group + g) * HD, HD)] for g in range(group)], axis=0
    )


def scores_of(queries, keys):
    return lax.dot_general(
        queries, keys, (((1,), (1,)), ((), ())), preferred_element_type=jnp.float32
    )


def early_kernel(kv_local, group, count, step, *refs):
    q_ref, docs_ref, docs_t_ref = refs[:3]
    blocks = refs[3 : 3 + count]
    w_hbm = refs[3 + count]
    acc_ref, top_ref, sum_ref, w_ref = refs[4 + count : 8 + count]
    bias_ref, s_ref, p_ref, sem = refs[8 + count :]
    copy = pltpu.make_async_copy(w_hbm, w_ref, sem)
    copy.start()
    tokens = q_ref.shape[0]
    stacked = group * tokens
    me = lax.axis_index("seq")
    row, col = me // 2, me % 2
    docs = []
    for i in range(count):
        block = me - i if i % 2 == 0 else (row - i // 2) * 2 + 1 - col
        docs.append(key_doc(docs_ref, block, me))
    allowed = query_doc(docs_t_ref, me) == jnp.concatenate(docs, axis=1)
    key_at = lax.broadcasted_iota(jnp.int32, (tokens, count * tokens), 1)
    query_at = lax.broadcasted_iota(jnp.int32, (tokens, count * tokens), 0)
    allowed = allowed & ((key_at <= query_at) | (key_at >= tokens))
    bias_ref[...] = jnp.where(allowed, 0.0, -jnp.inf)
    for h in range(kv_local):
        keys = jnp.concatenate([b[:, pl.ds(h * HD, HD)] for b in blocks], axis=0)
        s_ref[...] = scores_of(stack(q_ref, h, group), keys)
        for r in range(0, stacked, step):
            at = pl.ds(r, step)
            into = pl.ds(h * stacked + r, step)
            scores = s_ref[at, :] * SCALE + bias_ref[pl.ds(r % tokens, step), :]
            top = jnp.max(scores, axis=-1, keepdims=True)
            weight = jnp.exp2(scores - top)
            total = jnp.sum(weight, axis=-1, keepdims=True)
            p_ref[at, :] = weight.astype(jnp.bfloat16)
            top_ref[into, :] = jnp.broadcast_to(top, (step, HD))
            sum_ref[into, :] = jnp.broadcast_to(total, (step, HD))
        cols = pl.ds((kv_local + h) * HD, HD)
        values = jnp.concatenate([b[:, cols] for b in blocks], axis=0)
        acc_ref[pl.ds(h * stacked, stacked), :] = jnp.dot(
            p_ref[...], values, preferred_element_type=jnp.float32
        )
    copy.wait()


def project(context_ref, w_ref, start, width, send_ref, keep_ref, part):
    step = 512
    for c in range(0, width, step):
        at = pl.ds(c, step)
        rows = jnp.dot(
            context_ref[...],
            w_ref[:, pl.ds(start + c, step)],
            preferred_element_type=jnp.float32,
        ).astype(jnp.bfloat16)
        for i in range(rows.shape[0] // (2 * part)):
            into = pl.ds(i * part, part)
            keep_ref[into, at] = rows[2 * i * part : (2 * i + 1) * part]
            send_ref[into, at] = rows[(2 * i + 1) * part : (2 * i + 2) * part]


def late_kernel(kv_local, group, part, depth, *refs):
    q_ref, docs_ref, docs_t_ref, block, acc_ref, top_ref, sum_ref, w_ref = refs[:8]
    out_ref, send_ref, keep_ref, context_ref = refs[8:]
    tokens = q_ref.shape[0]
    stacked = group * tokens
    me, rank = lax.axis_index("seq"), lax.axis_index("tp")
    chips = lax.axis_size("tp") // 2
    far = (me // 2 - depth) * 2 + 1 - me % 2
    bias = jnp.where(
        query_doc(docs_t_ref, me) == key_doc(docs_ref, far, me), 0.0, -jnp.inf
    )
    for h in range(kv_local):
        keys = block[:, pl.ds(h * HD, HD)]
        values = block[:, pl.ds((kv_local + h) * HD, HD)]
        scores = scores_of(stack(q_ref, h, group), keys)
        scores = scores * SCALE + jnp.concatenate([bias] * group, axis=0)
        at = pl.ds(h * stacked, stacked)
        old = top_ref[at, :]
        new = jnp.maximum(old[:, :1], jnp.max(scores, axis=-1, keepdims=True))
        weight = jnp.exp2(scores - new)
        rescale = jnp.exp2(old - new)
        total = sum_ref[at, :] * rescale + jnp.sum(weight, axis=-1, keepdims=True)
        added = jnp.dot(
            weight.astype(jnp.bfloat16), values, preferred_element_type=jnp.float32
        )
        context = (acc_ref[at, :] * rescale + added) / total
        context = context.astype(jnp.bfloat16)
        for g in range(group):
            cols = pl.ds((h * group + g) * HD, HD)
            context_ref[:, cols] = context[g * tokens : (g + 1) * tokens]
    at = 0
    for distance in range(1, chips + 1):
        base = lax.rem(rank // 2 + distance, chips) * 2
        for core in (rank % 2, 1 - rank % 2):
            first = pl.multiple_of((base + core) * part, 8)
            out_ref[pl.ds(at, part), :] = context_ref[pl.ds(first, part), :]
            at += part
    project(out_ref, w_ref, 0, send_ref.shape[1], send_ref, keep_ref, part)


def project_kernel(part, start, context_ref, w_ref, send_ref, keep_ref):
    width = send_ref.shape[1]
    project(context_ref, w_ref, start, width, send_ref, keep_ref, part)


def project_call(context, weight, start, width, part):
    tokens, depth = context.shape
    out = jax.ShapeDtypeStruct((tokens // 2, width), jnp.bfloat16)
    return pl.pallas_call(
        functools.partial(project_kernel, part, start),
        out_shape=(out, out),
        in_specs=[VMEM, VMEM],
        out_specs=(VMEM, VMEM),
        cost_estimate=pl.CostEstimate(
            flops=2 * tokens * depth * width,
            transcendentals=0,
            bytes_accessed=2 * depth * width,
        ),
        compiler_params=pltpu.CompilerParams(vmem_limit_bytes=8 * MIB),
        name="project_rest",
    )(context, weight)


def layer(query_rows, key_rows, value_rows, document_ids, output_weight):
    tokens = query_rows.shape[0]
    kv_local = key_rows.shape[1] // HD
    group = HEADS // KV
    width = query_rows.shape[1]
    model = output_weight.shape[1]
    seq, tp = lax.axis_size("seq"), lax.axis_size("tp")
    part = tokens // tp
    chips = tp // 2
    reach = min(12, seq // 2)
    depth = (reach + 1) // 2
    route = routes(seq, tp)
    odd_row = (lax.axis_index("seq") // 2) % 2 == 1

    def send(x, name):
        return lax.ppermute(x, AXES, route[name])

    own = pl.pallas_call(
        join_kernel,
        out_shape=jax.ShapeDtypeStruct((tokens, 2 * kv_local * HD), jnp.bfloat16),
        in_specs=[ANY, ANY],
        out_specs=VMEM,
        scratch_shapes=[pltpu.SemaphoreType.DMA((2,))],
        compiler_params=pltpu.CompilerParams(vmem_limit_bytes=2 * MIB),
        name="join",
    )(key_rows, value_rows)
    docs = document_ids.astype(jnp.float32).reshape(seq, tokens)
    docs_t = docs.T
    even, odd = send(own, "even"), send(own, "odd")
    blocks = [own, send(own, "col")]
    even, odd, docs, docs_t = lax.optimization_barrier((even, odd, docs, docs_t))
    for distance in range(1, depth + 1):
        blocks.append(jnp.where(odd_row, even, odd))
        if distance < depth:
            even, odd = send(odd, "even"), send(even, "odd")
        blocks.append(send(blocks[-1], "col"))
    last_block = blocks.pop()
    count = len(blocks)

    stacked = group * tokens
    state = jax.ShapeDtypeStruct((kv_local * stacked, HD), jnp.float32)
    acc, top, total, weight = pl.pallas_call(
        functools.partial(early_kernel, kv_local, group, count, 32),
        out_shape=(
            state,
            state,
            state,
            pltpu.VMEM(output_weight.shape, output_weight.dtype),
        ),
        in_specs=[VMEM] * (3 + count) + [ANY],
        out_specs=(VMEM,) * 4,
        scratch_shapes=[
            pltpu.VMEM((tokens, count * tokens), jnp.float32),
            pltpu.VMEM((stacked, count * tokens), jnp.float32),
            pltpu.VMEM((stacked, count * tokens), jnp.bfloat16),
            pltpu.SemaphoreType.DMA,
        ],
        cost_estimate=pl.CostEstimate(
            flops=4 * tokens * tokens * count * width,
            transcendentals=tokens * tokens * count * width // HD,
            bytes_accessed=2 * width * model,
        ),
        compiler_params=pltpu.CompilerParams(vmem_limit_bytes=24 * MIB),
        name="attend_early",
    )(query_rows, docs, docs_t, *blocks, output_weight)

    cuts = [model * 3 // 16, model // 2, model]
    out = jax.ShapeDtypeStruct((tokens // 2, cuts[0]), jnp.bfloat16)
    context, sent, kept = pl.pallas_call(
        functools.partial(late_kernel, kv_local, group, part, depth),
        out_shape=(jax.ShapeDtypeStruct((tokens, width), jnp.bfloat16), out, out),
        in_specs=[VMEM] * 8,
        out_specs=(VMEM, VMEM, VMEM),
        scratch_shapes=[pltpu.VMEM((tokens, width), jnp.bfloat16)],
        cost_estimate=pl.CostEstimate(
            flops=4 * tokens * tokens * width + 2 * tokens * width * cuts[0],
            transcendentals=tokens * tokens * width // HD,
            bytes_accessed=4 * tokens * width + 2 * width * cuts[0],
        ),
        compiler_params=pltpu.CompilerParams(vmem_limit_bytes=16 * MIB),
        name="attend_late",
    )(query_rows, docs, docs_t, last_block, acc, top, total, weight)

    pieces = []
    remote = (chips - 1) * part
    for i, stop in enumerate(cuts):
        if i:
            start = cuts[i - 1]
            sent, kept = project_call(context, weight, start, stop - start, part)
        received = send(sent, "core")
        moved = (
            kept[:remote].astype(jnp.float32) + received[:remote].astype(jnp.float32)
        ).astype(jnp.bfloat16)
        context, moved = lax.optimization_barrier((context, moved))
        piece = kept[remote:].astype(jnp.float32) + received[remote:].astype(
            jnp.float32
        )
        for distance in range(1, chips):
            at = (distance - 1) * part
            arrived = lax.ppermute(
                moved[at : at + part], AXES, y_route(seq, tp, distance)
            )
            piece = piece + arrived.astype(jnp.float32)
        pieces.append(piece.astype(jnp.bfloat16))
    return jnp.concatenate(pieces, axis=1)


def solution(mesh):
    in_specs = (P("seq", "tp"), P("seq", "tp"), P("seq", "tp"), P(), P("tp", None))
    out_specs = P(("seq", "tp"), None)
    return jax.shard_map(
        layer, mesh=mesh, in_specs=in_specs, out_specs=out_specs, check_vma=False
    )
```

profile of v0, /device:TPU:0, one launch (start us, length us, event | category | flops | bytes accessed | tf_op | source)
XLA Modules:
  0.0 62.2 jit_solution(17031798903528213409)
XLA Ops:
  0.0 0.0 copy-start
  0.0 0.0 copy-start.1
  0.0 0.9 %copy-done.1 = bf16[192,256]{1,0:T(8,128)(2,1)S(1)} copy-done((bf16[192,256]{1,0:T(8,128)(2,1)S(1)}, bf16[192,256]{1,0:T(8,128)(2,1)}, u32[]{:S(2)}) %copy-start.1) | copy-done | bytes 98328
  0.9 0.0 copy-start.2
  0.9 0.9 %copy-done.2 = bf16[192,256]{1,0:T(8,128)(2,1)S(1)} copy-done((bf16[192,256]{1,0:T(8,128)(2,1)S(1)}, bf16[192,256]{1,0:T(8,128)(2,1)}, u32[]{:S(2)}) %copy-start.2) | copy-done | bytes 98328
  1.9 0.6 collective-permute-start.1
  2.4 4.1 %collective-permute-start = (bf16[192,512]{1,0:T(8,128)(2,1)S(1)}, bf16[192,512]{1,0:T(8,128)(2,1)S(1)}, u32[]{:S(2)}, u32[]{:S(2)}) collective-permute-start(bf16[192,512]{1,0:T(8,128)(2,1)S(1)} %join.1.refs_3_), channel_id=1, source_target_pairs={{0,8},{1,9},{2,10},{3,11},{4,12},{5,13},{6,14},{7,15},{8,0},{9,1},... | collective-permute-start | bytes 589832 | tf_op jit(solution)/shard_map/ppermute | solution.py:229
  6.6 1.5 %collective-permute-start.5 = (bf16[192,512]{1,0:T(8,128)(2,1)S(1)}, bf16[192,512]{1,0:T(8,128)(2,1)S(1)}, u32[]{:S(2)}, u32[]{:S(2)}) collective-permute-start(bf16[192,512]{1,0:T(8,128)(2,1)S(1)} %join.1.refs_3_), channel_id=1, source_target_pairs={{0,4},{1,5},{2,6},{3,7},{4,0},{5,1},{6,2},{7,3},{8,12},{9,13},{10,... | collective-permute-start | bytes 589832 | tf_op jit(solution)/shard_map/ppermute | solution.py:229
  8.1 0.7 %convert_element_type.66 = f32[1536]{0:T(1024)S(1)} convert(s32[1536]{0:T(1024)} %param.8) | non-fusion elementwise | flops 1536 | bytes 12288 | tf_op jit(solution)/shard_map/convert_element_type | solution.py:240
  8.8 0.1 reshape.3.refs_1_
  8.8 0.1 copy.8
  9.0 0.0 collective-permute-done.1
  9.0 2.2 %collective-permute-done = bf16[192,512]{1,0:T(8,128)(2,1)S(1)} collective-permute-done((bf16[192,512]{1,0:T(8,128)(2,1)S(1)}, bf16[192,512]{1,0:T(8,128)(2,1)S(1)}, u32[]{:S(2)}, u32[]{:S(2)}) %collective-permute-start) | collective-permute-done | bytes 196640 | tf_op jit(solution)/shard_map/ppermute | solution.py:229
  11.2 1.7 %collective-permute-start.2 = (bf16[192,512]{1,0:T(8,128)(2,1)S(1)}, bf16[192,512]{1,0:T(8,128)(2,1)S(1)}, u32[]{:S(2)}, u32[]{:S(2)}) collective-permute-start(bf16[192,512]{1,0:T(8,128)(2,1)S(1)} %collective-permute-done.1), channel_id=1, source_target_pairs={{0,8},{1,9},{2,10},{3,11},{4,12},{5,13},{6,14},{7,15},{8,0},{9,1},... | collective-permute-start | bytes 589832 | tf_op jit(solution)/shard_map/ppermute | solution.py:229
  12.9 0.0 collective-permute-start.3
  13.0 1.6 %collective-permute-start.6 = (bf16[192,512]{1,0:T(8,128)(2,1)S(1)}, bf16[192,512]{1,0:T(8,128)(2,1)S(1)}, u32[]{:S(2)}, u32[]{:S(2)}) collective-permute-start(bf16[192,512]{1,0:T(8,128)(2,1)S(1)} %broadcast_select_fusion.refs_5_), channel_id=1, source_target_pairs={{0,4},{1,5},{2,6},{3,7},{4,0},{5,1},{6,2},{7,3},{8,12},{9,13},{10,... | collective-permute-start | bytes 589832 | tf_op jit(solution)/shard_map/ppermute | solution.py:229
  14.5 2.5 %collective-permute-done.2 = bf16[192,512]{1,0:T(8,128)(2,1)S(1)} collective-permute-done((bf16[192,512]{1,0:T(8,128)(2,1)S(1)}, bf16[192,512]{1,0:T(8,128)(2,1)S(1)}, u32[]{:S(2)}, u32[]{:S(2)}) %collective-permute-start.2) | collective-permute-done | bytes 196640 | tf_op jit(solution)/shard_map/ppermute | solution.py:229
  17.0 0.0 collective-permute-done.3
  17.0 1.6 %collective-permute-start.4 = (bf16[192,512]{1,0:T(8,128)(2,1)S(1)}, bf16[192,512]{1,0:T(8,128)(2,1)S(1)}, u32[]{:S(2)}, u32[]{:S(2)}) collective-permute-start(bf16[192,512]{1,0:T(8,128)(2,1)S(1)} %broadcast_select_fusion.1.refs_7_), channel_id=1, source_target_pairs={{0,4},{1,5},{2,6},{3,7},{4,0},{5,1},{6,2},{7,3},{8,12},{9,13},{10,... | collective-permute-start | bytes 589832 | tf_op jit(solution)/shard_map/ppermute | solution.py:229
  18.6 0.0 collective-permute-done.5.refs_4_
  18.6 2.2 %collective-permute-done.6.refs_6_ = bf16[192,512]{1,0:T(8,128)(2,1)S(1)} collective-permute-done((bf16[192,512]{1,0:T(8,128)(2,1)S(1)}, bf16[192,512]{1,0:T(8,128)(2,1)S(1)}, u32[]{:S(2)}, u32[]{:S(2)}) %collective-permute-start.6) | collective-permute-done | bytes 196640 | tf_op jit(solution)/shard_map/ppermute | solution.py:229
  20.8 0.0 copy-done
  20.8 8.7 %attend_early.1 = (f32[1536,128]{1,0:T(8,128)S(1)}, f32[1536,128]{1,0:T(8,128)S(1)}, f32[1536,128]{1,0:T(8,128)S(1)}, bf16[1024,8192]{1,0:T(8,128)(2,1)S(1)}) custom-call(bf16[192,1024]{1,0:T(8,128)(2,1)S(1)} %copy-done, f32[8,192]{1,0:T(8,128)S(1)} %reshape.3.refs_1_, f32[192,8]{1,0:T(8,128)S(1)} %bitcast.1, bf16[192,512]{1,0:T(8,128)(2,1)S(1)} %join.1.refs_3_, ...), custom_call_target="tpu_custom_call" | custom-call | flops 754974720 | bytes 16777216 | tf_op jit(solution)/shard_map/attend_early/pallas_call | solution.py:255
  29.5 0.0 collective-permute-done.4.refs_3_
  29.5 2.5 %attend_late.1 = (bf16[192,1024]{1,0:T(8,128)(2,1)S(1)}, bf16[96,1536]{1,0:T(8,128)(2,1)S(1)}, bf16[96,1536]{1,0:T(8,128)(2,1)S(1)}) custom-call(bf16[192,1024]{1,0:T(8,128)(2,1)S(1)} %copy-done, f32[8,192]{1,0:T(8,128)S(1)} %reshape.3.refs_1_, f32[192,8]{1,0:T(8,128)S(1)} %bitcast.2, bf16[192,512]{1,0:T(8,128)(2,1)S(1)} %collective-permute-done.4.refs_3_, ...), custom_call_target="tpu_custom_call" | custom-call | flops 754974720 | bytes 3932160 | tf_op jit(solution)/shard_map/attend_late/pallas_call | solution.py:282
  32.1 0.1 collective-permute-start.7
  32.1 1.6 %collective-permute-done.7 = bf16[96,1536]{1,0:T(8,128)(2,1)S(1)} collective-permute-done((bf16[96,1536]{1,0:T(8,128)(2,1)S(1)}, bf16[96,1536]{1,0:T(8,128)(2,1)S(1)}, u32[]{:S(2)}, u32[]{:S(2)}) %collective-permute-start.7) | collective-permute-done | bytes 294944 | tf_op jit(solution)/shard_map/ppermute | solution.py:229
  33.7 1.2 %project_rest.2 = (bf16[96,2560]{1,0:T(8,128)(2,1)S(1)}, bf16[96,2560]{1,0:T(8,128)(2,1)S(1)}) custom-call(bf16[192,1024]{1,0:T(8,128)(2,1)S(1)} %get-tuple-element.41.context_ref, bf16[1024,8192]{1,0:T(8,128)(2,1)S(1)} %get-tuple-element.32.refs_7_.w_ref), custom_call_target="tpu_custom_call" | custom-call | flops 1006632960 | bytes 5242880 | tf_op jit(solution)/shard_map/project_rest/pallas_call | solution.py:199
  35.0 0.2 collective-permute-start.9
  35.2 1.7 %collective-permute-done.9 = bf16[96,2560]{1,0:T(8,128)(2,1)S(1)} collective-permute-done((bf16[96,2560]{1,0:T(8,128)(2,1)S(1)}, bf16[96,2560]{1,0:T(8,128)(2,1)S(1)}, u32[]{:S(2)}, u32[]{:S(2)}) %collective-permute-start.9) | collective-permute-done | bytes 491552 | tf_op jit(solution)/shard_map/ppermute | solution.py:229
  36.9 0.1 add_convert_fusion.3
  37.0 1.8 %project_rest.3 = (bf16[96,4096]{1,0:T(8,128)(2,1)S(1)}, bf16[96,4096]{1,0:T(8,128)(2,1)S(1)}) custom-call(bf16[192,1024]{1,0:T(8,128)(2,1)S(1)} %get-tuple-element.41.context_ref, bf16[1024,8192]{1,0:T(8,128)(2,1)S(1)} %get-tuple-element.32.refs_7_.w_ref), custom_call_target="tpu_custom_call" | custom-call | flops 1610612736 | bytes 8388608 | tf_op jit(solution)/shard_map/project_rest/pallas_call | solution.py:199
  38.8 0.2 collective-permute-start.11
  39.0 1.5 %collective-permute-start.8 = (bf16[48,1536]{1,0:T(8,128)(2,1)S(1)}, bf16[48,1536]{1,0:T(8,128)(2,1)S(1)}, u32[]{:S(2)}, u32[]{:S(2)}) collective-permute-start(bf16[48,1536]{1,0:T(8,128)(2,1)S(1)} %add_convert_fusion.5), channel_id=1, source_target_pairs={{0,2},{1,3},{2,0},{3,1},{4,6},{5,7},{6,4},{7,5},{8,10},{9,11},{10,... | collective-permute-start | bytes 442376 | tf_op jit(solution)/shard_map/ppermute | solution.py:313
  40.6 4.6 %collective-permute-done.8 = bf16[48,1536]{1,0:T(8,128)(2,1)S(1)} collective-permute-done((bf16[48,1536]{1,0:T(8,128)(2,1)S(1)}, bf16[48,1536]{1,0:T(8,128)(2,1)S(1)}, u32[]{:S(2)}, u32[]{:S(2)}) %collective-permute-start.8) | collective-permute-done | bytes 147488 | tf_op jit(solution)/shard_map/ppermute | solution.py:313
  45.2 0.1 add_convert_fusion.4
  45.2 1.6 %collective-permute-start.10 = (bf16[48,2560]{1,0:T(8,128)(2,1)S(1)}, bf16[48,2560]{1,0:T(8,128)(2,1)S(1)}, u32[]{:S(2)}, u32[]{:S(2)}) collective-permute-start(bf16[48,2560]{1,0:T(8,128)(2,1)S(1)} %add_convert_fusion.3), channel_id=1, source_target_pairs={{0,2},{1,3},{2,0},{3,1},{4,6},{5,7},{6,4},{7,5},{8,10},{9,11},{10,... | collective-permute-start | bytes 737288 | tf_op jit(solution)/shard_map/ppermute | solution.py:313
  46.8 0.0 collective-permute-done.11
  46.8 0.1 add_convert_fusion.1
  46.9 0.6 collective-permute-start.12
  47.5 6.6 %collective-permute-done.10 = bf16[48,2560]{1,0:T(8,128)(2,1)S(1)} collective-permute-done((bf16[48,2560]{1,0:T(8,128)(2,1)S(1)}, bf16[48,2560]{1,0:T(8,128)(2,1)S(1)}, u32[]{:S(2)}, u32[]{:S(2)}) %collective-permute-start.10) | collective-permute-done | bytes 245792 | tf_op jit(solution)/shard_map/ppermute | solution.py:313
  54.1 0.1 add_convert_fusion.2
  54.2 6.9 %collective-permute-done.12 = bf16[48,4096]{1,0:T(8,128)(2,1)S(1)} collective-permute-done((bf16[48,4096]{1,0:T(8,128)(2,1)S(1)}, bf16[48,4096]{1,0:T(8,128)(2,1)S(1)}, u32[]{:S(2)}, u32[]{:S(2)}) %collective-permute-start.12) | collective-permute-done | bytes 393248 | tf_op jit(solution)/shard_map/ppermute | solution.py:313
  61.1 0.1 add_convert_fusion
  61.2 0.9 %pad_maximum_fusion = bf16[48,8192]{1,0:T(8,128)(2,1)} fusion(bf16[48,4096]{1,0:T(8,128)(2,1)S(1)} %add_convert_fusion, bf16[48,2560]{1,0:T(8,128)(2,1)S(1)} %add_convert_fusion.2, bf16[48,1536]{1,0:T(8,128)(2,1)S(1)} %add_convert_fusion.4), kind=kLoop, calls=%fused_computation | loop fusion | flops 2359296 | bytes 1572864 | tf_op jit(solution)/shard_map/concatenate | solution.py:318
  (4 shorter events, 0.1 us)
Async XLA Ops:
  0.0 20.8 %copy-start = (bf16[192,1024]{1,0:T(8,128)(2,1)S(1)}, bf16[192,1024]{1,0:T(8,128)(2,1)}, u32[]{:S(2)}) copy-start(bf16[192,1024]{1,0:T(8,128)(2,1)} %refs_0_.3) | copy-start | bytes 1179652
  0.0 0.9 %copy-start.1 = (bf16[192,256]{1,0:T(8,128)(2,1)S(1)}, bf16[192,256]{1,0:T(8,128)(2,1)}, u32[]{:S(2)}) copy-start(bf16[192,256]{1,0:T(8,128)(2,1)} %k_ref.1) | copy-start | bytes 294916
  0.9 0.9 %copy-start.2 = (bf16[192,256]{1,0:T(8,128)(2,1)S(1)}, bf16[192,256]{1,0:T(8,128)(2,1)}, u32[]{:S(2)}) copy-start(bf16[192,256]{1,0:T(8,128)(2,1)} %v_ref.1) | copy-start | bytes 294916
  1.9 7.1 %collective-permute-start.1 = (bf16[192,512]{1,0:T(8,128)(2,1)S(1)}, bf16[192,512]{1,0:T(8,128)(2,1)S(1)}, u32[]{:S(2)}, u32[]{:S(2)}) collective-permute-start(bf16[192,512]{1,0:T(8,128)(2,1)S(1)} %join.1.refs_3_), channel_id=1, source_target_pairs={{0,1},{1,0},{2,3},{3,2},{4,5},{5,4},{6,7},{7,6},{8,16},{9,17},{10,... | collective-permute-start | bytes 589832 | tf_op jit(solution)/shard_map/ppermute | solution.py:229
  2.4 8.8 %collective-permute-start = (bf16[192,512]{1,0:T(8,128)(2,1)S(1)}, bf16[192,512]{1,0:T(8,128)(2,1)S(1)}, u32[]{:S(2)}, u32[]{:S(2)}) collective-permute-start(bf16[192,512]{1,0:T(8,128)(2,1)S(1)} %join.1.refs_3_), channel_id=1, source_target_pairs={{0,8},{1,9},{2,10},{3,11},{4,12},{5,13},{6,14},{7,15},{8,0},{9,1},... | collective-permute-start | bytes 589832 | tf_op jit(solution)/shard_map/ppermute | solution.py:229
  6.6 12.0 %collective-permute-start.5 = (bf16[192,512]{1,0:T(8,128)(2,1)S(1)}, bf16[192,512]{1,0:T(8,128)(2,1)S(1)}, u32[]{:S(2)}, u32[]{:S(2)}) collective-permute-start(bf16[192,512]{1,0:T(8,128)(2,1)S(1)} %join.1.refs_3_), channel_id=1, source_target_pairs={{0,4},{1,5},{2,6},{3,7},{4,0},{5,1},{6,2},{7,3},{8,12},{9,13},{10,... | collective-permute-start | bytes 589832 | tf_op jit(solution)/shard_map/ppermute | solution.py:229
  11.2 5.8 %collective-permute-start.2 = (bf16[192,512]{1,0:T(8,128)(2,1)S(1)}, bf16[192,512]{1,0:T(8,128)(2,1)S(1)}, u32[]{:S(2)}, u32[]{:S(2)}) collective-permute-start(bf16[192,512]{1,0:T(8,128)(2,1)S(1)} %collective-permute-done.1), channel_id=1, source_target_pairs={{0,8},{1,9},{2,10},{3,11},{4,12},{5,13},{6,14},{7,15},{8,0},{9,1},... | collective-permute-start | bytes 589832 | tf_op jit(solution)/shard_map/ppermute | solution.py:229
  12.9 4.0 %collective-permute-start.3 = (bf16[192,512]{1,0:T(8,128)(2,1)S(1)}, bf16[192,512]{1,0:T(8,128)(2,1)S(1)}, u32[]{:S(2)}, u32[]{:S(2)}) collective-permute-start(bf16[192,512]{1,0:T(8,128)(2,1)S(1)} %collective-permute-done), channel_id=1, source_target_pairs={{0,1},{1,0},{2,3},{3,2},{4,5},{5,4},{6,7},{7,6},{8,16},{9,17},{10,... | collective-permute-start | bytes 589832 | tf_op jit(solution)/shard_map/ppermute | solution.py:229
  13.0 7.8 %collective-permute-start.6 = (bf16[192,512]{1,0:T(8,128)(2,1)S(1)}, bf16[192,512]{1,0:T(8,128)(2,1)S(1)}, u32[]{:S(2)}, u32[]{:S(2)}) collective-permute-start(bf16[192,512]{1,0:T(8,128)(2,1)S(1)} %broadcast_select_fusion.refs_5_), channel_id=1, source_target_pairs={{0,4},{1,5},{2,6},{3,7},{4,0},{5,1},{6,2},{7,3},{8,12},{9,13},{10,... | collective-permute-start | bytes 589832 | tf_op jit(solution)/shard_map/ppermute | solution.py:229
  17.0 12.5 %collective-permute-start.4 = (bf16[192,512]{1,0:T(8,128)(2,1)S(1)}, bf16[192,512]{1,0:T(8,128)(2,1)S(1)}, u32[]{:S(2)}, u32[]{:S(2)}) collective-permute-start(bf16[192,512]{1,0:T(8,128)(2,1)S(1)} %broadcast_select_fusion.1.refs_7_), channel_id=1, source_target_pairs={{0,4},{1,5},{2,6},{3,7},{4,0},{5,1},{6,2},{7,3},{8,12},{9,13},{10,... | collective-permute-start | bytes 589832 | tf_op jit(solution)/shard_map/ppermute | solution.py:229
  32.1 1.6 %collective-permute-start.7 = (bf16[96,1536]{1,0:T(8,128)(2,1)S(1)}, bf16[96,1536]{1,0:T(8,128)(2,1)S(1)}, u32[]{:S(2)}, u32[]{:S(2)}) collective-permute-start(bf16[96,1536]{1,0:T(8,128)(2,1)S(1)} %get-tuple-element.34), channel_id=1, source_target_pairs={{0,1},{1,0},{2,3},{3,2},{4,5},{5,4},{6,7},{7,6},{8,9},{9,8},{10,11... | collective-permute-start | bytes 884744 | tf_op jit(solution)/shard_map/ppermute | solution.py:229
  35.0 1.9 %collective-permute-start.9 = (bf16[96,2560]{1,0:T(8,128)(2,1)S(1)}, bf16[96,2560]{1,0:T(8,128)(2,1)S(1)}, u32[]{:S(2)}, u32[]{:S(2)}) collective-permute-start(bf16[96,2560]{1,0:T(8,128)(2,1)S(1)} %get-tuple-element.39), channel_id=1, source_target_pairs={{0,1},{1,0},{2,3},{3,2},{4,5},{5,4},{6,7},{7,6},{8,9},{9,8},{10,11... | collective-permute-start | bytes 1474568 | tf_op jit(solution)/shard_map/ppermute | solution.py:229
  38.8 8.0 %collective-permute-start.11 = (bf16[96,4096]{1,0:T(8,128)(2,1)S(1)}, bf16[96,4096]{1,0:T(8,128)(2,1)S(1)}, u32[]{:S(2)}, u32[]{:S(2)}) collective-permute-start(bf16[96,4096]{1,0:T(8,128)(2,1)S(1)} %get-tuple-element.43), channel_id=1, source_target_pairs={{0,1},{1,0},{2,3},{3,2},{4,5},{5,4},{6,7},{7,6},{8,9},{9,8},{10,11... | collective-permute-start | bytes 2359304 | tf_op jit(solution)/shard_map/ppermute | solution.py:229
  39.0 6.1 %collective-permute-start.8 = (bf16[48,1536]{1,0:T(8,128)(2,1)S(1)}, bf16[48,1536]{1,0:T(8,128)(2,1)S(1)}, u32[]{:S(2)}, u32[]{:S(2)}) collective-permute-start(bf16[48,1536]{1,0:T(8,128)(2,1)S(1)} %add_convert_fusion.5), channel_id=1, source_target_pairs={{0,2},{1,3},{2,0},{3,1},{4,6},{5,7},{6,4},{7,5},{8,10},{9,11},{10,... | collective-permute-start | bytes 442376 | tf_op jit(solution)/shard_map/ppermute | solution.py:313
  45.2 8.9 %collective-permute-start.10 = (bf16[48,2560]{1,0:T(8,128)(2,1)S(1)}, bf16[48,2560]{1,0:T(8,128)(2,1)S(1)}, u32[]{:S(2)}, u32[]{:S(2)}) collective-permute-start(bf16[48,2560]{1,0:T(8,128)(2,1)S(1)} %add_convert_fusion.3), channel_id=1, source_target_pairs={{0,2},{1,3},{2,0},{3,1},{4,6},{5,7},{6,4},{7,5},{8,10},{9,11},{10,... | collective-permute-start | bytes 737288 | tf_op jit(solution)/shard_map/ppermute | solution.py:313
  46.9 14.2 %collective-permute-start.12 = (bf16[48,4096]{1,0:T(8,128)(2,1)S(1)}, bf16[48,4096]{1,0:T(8,128)(2,1)S(1)}, u32[]{:S(2)}, u32[]{:S(2)}) collective-permute-start(bf16[48,4096]{1,0:T(8,128)(2,1)S(1)} %add_convert_fusion.1), channel_id=1, source_target_pairs={{0,2},{1,3},{2,0},{3,1},{4,6},{5,7},{6,4},{7,5},{8,10},{9,11},{10,... | collective-permute-start | bytes 1179656 | tf_op jit(solution)/shard_map/ppermute | solution.py:313
where the time goes:
time: 62.4 us; the launch traced here: 62.2 us
  waiting for transfers between devices  28.3 us (45%)
  starting transfers between devices  15.2 us (24%)
  Pallas kernels  14.3 us (23%)
  other arithmetic  2.16 us (3%)
  local copies, waits for them, and re-layouts  2.02 us (3%)
    ppermute x3, waiting for transfers between devices, layer(): lax.ppermute(moved[at:at + part], AXES, y_route(seq, tp, distance))  18.1 us
    ppermute x10, starting transfers between devices, send(): return lax.ppermute(x, AXES, route[name])  11.5 us
    ppermute x10, waiting for transfers between devices, send(): return lax.ppermute(x, AXES, route[name])  10.2 us
    pallas_call x1, Pallas kernels, layer(): pl.pallas_call(functools.partial(early_kernel, kv_local, group, count, 32...  8.69 us
    ppermute x3, starting transfers between devices, layer(): lax.ppermute(moved[at:at + part], AXES, y_route(seq, tp, distance))  3.68 us
    pallas_call x2, Pallas kernels, project_call(): pl.pallas_call(functools.partial(project_kernel, part, start), out_shape=...  3.08 us
    pallas_call x1, Pallas kernels, layer(): pl.pallas_call(functools.partial(late_kernel, kv_local, group, part, dept...  2.53 us
    unnamed x6, local copies, waits for them, and re-layouts  1.84 us
  transfers between devices with their start and end apart: 13, of which 8 were waited for; matrix products, arithmetic and copies ran while one was open for 2% of the time, Pallas kernels for 14%

commit v1 on v0

--- a/solution.py
+++ b/solution.py
@@ -68,6 +68,33 @@
         copy.wait()
 
 
+def load_kernel(start, w_hbm, out_ref, sem):
+    width = out_ref.shape[1]
+    copy = pltpu.make_async_copy(w_hbm.at[:, pl.ds(start, width)], out_ref, sem)
+    copy.start()
+    copy.wait()
+
+
+def load_call(weight, start, stop):
+    shape = (weight.shape[0], stop - start)
+    return pl.pallas_call(
+        functools.partial(load_kernel, start),
+        out_shape=pltpu.VMEM(shape, weight.dtype),
+        in_specs=[ANY],
+        out_specs=VMEM,
+        scratch_shapes=[pltpu.SemaphoreType.DMA],
+        cost_estimate=pl.CostEstimate(
+            flops=0, transcendentals=0, bytes_accessed=2 * shape[0] * shape[1]
+        ),
+        compiler_params=pltpu.CompilerParams(vmem_limit_bytes=MIB),
+        name="load",
+    )(weight)
+
+
+def in_hbm(x):
+    return pltpu.with_memory_space_constraint(x, pltpu.HBM)
+
+
 def query_doc(docs_t_ref, me):
     docs = docs_t_ref[...]
     lane = lax.broadcasted_iota(jnp.int32, docs.shape, 1)
@@ -94,11 +121,8 @@
 def early_kernel(kv_local, group, count, step, *refs):
     q_ref, docs_ref, docs_t_ref = refs[:3]
     blocks = refs[3 : 3 + count]
-    w_hbm = refs[3 + count]
-    acc_ref, top_ref, sum_ref, w_ref = refs[4 + count : 8 + count]
-    bias_ref, s_ref, p_ref, sem = refs[8 + count :]
-    copy = pltpu.make_async_copy(w_hbm, w_ref, sem)
-    copy.start()
+    acc_ref, top_ref, sum_ref = refs[3 + count : 6 + count]
+    bias_ref, s_ref, p_ref = refs[6 + count :]
     tokens = q_ref.shape[0]
     stacked = group * tokens
     me = lax.axis_index("seq")
@@ -130,11 +154,10 @@
         acc_ref[pl.ds(h * stacked, stacked), :] = jnp.dot(
             p_ref[...], values, preferred_element_type=jnp.float32
         )
-    copy.wait()
 
 
 def project(context_ref, w_ref, start, width, send_ref, keep_ref, part):
-    step = 512
+    step = 256
     for c in range(0, width, step):
         at = pl.ds(c, step)
         rows = jnp.dot(
@@ -230,54 +253,51 @@
 
     own = pl.pallas_call(
         join_kernel,
-        out_shape=jax.ShapeDtypeStruct((tokens, 2 * kv_local * HD), jnp.bfloat16),
+        out_shape=pltpu.VMEM((tokens, 2 * kv_local * HD), jnp.bfloat16),
         in_specs=[ANY, ANY],
         out_specs=VMEM,
         scratch_shapes=[pltpu.SemaphoreType.DMA((2,))],
         compiler_params=pltpu.CompilerParams(vmem_limit_bytes=2 * MIB),
         name="join",
-    )(key_rows, value_rows)
+    )(in_hbm(key_rows), in_hbm(value_rows))
     docs = document_ids.astype(jnp.float32).reshape(seq, tokens)
     docs_t = docs.T
+    cuts = [model * 7 // 32, model * 17 // 32, model]
+    weight = in_hbm(output_weight)
+    near_weight = load_call(weight, 0, cuts[1])
+    far_weight = load_call(weight, cuts[1], model)
     even, odd = send(own, "even"), send(own, "odd")
     blocks = [own, send(own, "col")]
     even, odd, docs, docs_t = lax.optimization_barrier((even, odd, docs, docs_t))
     for distance in range(1, depth + 1):
         blocks.append(jnp.where(odd_row, even, odd))
         if distance < depth:
-            even, odd = send(odd, "even"), send(even, "odd")
+            even, odd = (send(odd, "even"), send(even, "odd"))
         blocks.append(send(blocks[-1], "col"))
     last_block = blocks.pop()
     count = len(blocks)
 
     stacked = group * tokens
     state = jax.ShapeDtypeStruct((kv_local * stacked, HD), jnp.float32)
-    acc, top, total, weight = pl.pallas_call(
+    acc, top, total = pl.pallas_call(
         functools.partial(early_kernel, kv_local, group, count, 32),
-        out_shape=(
-            state,
-            state,
-            state,
-            pltpu.VMEM(output_weight.shape, output_weight.dtype),
-        ),
-        in_specs=[VMEM] * (3 + count) + [ANY],
-        out_specs=(VMEM,) * 4,
+        out_shape=(state, state, state),
+        in_specs=[VMEM] * (3 + count),
+        out_specs=(VMEM,) * 3,
         scratch_shapes=[
             pltpu.VMEM((tokens, count * tokens), jnp.float32),
             pltpu.VMEM((stacked, count * tokens), jnp.float32),
             pltpu.VMEM((stacked, count * tokens), jnp.bfloat16),
-            pltpu.SemaphoreType.DMA,
         ],
         cost_estimate=pl.CostEstimate(
             flops=4 * tokens * tokens * count * width,
             transcendentals=tokens * tokens * count * width // HD,
-            bytes_accessed=2 * width * model,
+            bytes_accessed=4 * tokens * width,
         ),
         compiler_params=pltpu.CompilerParams(vmem_limit_bytes=24 * MIB),
         name="attend_early",
-    )(query_rows, docs, docs_t, *blocks, output_weight)
-
-    cuts = [model * 3 // 16, model // 2, model]
+    )(query_rows, docs, docs_t, *blocks)
+
     out = jax.ShapeDtypeStruct((tokens // 2, cuts[0]), jnp.bfloat16)
     context, sent, kept = pl.pallas_call(
         functools.partial(late_kernel, kv_local, group, part, depth),
@@ -292,19 +312,21 @@
         ),
         compiler_params=pltpu.CompilerParams(vmem_limit_bytes=16 * MIB),
         name="attend_late",
-    )(query_rows, docs, docs_t, last_block, acc, top, total, weight)
+    )(query_rows, docs, docs_t, last_block, acc, top, total, near_weight)
 
     pieces = []
     remote = (chips - 1) * part
     for i, stop in enumerate(cuts):
         if i:
-            start = cuts[i - 1]
-            sent, kept = project_call(context, weight, start, stop - start, part)
+            from_weight = near_weight if i == 1 else far_weight
+            start = cuts[0] if i == 1 else 0
+            sent, kept = project_call(
+                context, from_weight, start, stop - cuts[i - 1], part
+            )
         received = send(sent, "core")
         moved = (
             kept[:remote].astype(jnp.float32) + received[:remote].astype(jnp.float32)
         ).astype(jnp.bfloat16)
-        context, moved = lax.optimization_barrier((context, moved))
         piece = kept[remote:].astype(jnp.float32) + received[remote:].astype(
             jnp.float32
         )

time: 62.4 us -> 55.5 us (0.89)
  waiting for transfers between devices: 28.3 us -> 20.9 us
  Pallas kernels: 14.3 us -> 16.8 us
  local copies, waits for them, and re-layouts: 2.02 us -> 0.19 us
    pallas_call x1 -> x3, Pallas kernels: 0.04 us -> 7.74 us  [the longest x2 6.78 us: load_call(): pl.pallas_call(functools.partial(load_kernel, start), out_shape=pltpu.VME...]
    pallas_call x1, Pallas kernels: 8.69 us -> 3.39 us  [layer(): pl.pallas_call(functools.partial(early_kernel, kv_local, group, count, 32...]
    ppermute x10, waiting for transfers between devices: 10.2 us -> 5 us  [send(): return lax.ppermute(x, AXES, route[name])]
    ppermute x3, waiting for transfers between devices: 18.1 us -> 15.9 us  [layer(): lax.ppermute(moved[at:at + part], AXES, y_route(seq, tp, distance))]
    unnamed x6 -> x2, local copies, waits for them, and re-layouts: 1.84 us -> 0.01 us
  transfers between devices with their start and end apart: 13 -> 13, of which waited for: 8 -> 5; matrix products, arithmetic and copies ran while one was open for 2% -> 2% of each run, Pallas kernels for 14% -> 24%
where the time goes in v1:
time: 55.5 us; the launch traced here: 55.3 us
  waiting for transfers between devices  20.9 us (38%)
  Pallas kernels  16.8 us (30%)
  starting transfers between devices  15 us (27%)
  other arithmetic  2.17 us (4%)
    ppermute x3, waiting for transfers between devices, layer(): lax.ppermute(moved[at:at + part], AXES, y_route(seq, tp, distance))  15.9 us
    ppermute x10, starting transfers between devices, send(): return lax.ppermute(x, AXES, route[name])  11.3 us
    pallas_call x2, Pallas kernels, load_call(): pl.pallas_call(functools.partial(load_kernel, start), out_shape=pltpu.VME...  6.78 us
    ppermute x10, waiting for transfers between devices, send(): return lax.ppermute(x, AXES, route[name])  5 us
    ppermute x3, starting transfers between devices, layer(): lax.ppermute(moved[at:at + part], AXES, y_route(seq, tp, distance))  3.74 us
    pallas_call x1, Pallas kernels, layer(): pl.pallas_call(functools.partial(early_kernel, kv_local, group, count, 32...  3.39 us
    pallas_call x2, Pallas kernels, project_call(): pl.pallas_call(functools.partial(project_kernel, part, start), out_shape=...  3 us
    pallas_call x1, Pallas kernels, layer(): pl.pallas_call(functools.partial(late_kernel, kv_local, group, part, dept...  2.68 us
  transfers between devices with their start and end apart: 13, of which 5 were waited for; matrix products, arithmetic and copies ran while one was open for 2% of the time, Pallas kernels for 24%

profile of v1, /device:TPU:0, one launch (start us, length us, event | category | flops | bytes accessed | tf_op | source)
XLA Modules:
  0.0 55.3 jit_solution(14393753843038874565)
XLA Ops:
  0.0 1.0 %join.1.refs_3_ = bf16[192,512]{1,0:T(8,128)(2,1)S(1)} custom-call(bf16[192,256]{1,0:T(8,128)(2,1)} %k_ref.1, bf16[192,256]{1,0:T(8,128)(2,1)} %v_ref.1), custom_call_target="tpu_custom_call" | custom-call | tf_op jit(solution)/shard_map/join/pallas_call | solution.py:254
  1.0 3.1 %collective-permute-start = (bf16[192,512]{1,0:T(8,128)(2,1)S(1)}, bf16[192,512]{1,0:T(8,128)(2,1)S(1)}, u32[]{:S(2)}, u32[]{:S(2)}) collective-permute-start(bf16[192,512]{1,0:T(8,128)(2,1)S(1)} %join.1.refs_3_), channel_id=1, source_target_pairs={{0,8},{1,9},{2,10},{3,11},{4,12},{5,13},{6,14},{7,15},{8,0},{9,1},... | collective-permute-start | bytes 589832 | tf_op jit(solution)/shard_map/ppermute | solution.py:252
  4.1 0.0 collective-permute-start.1
  4.1 1.5 %collective-permute-start.5 = (bf16[192,512]{1,0:T(8,128)(2,1)S(1)}, bf16[192,512]{1,0:T(8,128)(2,1)S(1)}, u32[]{:S(2)}, u32[]{:S(2)}) collective-permute-start(bf16[192,512]{1,0:T(8,128)(2,1)S(1)} %join.1.refs_3_), channel_id=1, source_target_pairs={{0,4},{1,5},{2,6},{3,7},{4,0},{5,1},{6,2},{7,3},{8,12},{9,13},{10,... | collective-permute-start | bytes 589832 | tf_op jit(solution)/shard_map/ppermute | solution.py:252
  5.6 0.7 %convert_element_type.66 = f32[1536]{0:T(1024)S(1)} convert(s32[1536]{0:T(1024)} %param.8) | non-fusion elementwise | flops 1536 | bytes 12288 | tf_op jit(solution)/shard_map/convert_element_type | solution.py:263
  6.3 0.1 reshape.3.refs_1_
  6.4 0.1 copy.8
  6.5 2.5 %collective-permute-done = bf16[192,512]{1,0:T(8,128)(2,1)S(1)} collective-permute-done((bf16[192,512]{1,0:T(8,128)(2,1)S(1)}, bf16[192,512]{1,0:T(8,128)(2,1)S(1)}, u32[]{:S(2)}, u32[]{:S(2)}) %collective-permute-start) | collective-permute-done | bytes 196640 | tf_op jit(solution)/shard_map/ppermute | solution.py:252
  9.0 0.0 collective-permute-done.1
  9.0 2.9 %collective-permute-start.2 = (bf16[192,512]{1,0:T(8,128)(2,1)S(1)}, bf16[192,512]{1,0:T(8,128)(2,1)S(1)}, u32[]{:S(2)}, u32[]{:S(2)}) collective-permute-start(bf16[192,512]{1,0:T(8,128)(2,1)S(1)} %collective-permute-done.1), channel_id=1, source_target_pairs={{0,8},{1,9},{2,10},{3,11},{4,12},{5,13},{6,14},{7,15},{8,0},{9,1},... | collective-permute-start | bytes 589832 | tf_op jit(solution)/shard_map/ppermute | solution.py:252
  11.9 0.0 collective-permute-start.3
  11.9 1.6 %collective-permute-start.6 = (bf16[192,512]{1,0:T(8,128)(2,1)S(1)}, bf16[192,512]{1,0:T(8,128)(2,1)S(1)}, u32[]{:S(2)}, u32[]{:S(2)}) collective-permute-start(bf16[192,512]{1,0:T(8,128)(2,1)S(1)} %broadcast_select_fusion.refs_5_), channel_id=1, source_target_pairs={{0,4},{1,5},{2,6},{3,7},{4,0},{5,1},{6,2},{7,3},{8,12},{9,13},{10,... | collective-permute-start | bytes 589832 | tf_op jit(solution)/shard_map/ppermute | solution.py:252
  13.4 2.5 %collective-permute-done.2 = bf16[192,512]{1,0:T(8,128)(2,1)S(1)} collective-permute-done((bf16[192,512]{1,0:T(8,128)(2,1)S(1)}, bf16[192,512]{1,0:T(8,128)(2,1)S(1)}, u32[]{:S(2)}, u32[]{:S(2)}) %collective-permute-start.2) | collective-permute-done | bytes 196640 | tf_op jit(solution)/shard_map/ppermute | solution.py:252
  15.9 0.0 collective-permute-done.3
  15.9 0.0 copy-start
  15.9 1.6 %collective-permute-start.4 = (bf16[192,512]{1,0:T(8,128)(2,1)S(1)}, bf16[192,512]{1,0:T(8,128)(2,1)S(1)}, u32[]{:S(2)}, u32[]{:S(2)}) collective-permute-start(bf16[192,512]{1,0:T(8,128)(2,1)S(1)} %broadcast_select_fusion.1.refs_7_), channel_id=1, source_target_pairs={{0,4},{1,5},{2,6},{3,7},{4,0},{5,1},{6,2},{7,3},{8,12},{9,13},{10,... | collective-permute-start | bytes 589832 | tf_op jit(solution)/shard_map/ppermute | solution.py:252
  17.5 3.5 %load.2.refs_7_.w_ref = bf16[1024,4352]{1,0:T(8,128)(2,1)S(1)} custom-call(bf16[1024,8192]{1,0:T(8,128)(2,1)} %w_hbm.3), custom_call_target="tpu_custom_call" | custom-call | bytes 8912896 | tf_op jit(solution)/shard_map/load/pallas_call | solution.py:80
  21.0 0.0 collective-permute-done.5.refs_4_
  21.1 0.0 collective-permute-done.6.refs_6_
  21.1 0.0 copy-done
  21.1 3.4 %attend_early.1 = (f32[1536,128]{1,0:T(8,128)S(1)}, f32[1536,128]{1,0:T(8,128)S(1)}, f32[1536,128]{1,0:T(8,128)S(1)}) custom-call(bf16[192,1024]{1,0:T(8,128)(2,1)S(1)} %copy-done, f32[8,192]{1,0:T(8,128)S(1)} %reshape.3.refs_1_, f32[192,8]{1,0:T(8,128)S(1)} %bitcast.1, bf16[192,512]{1,0:T(8,128)(2,1)S(1)} %join.1.refs_3_, ...), custom_call_target="tpu_custom_call" | custom-call | flops 754974720 | bytes 786432 | tf_op jit(solution)/shard_map/attend_early/pallas_call | solution.py:282
  24.5 0.0 collective-permute-done.4.refs_3_
  24.5 2.7 %attend_late.1 = (bf16[192,1024]{1,0:T(8,128)(2,1)S(1)}, bf16[96,1792]{1,0:T(8,128)(2,1)S(1)}, bf16[96,1792]{1,0:T(8,128)(2,1)S(1)}) custom-call(bf16[192,1024]{1,0:T(8,128)(2,1)S(1)} %copy-done, f32[8,192]{1,0:T(8,128)S(1)} %reshape.3.refs_1_, f32[192,8]{1,0:T(8,128)S(1)} %bitcast.2, bf16[192,512]{1,0:T(8,128)(2,1)S(1)} %collective-permute-done.4.refs_3_, ...), custom_call_target="tpu_custom_call" | custom-call | flops 855638016 | bytes 4456448 | tf_op jit(solution)/shard_map/attend_late/pallas_call | solution.py:302
  27.2 0.1 collective-permute-start.7
  27.3 3.2 %load.3.w_ref = bf16[1024,3840]{1,0:T(8,128)(2,1)S(1)} custom-call(bf16[1024,8192]{1,0:T(8,128)(2,1)} %w_hbm.3), custom_call_target="tpu_custom_call" | custom-call | bytes 7864320 | tf_op jit(solution)/shard_map/load/pallas_call | solution.py:80
  30.5 1.2 %project_rest.2 = (bf16[96,2560]{1,0:T(8,128)(2,1)S(1)}, bf16[96,2560]{1,0:T(8,128)(2,1)S(1)}) custom-call(bf16[192,1024]{1,0:T(8,128)(2,1)S(1)} %get-tuple-element.28.context_ref, bf16[1024,4352]{1,0:T(8,128)(2,1)S(1)} %load.2.refs_7_.w_ref), custom_call_target="tpu_custom_call" | custom-call | flops 1006632960 | bytes 5242880 | tf_op jit(solution)/shard_map/project_rest/pallas_call | solution.py:222
  31.7 0.6 %collective-permute-start.9 = (bf16[96,2560]{1,0:T(8,128)(2,1)S(1)}, bf16[96,2560]{1,0:T(8,128)(2,1)S(1)}, u32[]{:S(2)}, u32[]{:S(2)}) collective-permute-start(bf16[96,2560]{1,0:T(8,128)(2,1)S(1)} %get-tuple-element.30), channel_id=1, source_target_pairs={{0,1},{1,0},{2,3},{3,2},{4,5},{5,4},{6,7},{7,6},{8,9},{9,8},{10,11... | collective-permute-start | bytes 1474568 | tf_op jit(solution)/shard_map/ppermute | solution.py:252
  32.3 1.8 %project_rest.3 = (bf16[96,3840]{1,0:T(8,128)(2,1)S(1)}, bf16[96,3840]{1,0:T(8,128)(2,1)S(1)}) custom-call(bf16[192,1024]{1,0:T(8,128)(2,1)S(1)} %get-tuple-element.28.context_ref, bf16[1024,3840]{1,0:T(8,128)(2,1)S(1)} %load.3.w_ref), custom_call_target="tpu_custom_call" | custom-call | flops 1509949440 | bytes 7864320 | tf_op jit(solution)/shard_map/project_rest/pallas_call | solution.py:222
  34.1 0.1 collective-permute-start.11
  34.2 0.0 collective-permute-done.7
  34.2 1.6 %collective-permute-start.8 = (bf16[48,1792]{1,0:T(8,128)(2,1)S(1)}, bf16[48,1792]{1,0:T(8,128)(2,1)S(1)}, u32[]{:S(2)}, u32[]{:S(2)}) collective-permute-start(bf16[48,1792]{1,0:T(8,128)(2,1)S(1)} %add_convert_fusion.5), channel_id=1, source_target_pairs={{0,2},{1,3},{2,0},{3,1},{4,6},{5,7},{6,4},{7,5},{8,10},{9,11},{10,... | collective-permute-start | bytes 516104 | tf_op jit(solution)/shard_map/ppermute | solution.py:335
  35.8 0.0 collective-permute-done.9
  35.8 0.1 add_convert_fusion.3
  35.9 0.6 %collective-permute-start.10 = (bf16[48,2560]{1,0:T(8,128)(2,1)S(1)}, bf16[48,2560]{1,0:T(8,128)(2,1)S(1)}, u32[]{:S(2)}, u32[]{:S(2)}) collective-permute-start(bf16[48,2560]{1,0:T(8,128)(2,1)S(1)} %add_convert_fusion.3), channel_id=1, source_target_pairs={{0,2},{1,3},{2,0},{3,1},{4,6},{5,7},{6,4},{7,5},{8,10},{9,11},{10,... | collective-permute-start | bytes 737288 | tf_op jit(solution)/shard_map/ppermute | solution.py:335
  36.4 5.1 %collective-permute-done.8 = bf16[48,1792]{1,0:T(8,128)(2,1)S(1)} collective-permute-done((bf16[48,1792]{1,0:T(8,128)(2,1)S(1)}, bf16[48,1792]{1,0:T(8,128)(2,1)S(1)}, u32[]{:S(2)}, u32[]{:S(2)}) %collective-permute-start.8) | collective-permute-done | bytes 172064 | tf_op jit(solution)/shard_map/ppermute | solution.py:335
  41.5 0.1 add_convert_fusion.4
  41.6 0.0 collective-permute-done.11
  41.6 0.1 add_convert_fusion.1
  41.7 1.6 %collective-permute-start.12 = (bf16[48,3840]{1,0:T(8,128)(2,1)S(1)}, bf16[48,3840]{1,0:T(8,128)(2,1)S(1)}, u32[]{:S(2)}, u32[]{:S(2)}) collective-permute-start(bf16[48,3840]{1,0:T(8,128)(2,1)S(1)} %add_convert_fusion.1), channel_id=1, source_target_pairs={{0,2},{1,3},{2,0},{3,1},{4,6},{5,7},{6,4},{7,5},{8,10},{9,11},{10,... | collective-permute-start | bytes 1105928 | tf_op jit(solution)/shard_map/ppermute | solution.py:335
  43.3 3.5 %collective-permute-done.10 = bf16[48,2560]{1,0:T(8,128)(2,1)S(1)} collective-permute-done((bf16[48,2560]{1,0:T(8,128)(2,1)S(1)}, bf16[48,2560]{1,0:T(8,128)(2,1)S(1)}, u32[]{:S(2)}, u32[]{:S(2)}) %collective-permute-start.10) | collective-permute-done | bytes 245792 | tf_op jit(solution)/shard_map/ppermute | solution.py:335
  46.8 0.1 add_convert_fusion.2
  46.9 7.3 %collective-permute-done.12 = bf16[48,3840]{1,0:T(8,128)(2,1)S(1)} collective-permute-done((bf16[48,3840]{1,0:T(8,128)(2,1)S(1)}, bf16[48,3840]{1,0:T(8,128)(2,1)S(1)}, u32[]{:S(2)}, u32[]{:S(2)}) %collective-permute-start.12) | collective-permute-done | bytes 368672 | tf_op jit(solution)/shard_map/ppermute | solution.py:335
  54.2 0.1 add_convert_fusion
  54.4 0.9 %pad_maximum_fusion = bf16[48,8192]{1,0:T(8,128)(2,1)} fusion(bf16[48,3840]{1,0:T(8,128)(2,1)S(1)} %add_convert_fusion, bf16[48,2560]{1,0:T(8,128)(2,1)S(1)} %add_convert_fusion.2, bf16[48,1792]{1,0:T(8,128)(2,1)S(1)} %add_convert_fusion.4), kind=kLoop, calls=%fused_computation | loop fusion | flops 2359296 | bytes 1572864 | tf_op jit(solution)/shard_map/concatenate | solution.py:340
  (3 shorter events, 0.1 us)
Async XLA Ops:
  1.0 8.0 %collective-permute-start = (bf16[192,512]{1,0:T(8,128)(2,1)S(1)}, bf16[192,512]{1,0:T(8,128)(2,1)S(1)}, u32[]{:S(2)}, u32[]{:S(2)}) collective-permute-start(bf16[192,512]{1,0:T(8,128)(2,1)S(1)} %join.1.refs_3_), channel_id=1, source_target_pairs={{0,8},{1,9},{2,10},{3,11},{4,12},{5,13},{6,14},{7,15},{8,0},{9,1},... | collective-permute-start | bytes 589832 | tf_op jit(solution)/shard_map/ppermute | solution.py:252
  4.1 4.9 %collective-permute-start.1 = (bf16[192,512]{1,0:T(8,128)(2,1)S(1)}, bf16[192,512]{1,0:T(8,128)(2,1)S(1)}, u32[]{:S(2)}, u32[]{:S(2)}) collective-permute-start(bf16[192,512]{1,0:T(8,128)(2,1)S(1)} %join.1.refs_3_), channel_id=1, source_target_pairs={{0,1},{1,0},{2,3},{3,2},{4,5},{5,4},{6,7},{7,6},{8,16},{9,17},{10,... | collective-permute-start | bytes 589832 | tf_op jit(solution)/shard_map/ppermute | solution.py:252
  4.1 17.0 %collective-permute-start.5 = (bf16[192,512]{1,0:T(8,128)(2,1)S(1)}, bf16[192,512]{1,0:T(8,128)(2,1)S(1)}, u32[]{:S(2)}, u32[]{:S(2)}) collective-permute-start(bf16[192,512]{1,0:T(8,128)(2,1)S(1)} %join.1.refs_3_), channel_id=1, source_target_pairs={{0,4},{1,5},{2,6},{3,7},{4,0},{5,1},{6,2},{7,3},{8,12},{9,13},{10,... | collective-permute-start | bytes 589832 | tf_op jit(solution)/shard_map/ppermute | solution.py:252
  9.0 6.9 %collective-permute-start.2 = (bf16[192,512]{1,0:T(8,128)(2,1)S(1)}, bf16[192,512]{1,0:T(8,128)(2,1)S(1)}, u32[]{:S(2)}, u32[]{:S(2)}) collective-permute-start(bf16[192,512]{1,0:T(8,128)(2,1)S(1)} %collective-permute-done.1), channel_id=1, source_target_pairs={{0,8},{1,9},{2,10},{3,11},{4,12},{5,13},{6,14},{7,15},{8,0},{9,1},... | collective-permute-start | bytes 589832 | tf_op jit(solution)/shard_map/ppermute | solution.py:252
  11.9 4.0 %collective-permute-start.3 = (bf16[192,512]{1,0:T(8,128)(2,1)S(1)}, bf16[192,512]{1,0:T(8,128)(2,1)S(1)}, u32[]{:S(2)}, u32[]{:S(2)}) collective-permute-start(bf16[192,512]{1,0:T(8,128)(2,1)S(1)} %collective-permute-done), channel_id=1, source_target_pairs={{0,1},{1,0},{2,3},{3,2},{4,5},{5,4},{6,7},{7,6},{8,16},{9,17},{10,... | collective-permute-start | bytes 589832 | tf_op jit(solution)/shard_map/ppermute | solution.py:252
  11.9 9.2 %collective-permute-start.6 = (bf16[192,512]{1,0:T(8,128)(2,1)S(1)}, bf16[192,512]{1,0:T(8,128)(2,1)S(1)}, u32[]{:S(2)}, u32[]{:S(2)}) collective-permute-start(bf16[192,512]{1,0:T(8,128)(2,1)S(1)} %broadcast_select_fusion.refs_5_), channel_id=1, source_target_pairs={{0,4},{1,5},{2,6},{3,7},{4,0},{5,1},{6,2},{7,3},{8,12},{9,13},{10,... | collective-permute-start | bytes 589832 | tf_op jit(solution)/shard_map/ppermute | solution.py:252
  15.9 5.1 %copy-start = (bf16[192,1024]{1,0:T(8,128)(2,1)S(1)}, bf16[192,1024]{1,0:T(8,128)(2,1)}, u32[]{:S(2)}) copy-start(bf16[192,1024]{1,0:T(8,128)(2,1)} %refs_0_.3) | copy-start | bytes 1179652
  15.9 8.5 %collective-permute-start.4 = (bf16[192,512]{1,0:T(8,128)(2,1)S(1)}, bf16[192,512]{1,0:T(8,128)(2,1)S(1)}, u32[]{:S(2)}, u32[]{:S(2)}) collective-permute-start(bf16[192,512]{1,0:T(8,128)(2,1)S(1)} %broadcast_select_fusion.1.refs_7_), channel_id=1, source_target_pairs={{0,4},{1,5},{2,6},{3,7},{4,0},{5,1},{6,2},{7,3},{8,12},{9,13},{10,... | collective-permute-start | bytes 589832 | tf_op jit(solution)/shard_map/ppermute | solution.py:252
  27.2 7.0 %collective-permute-start.7 = (bf16[96,1792]{1,0:T(8,128)(2,1)S(1)}, bf16[96,1792]{1,0:T(8,128)(2,1)S(1)}, u32[]{:S(2)}, u32[]{:S(2)}) collective-permute-start(bf16[96,1792]{1,0:T(8,128)(2,1)S(1)} %get-tuple-element.27), channel_id=1, source_target_pairs={{0,1},{1,0},{2,3},{3,2},{4,5},{5,4},{6,7},{7,6},{8,9},{9,8},{10,11... | collective-permute-start | bytes 1032200 | tf_op jit(solution)/shard_map/ppermute | solution.py:252
  31.7 4.1 %collective-permute-start.9 = (bf16[96,2560]{1,0:T(8,128)(2,1)S(1)}, bf16[96,2560]{1,0:T(8,128)(2,1)S(1)}, u32[]{:S(2)}, u32[]{:S(2)}) collective-permute-start(bf16[96,2560]{1,0:T(8,128)(2,1)S(1)} %get-tuple-element.30), channel_id=1, source_target_pairs={{0,1},{1,0},{2,3},{3,2},{4,5},{5,4},{6,7},{7,6},{8,9},{9,8},{10,11... | collective-permute-start | bytes 1474568 | tf_op jit(solution)/shard_map/ppermute | solution.py:252
  34.1 7.5 %collective-permute-start.11 = (bf16[96,3840]{1,0:T(8,128)(2,1)S(1)}, bf16[96,3840]{1,0:T(8,128)(2,1)S(1)}, u32[]{:S(2)}, u32[]{:S(2)}) collective-permute-start(bf16[96,3840]{1,0:T(8,128)(2,1)S(1)} %get-tuple-element.32), channel_id=1, source_target_pairs={{0,1},{1,0},{2,3},{3,2},{4,5},{5,4},{6,7},{7,6},{8,9},{9,8},{10,11... | collective-permute-start | bytes 2211848 | tf_op jit(solution)/shard_map/ppermute | solution.py:252
  34.2 7.3 %collective-permute-start.8 = (bf16[48,1792]{1,0:T(8,128)(2,1)S(1)}, bf16[48,1792]{1,0:T(8,128)(2,1)S(1)}, u32[]{:S(2)}, u32[]{:S(2)}) collective-permute-start(bf16[48,1792]{1,0:T(8,128)(2,1)S(1)} %add_convert_fusion.5), channel_id=1, source_target_pairs={{0,2},{1,3},{2,0},{3,1},{4,6},{5,7},{6,4},{7,5},{8,10},{9,11},{10,... | collective-permute-start | bytes 516104 | tf_op jit(solution)/shard_map/ppermute | solution.py:335
  35.9 10.9 %collective-permute-start.10 = (bf16[48,2560]{1,0:T(8,128)(2,1)S(1)}, bf16[48,2560]{1,0:T(8,128)(2,1)S(1)}, u32[]{:S(2)}, u32[]{:S(2)}) collective-permute-start(bf16[48,2560]{1,0:T(8,128)(2,1)S(1)} %add_convert_fusion.3), channel_id=1, source_target_pairs={{0,2},{1,3},{2,0},{3,1},{4,6},{5,7},{6,4},{7,5},{8,10},{9,11},{10,... | collective-permute-start | bytes 737288 | tf_op jit(solution)/shard_map/ppermute | solution.py:335
  41.7 12.5 %collective-permute-start.12 = (bf16[48,3840]{1,0:T(8,128)(2,1)S(1)}, bf16[48,3840]{1,0:T(8,128)(2,1)S(1)}, u32[]{:S(2)}, u32[]{:S(2)}) collective-permute-start(bf16[48,3840]{1,0:T(8,128)(2,1)S(1)} %add_convert_fusion.1), channel_id=1, source_target_pairs={{0,2},{1,3},{2,0},{3,1},{4,6},{5,7},{6,4},{7,5},{8,10},{9,11},{10,... | collective-permute-start | bytes 1105928 | tf_op jit(solution)/shard_map/ppermute | solution.py:335

commit v2 on v1

--- a/solution.py
+++ b/solution.py
@@ -19,7 +19,7 @@
 MIB = 1 << 20
 
 
-def routes(seq, tp):
+def routes(seq, tp, depth):
     rows = seq // 2
 
     def flat(rule):
@@ -30,22 +30,25 @@
                 pairs.append((s * tp + t, s2 * tp + t2))
         return pairs
 
-    def by_row(parity):
+    def by_row(parity, step):
         def rule(s, t):
             row, col = divmod(s, 2)
             other = row + 1 if row % 2 == parity else row - 1
-            if 0 <= other < rows:
+            if step - 1 <= min(row, other) and max(row, other) < rows:
                 return other * 2 + col, t
             return s, t ^ 1
 
         return flat(rule)
 
-    return {
-        "even": by_row(0),
-        "odd": by_row(1),
-        "col": flat(lambda s, t: (s ^ 1, t)),
-        "core": flat(lambda s, t: (s, t ^ 1)),
-    }
+    def by_col(step):
+        return flat(lambda s, t: (s ^ 1, t) if s // 2 >= step else (s, t ^ 1))
+
+    table = {("core", i): flat(lambda s, t: (s, t ^ 1)) for i in range(3)}
+    for step in range(depth + 1):
+        table["col", step] = by_col(step)
+        table["even", step] = by_row(0, step)
+        table["odd", step] = by_row(1, step)
+    return table
 
 
 def y_route(seq, tp, distance):
@@ -245,11 +248,11 @@
     chips = tp // 2
     reach = min(12, seq // 2)
     depth = (reach + 1) // 2
-    route = routes(seq, tp)
+    route = routes(seq, tp, depth)
     odd_row = (lax.axis_index("seq") // 2) % 2 == 1
 
-    def send(x, name):
-        return lax.ppermute(x, AXES, route[name])
+    def send(x, name, step):
+        return lax.ppermute(x, AXES, route[name, step])
 
     own = pl.pallas_call(
         join_kernel,
@@ -266,14 +269,17 @@
     weight = in_hbm(output_weight)
     near_weight = load_call(weight, 0, cuts[1])
     far_weight = load_call(weight, cuts[1], model)
-    even, odd = send(own, "even"), send(own, "odd")
-    blocks = [own, send(own, "col")]
+    even, odd = send(own, "even", 1), send(own, "odd", 1)
+    blocks = [own, send(own, "col", 0)]
     even, odd, docs, docs_t = lax.optimization_barrier((even, odd, docs, docs_t))
     for distance in range(1, depth + 1):
         blocks.append(jnp.where(odd_row, even, odd))
         if distance < depth:
-            even, odd = (send(odd, "even"), send(even, "odd"))
-        blocks.append(send(blocks[-1], "col"))
+            even, odd = (
+                send(odd, "even", distance + 1),
+                send(even, "odd", distance + 1),
+            )
+        blocks.append(send(blocks[-1], "col", distance))
     last_block = blocks.pop()
     count = len(blocks)
 
@@ -323,7 +329,7 @@
             sent, kept = project_call(
                 context, from_weight, start, stop - cuts[i - 1], part
             )
-        received = send(sent, "core")
+        received = send(sent, "core", i)
         moved = (
             kept[:remote].astype(jnp.float32) + received[:remote].astype(jnp.float32)
         ).astype(jnp.bfloat16)

time: 55.5 us -> 54.5 us (0.982)
  the two profiles are of different devices: /device:TPU:0 before, /device:TPU:20 now
where the time goes in v2:
time: 54.5 us; the launch traced here: 54.3 us
  waiting for transfers between devices  25 us (46%)
  Pallas kernels  16.8 us (31%)
  starting transfers between devices  9.97 us (18%)
  other arithmetic  2.17 us (4%)
    ppermute x3, waiting for transfers between devices, layer(): lax.ppermute(moved[at:at + part], AXES, y_route(seq, tp, distance))  16.9 us
    ppermute x10, waiting for transfers between devices, send(): return lax.ppermute(x, AXES, route[name, step])  8.08 us
    ppermute x10, starting transfers between devices, send(): return lax.ppermute(x, AXES, route[name, step])  7.24 us
    pallas_call x2, Pallas kernels, load_call(): pl.pallas_call(functools.partial(load_kernel, start), out_shape=pltpu.VME...  6.78 us
    pallas_call x1, Pallas kernels, layer(): pl.pallas_call(functools.partial(early_kernel, kv_local, group, count, 32...  3.39 us
    pallas_call x2, Pallas kernels, project_call(): pl.pallas_call(functools.partial(project_kernel, part, start), out_shape=...  3 us
    ppermute x3, starting transfers between devices, layer(): lax.ppermute(moved[at:at + part], AXES, y_route(seq, tp, distance))  2.72 us
    pallas_call x1, Pallas kernels, layer(): pl.pallas_call(functools.partial(late_kernel, kv_local, group, part, dept...  2.68 us
  transfers between devices with their start and end apart: 13, of which 7 were waited for; matrix products, arithmetic and copies ran while one was open for 2% of the time, Pallas kernels for 24%

profile of v2, /device:TPU:20, one launch (start us, length us, event | category | flops | bytes accessed | tf_op | source)
XLA Modules:
  0.0 54.3 jit_solution(6265454821830880551)
XLA Ops:
  0.0 1.0 %join.1.refs_3_ = bf16[192,512]{1,0:T(8,128)(2,1)S(1)} custom-call(bf16[192,256]{1,0:T(8,128)(2,1)} %k_ref.1, bf16[192,256]{1,0:T(8,128)(2,1)} %v_ref.1), custom_call_target="tpu_custom_call" | custom-call | tf_op jit(solution)/shard_map/join/pallas_call | solution.py:257
  1.0 1.6 %collective-permute-start = (bf16[192,512]{1,0:T(8,128)(2,1)S(1)}, bf16[192,512]{1,0:T(8,128)(2,1)S(1)}, u32[]{:S(2)}, u32[]{:S(2)}) collective-permute-start(bf16[192,512]{1,0:T(8,128)(2,1)S(1)} %join.1.refs_3_), channel_id=1, source_target_pairs={{0,8},{1,9},{2,10},{3,11},{4,12},{5,13},{6,14},{7,15},{8,0},{9,1},... | collective-permute-start | bytes 589832 | tf_op jit(solution)/shard_map/ppermute | solution.py:255
  2.6 0.0 collective-permute-start.1
  2.6 1.5 %collective-permute-start.5 = (bf16[192,512]{1,0:T(8,128)(2,1)S(1)}, bf16[192,512]{1,0:T(8,128)(2,1)S(1)}, u32[]{:S(2)}, u32[]{:S(2)}) collective-permute-start(bf16[192,512]{1,0:T(8,128)(2,1)S(1)} %join.1.refs_3_), channel_id=1, source_target_pairs={{0,4},{1,5},{2,6},{3,7},{4,0},{5,1},{6,2},{7,3},{8,12},{9,13},{10,... | collective-permute-start | bytes 589832 | tf_op jit(solution)/shard_map/ppermute | solution.py:255
  4.1 0.7 %convert_element_type.66 = f32[1536]{0:T(1024)S(1)} convert(s32[1536]{0:T(1024)} %param.8) | non-fusion elementwise | flops 1536 | bytes 12288 | tf_op jit(solution)/shard_map/convert_element_type | solution.py:266
  4.8 0.1 reshape.3.refs_1_
  4.9 0.1 copy.8
  5.0 2.7 %collective-permute-done = bf16[192,512]{1,0:T(8,128)(2,1)S(1)} collective-permute-done((bf16[192,512]{1,0:T(8,128)(2,1)S(1)}, bf16[192,512]{1,0:T(8,128)(2,1)S(1)}, u32[]{:S(2)}, u32[]{:S(2)}) %collective-permute-start) | collective-permute-done | bytes 196640 | tf_op jit(solution)/shard_map/ppermute | solution.py:255
  7.7 1.3 %collective-permute-done.1 = bf16[192,512]{1,0:T(8,128)(2,1)S(1)} collective-permute-done((bf16[192,512]{1,0:T(8,128)(2,1)S(1)}, bf16[192,512]{1,0:T(8,128)(2,1)S(1)}, u32[]{:S(2)}, u32[]{:S(2)}) %collective-permute-start.1) | collective-permute-done | bytes 196640 | tf_op jit(solution)/shard_map/ppermute | solution.py:255
  9.0 0.3 collective-permute-start.2
  9.3 0.0 collective-permute-start.3
  9.3 1.6 %collective-permute-start.6 = (bf16[192,512]{1,0:T(8,128)(2,1)S(1)}, bf16[192,512]{1,0:T(8,128)(2,1)S(1)}, u32[]{:S(2)}, u32[]{:S(2)}) collective-permute-start(bf16[192,512]{1,0:T(8,128)(2,1)S(1)} %broadcast_select_fusion.refs_5_), channel_id=1, source_target_pairs={{0,1},{1,0},{2,3},{3,2},{4,5},{5,4},{6,7},{7,6},{8,12},{9,13},{10,... | collective-permute-start | bytes 589832 | tf_op jit(solution)/shard_map/ppermute | solution.py:255
  10.8 3.8 %collective-permute-done.2 = bf16[192,512]{1,0:T(8,128)(2,1)S(1)} collective-permute-done((bf16[192,512]{1,0:T(8,128)(2,1)S(1)}, bf16[192,512]{1,0:T(8,128)(2,1)S(1)}, u32[]{:S(2)}, u32[]{:S(2)}) %collective-permute-start.2) | collective-permute-done | bytes 196640 | tf_op jit(solution)/shard_map/ppermute | solution.py:255
  14.6 0.3 collective-permute-done.3
  14.9 0.0 copy-start
  15.0 1.6 %collective-permute-start.4 = (bf16[192,512]{1,0:T(8,128)(2,1)S(1)}, bf16[192,512]{1,0:T(8,128)(2,1)S(1)}, u32[]{:S(2)}, u32[]{:S(2)}) collective-permute-start(bf16[192,512]{1,0:T(8,128)(2,1)S(1)} %broadcast_select_fusion.1.refs_7_), channel_id=1, source_target_pairs={{0,1},{1,0},{2,3},{3,2},{4,5},{5,4},{6,7},{7,6},{8,9},{9,8},{10,11... | collective-permute-start | bytes 589832 | tf_op jit(solution)/shard_map/ppermute | solution.py:255
  16.5 3.5 %load.2.refs_7_.w_ref = bf16[1024,4352]{1,0:T(8,128)(2,1)S(1)} custom-call(bf16[1024,8192]{1,0:T(8,128)(2,1)} %w_hbm.3), custom_call_target="tpu_custom_call" | custom-call | bytes 8912896 | tf_op jit(solution)/shard_map/load/pallas_call | solution.py:83
  20.1 0.0 collective-permute-done.5.refs_4_
  20.1 0.0 collective-permute-done.6.refs_6_
  20.1 0.0 copy-done
  20.1 3.4 %attend_early.1 = (f32[1536,128]{1,0:T(8,128)S(1)}, f32[1536,128]{1,0:T(8,128)S(1)}, f32[1536,128]{1,0:T(8,128)S(1)}) custom-call(bf16[192,1024]{1,0:T(8,128)(2,1)S(1)} %copy-done, f32[8,192]{1,0:T(8,128)S(1)} %reshape.3.refs_1_, f32[192,8]{1,0:T(8,128)S(1)} %bitcast.1, bf16[192,512]{1,0:T(8,128)(2,1)S(1)} %join.1.refs_3_, ...), custom_call_target="tpu_custom_call" | custom-call | flops 754974720 | bytes 786432 | tf_op jit(solution)/shard_map/attend_early/pallas_call | solution.py:288
  23.5 0.0 collective-permute-done.4.refs_3_
  23.5 2.7 %attend_late.1 = (bf16[192,1024]{1,0:T(8,128)(2,1)S(1)}, bf16[96,1792]{1,0:T(8,128)(2,1)S(1)}, bf16[96,1792]{1,0:T(8,128)(2,1)S(1)}) custom-call(bf16[192,1024]{1,0:T(8,128)(2,1)S(1)} %copy-done, f32[8,192]{1,0:T(8,128)S(1)} %reshape.3.refs_1_, f32[192,8]{1,0:T(8,128)S(1)} %bitcast.2, bf16[192,512]{1,0:T(8,128)(2,1)S(1)} %collective-permute-done.4.refs_3_, ...), custom_call_target="tpu_custom_call" | custom-call | flops 855638016 | bytes 4456448 | tf_op jit(solution)/shard_map/attend_late/pallas_call | solution.py:308
  26.2 0.1 collective-permute-start.7
  26.3 3.2 %load.3.w_ref = bf16[1024,3840]{1,0:T(8,128)(2,1)S(1)} custom-call(bf16[1024,8192]{1,0:T(8,128)(2,1)} %w_hbm.3), custom_call_target="tpu_custom_call" | custom-call | bytes 7864320 | tf_op jit(solution)/shard_map/load/pallas_call | solution.py:83
  29.5 1.2 %project_rest.2 = (bf16[96,2560]{1,0:T(8,128)(2,1)S(1)}, bf16[96,2560]{1,0:T(8,128)(2,1)S(1)}) custom-call(bf16[192,1024]{1,0:T(8,128)(2,1)S(1)} %get-tuple-element.28.context_ref, bf16[1024,4352]{1,0:T(8,128)(2,1)S(1)} %load.2.refs_7_.w_ref), custom_call_target="tpu_custom_call" | custom-call | flops 1006632960 | bytes 5242880 | tf_op jit(solution)/shard_map/project_rest/pallas_call | solution.py:225
  30.7 0.6 %collective-permute-start.9 = (bf16[96,2560]{1,0:T(8,128)(2,1)S(1)}, bf16[96,2560]{1,0:T(8,128)(2,1)S(1)}, u32[]{:S(2)}, u32[]{:S(2)}) collective-permute-start(bf16[96,2560]{1,0:T(8,128)(2,1)S(1)} %get-tuple-element.30), channel_id=1, source_target_pairs={{0,1},{1,0},{2,3},{3,2},{4,5},{5,4},{6,7},{7,6},{8,9},{9,8},{10,11... | collective-permute-start | bytes 1474568 | tf_op jit(solution)/shard_map/ppermute | solution.py:255
  31.3 1.8 %project_rest.3 = (bf16[96,3840]{1,0:T(8,128)(2,1)S(1)}, bf16[96,3840]{1,0:T(8,128)(2,1)S(1)}) custom-call(bf16[192,1024]{1,0:T(8,128)(2,1)S(1)} %get-tuple-element.28.context_ref, bf16[1024,3840]{1,0:T(8,128)(2,1)S(1)} %load.3.w_ref), custom_call_target="tpu_custom_call" | custom-call | flops 1509949440 | bytes 7864320 | tf_op jit(solution)/shard_map/project_rest/pallas_call | solution.py:225
  33.1 0.1 collective-permute-start.11
  33.2 0.0 collective-permute-done.7
  33.2 0.6 %collective-permute-start.8 = (bf16[48,1792]{1,0:T(8,128)(2,1)S(1)}, bf16[48,1792]{1,0:T(8,128)(2,1)S(1)}, u32[]{:S(2)}, u32[]{:S(2)}) collective-permute-start(bf16[48,1792]{1,0:T(8,128)(2,1)S(1)} %add_convert_fusion.5), channel_id=1, source_target_pairs={{0,2},{1,3},{2,0},{3,1},{4,6},{5,7},{6,4},{7,5},{8,10},{9,11},{10,... | collective-permute-start | bytes 516104 | tf_op jit(solution)/shard_map/ppermute | solution.py:341
  33.8 0.0 collective-permute-done.9
  33.8 0.1 add_convert_fusion.3
  33.9 1.6 %collective-permute-start.10 = (bf16[48,2560]{1,0:T(8,128)(2,1)S(1)}, bf16[48,2560]{1,0:T(8,128)(2,1)S(1)}, u32[]{:S(2)}, u32[]{:S(2)}) collective-permute-start(bf16[48,2560]{1,0:T(8,128)(2,1)S(1)} %add_convert_fusion.3), channel_id=1, source_target_pairs={{0,2},{1,3},{2,0},{3,1},{4,6},{5,7},{6,4},{7,5},{8,10},{9,11},{10,... | collective-permute-start | bytes 737288 | tf_op jit(solution)/shard_map/ppermute | solution.py:341
  35.5 5.1 %collective-permute-done.8 = bf16[48,1792]{1,0:T(8,128)(2,1)S(1)} collective-permute-done((bf16[48,1792]{1,0:T(8,128)(2,1)S(1)}, bf16[48,1792]{1,0:T(8,128)(2,1)S(1)}, u32[]{:S(2)}, u32[]{:S(2)}) %collective-permute-start.8) | collective-permute-done | bytes 172064 | tf_op jit(solution)/shard_map/ppermute | solution.py:341
  40.6 0.1 add_convert_fusion.4
  40.6 0.0 collective-permute-done.11
  40.6 0.1 add_convert_fusion.1
  40.7 0.6 %collective-permute-start.12 = (bf16[48,3840]{1,0:T(8,128)(2,1)S(1)}, bf16[48,3840]{1,0:T(8,128)(2,1)S(1)}, u32[]{:S(2)}, u32[]{:S(2)}) collective-permute-start(bf16[48,3840]{1,0:T(8,128)(2,1)S(1)} %add_convert_fusion.1), channel_id=1, source_target_pairs={{0,2},{1,3},{2,0},{3,1},{4,6},{5,7},{6,4},{7,5},{8,10},{9,11},{10,... | collective-permute-start | bytes 1105928 | tf_op jit(solution)/shard_map/ppermute | solution.py:341
  41.3 4.5 %collective-permute-done.10 = bf16[48,2560]{1,0:T(8,128)(2,1)S(1)} collective-permute-done((bf16[48,2560]{1,0:T(8,128)(2,1)S(1)}, bf16[48,2560]{1,0:T(8,128)(2,1)S(1)}, u32[]{:S(2)}, u32[]{:S(2)}) %collective-permute-start.10) | collective-permute-done | bytes 245792 | tf_op jit(solution)/shard_map/ppermute | solution.py:341
  45.8 0.1 add_convert_fusion.2
  45.9 7.3 %collective-permute-done.12 = bf16[48,3840]{1,0:T(8,128)(2,1)S(1)} collective-permute-done((bf16[48,3840]{1,0:T(8,128)(2,1)S(1)}, bf16[48,3840]{1,0:T(8,128)(2,1)S(1)}, u32[]{:S(2)}, u32[]{:S(2)}) %collective-permute-start.12) | collective-permute-done | bytes 368672 | tf_op jit(solution)/shard_map/ppermute | solution.py:341
  53.2 0.1 add_convert_fusion
  53.4 0.9 %pad_maximum_fusion = bf16[48,8192]{1,0:T(8,128)(2,1)} fusion(bf16[48,3840]{1,0:T(8,128)(2,1)S(1)} %add_convert_fusion, bf16[48,2560]{1,0:T(8,128)(2,1)S(1)} %add_convert_fusion.2, bf16[48,1792]{1,0:T(8,128)(2,1)S(1)} %add_convert_fusion.4), kind=kLoop, calls=%fused_computation | loop fusion | flops 2359296 | bytes 1572864 | tf_op jit(solution)/shard_map/concatenate | solution.py:346
  (3 shorter events, 0.1 us)
Async XLA Ops:
  1.0 6.7 %collective-permute-start = (bf16[192,512]{1,0:T(8,128)(2,1)S(1)}, bf16[192,512]{1,0:T(8,128)(2,1)S(1)}, u32[]{:S(2)}, u32[]{:S(2)}) collective-permute-start(bf16[192,512]{1,0:T(8,128)(2,1)S(1)} %join.1.refs_3_), channel_id=1, source_target_pairs={{0,8},{1,9},{2,10},{3,11},{4,12},{5,13},{6,14},{7,15},{8,0},{9,1},... | collective-permute-start | bytes 589832 | tf_op jit(solution)/shard_map/ppermute | solution.py:255
  2.6 6.4 %collective-permute-start.1 = (bf16[192,512]{1,0:T(8,128)(2,1)S(1)}, bf16[192,512]{1,0:T(8,128)(2,1)S(1)}, u32[]{:S(2)}, u32[]{:S(2)}) collective-permute-start(bf16[192,512]{1,0:T(8,128)(2,1)S(1)} %join.1.refs_3_), channel_id=1, source_target_pairs={{0,1},{1,0},{2,3},{3,2},{4,5},{5,4},{6,7},{7,6},{8,16},{9,17},{10,... | collective-permute-start | bytes 589832 | tf_op jit(solution)/shard_map/ppermute | solution.py:255
  2.6 17.5 %collective-permute-start.5 = (bf16[192,512]{1,0:T(8,128)(2,1)S(1)}, bf16[192,512]{1,0:T(8,128)(2,1)S(1)}, u32[]{:S(2)}, u32[]{:S(2)}) collective-permute-start(bf16[192,512]{1,0:T(8,128)(2,1)S(1)} %join.1.refs_3_), channel_id=1, source_target_pairs={{0,4},{1,5},{2,6},{3,7},{4,0},{5,1},{6,2},{7,3},{8,12},{9,13},{10,... | collective-permute-start | bytes 589832 | tf_op jit(solution)/shard_map/ppermute | solution.py:255
  9.0 5.7 %collective-permute-start.2 = (bf16[192,512]{1,0:T(8,128)(2,1)S(1)}, bf16[192,512]{1,0:T(8,128)(2,1)S(1)}, u32[]{:S(2)}, u32[]{:S(2)}) collective-permute-start(bf16[192,512]{1,0:T(8,128)(2,1)S(1)} %collective-permute-done.1), channel_id=1, source_target_pairs={{0,1},{1,0},{2,3},{3,2},{4,5},{5,4},{6,7},{7,6},{8,9},{9,8},{10,11... | collective-permute-start | bytes 589832 | tf_op jit(solution)/shard_map/ppermute | solution.py:255
  9.3 5.7 %collective-permute-start.3 = (bf16[192,512]{1,0:T(8,128)(2,1)S(1)}, bf16[192,512]{1,0:T(8,128)(2,1)S(1)}, u32[]{:S(2)}, u32[]{:S(2)}) collective-permute-start(bf16[192,512]{1,0:T(8,128)(2,1)S(1)} %collective-permute-done), channel_id=1, source_target_pairs={{0,1},{1,0},{2,3},{3,2},{4,5},{5,4},{6,7},{7,6},{8,16},{9,17},{10,... | collective-permute-start | bytes 589832 | tf_op jit(solution)/shard_map/ppermute | solution.py:255
  9.3 10.8 %collective-permute-start.6 = (bf16[192,512]{1,0:T(8,128)(2,1)S(1)}, bf16[192,512]{1,0:T(8,128)(2,1)S(1)}, u32[]{:S(2)}, u32[]{:S(2)}) collective-permute-start(bf16[192,512]{1,0:T(8,128)(2,1)S(1)} %broadcast_select_fusion.refs_5_), channel_id=1, source_target_pairs={{0,1},{1,0},{2,3},{3,2},{4,5},{5,4},{6,7},{7,6},{8,12},{9,13},{10,... | collective-permute-start | bytes 589832 | tf_op jit(solution)/shard_map/ppermute | solution.py:255
  14.9 5.1 %copy-start = (bf16[192,1024]{1,0:T(8,128)(2,1)S(1)}, bf16[192,1024]{1,0:T(8,128)(2,1)}, u32[]{:S(2)}) copy-start(bf16[192,1024]{1,0:T(8,128)(2,1)} %refs_0_.3) | copy-start | bytes 1179652
  15.0 8.5 %collective-permute-start.4 = (bf16[192,512]{1,0:T(8,128)(2,1)S(1)}, bf16[192,512]{1,0:T(8,128)(2,1)S(1)}, u32[]{:S(2)}, u32[]{:S(2)}) collective-permute-start(bf16[192,512]{1,0:T(8,128)(2,1)S(1)} %broadcast_select_fusion.1.refs_7_), channel_id=1, source_target_pairs={{0,1},{1,0},{2,3},{3,2},{4,5},{5,4},{6,7},{7,6},{8,9},{9,8},{10,11... | collective-permute-start | bytes 589832 | tf_op jit(solution)/shard_map/ppermute | solution.py:255
  26.2 7.0 %collective-permute-start.7 = (bf16[96,1792]{1,0:T(8,128)(2,1)S(1)}, bf16[96,1792]{1,0:T(8,128)(2,1)S(1)}, u32[]{:S(2)}, u32[]{:S(2)}) collective-permute-start(bf16[96,1792]{1,0:T(8,128)(2,1)S(1)} %get-tuple-element.27), channel_id=1, source_target_pairs={{0,1},{1,0},{2,3},{3,2},{4,5},{5,4},{6,7},{7,6},{8,9},{9,8},{10,11... | collective-permute-start | bytes 1032200 | tf_op jit(solution)/shard_map/ppermute | solution.py:255
  30.7 3.1 %collective-permute-start.9 = (bf16[96,2560]{1,0:T(8,128)(2,1)S(1)}, bf16[96,2560]{1,0:T(8,128)(2,1)S(1)}, u32[]{:S(2)}, u32[]{:S(2)}) collective-permute-start(bf16[96,2560]{1,0:T(8,128)(2,1)S(1)} %get-tuple-element.30), channel_id=1, source_target_pairs={{0,1},{1,0},{2,3},{3,2},{4,5},{5,4},{6,7},{7,6},{8,9},{9,8},{10,11... | collective-permute-start | bytes 1474568 | tf_op jit(solution)/shard_map/ppermute | solution.py:255
  33.1 7.5 %collective-permute-start.11 = (bf16[96,3840]{1,0:T(8,128)(2,1)S(1)}, bf16[96,3840]{1,0:T(8,128)(2,1)S(1)}, u32[]{:S(2)}, u32[]{:S(2)}) collective-permute-start(bf16[96,3840]{1,0:T(8,128)(2,1)S(1)} %get-tuple-element.32), channel_id=1, source_target_pairs={{0,1},{1,0},{2,3},{3,2},{4,5},{5,4},{6,7},{7,6},{8,9},{9,8},{10,11... | collective-permute-start | bytes 2211848 | tf_op jit(solution)/shard_map/ppermute | solution.py:255
  33.2 7.3 %collective-permute-start.8 = (bf16[48,1792]{1,0:T(8,128)(2,1)S(1)}, bf16[48,1792]{1,0:T(8,128)(2,1)S(1)}, u32[]{:S(2)}, u32[]{:S(2)}) collective-permute-start(bf16[48,1792]{1,0:T(8,128)(2,1)S(1)} %add_convert_fusion.5), channel_id=1, source_target_pairs={{0,2},{1,3},{2,0},{3,1},{4,6},{5,7},{6,4},{7,5},{8,10},{9,11},{10,... | collective-permute-start | bytes 516104 | tf_op jit(solution)/shard_map/ppermute | solution.py:341
  33.9 11.9 %collective-permute-start.10 = (bf16[48,2560]{1,0:T(8,128)(2,1)S(1)}, bf16[48,2560]{1,0:T(8,128)(2,1)S(1)}, u32[]{:S(2)}, u32[]{:S(2)}) collective-permute-start(bf16[48,2560]{1,0:T(8,128)(2,1)S(1)} %add_convert_fusion.3), channel_id=1, source_target_pairs={{0,2},{1,3},{2,0},{3,1},{4,6},{5,7},{6,4},{7,5},{8,10},{9,11},{10,... | collective-permute-start | bytes 737288 | tf_op jit(solution)/shard_map/ppermute | solution.py:341
  40.7 12.5 %collective-permute-start.12 = (bf16[48,3840]{1,0:T(8,128)(2,1)S(1)}, bf16[48,3840]{1,0:T(8,128)(2,1)S(1)}, u32[]{:S(2)}, u32[]{:S(2)}) collective-permute-start(bf16[48,3840]{1,0:T(8,128)(2,1)S(1)} %add_convert_fusion.1), channel_id=1, source_target_pairs={{0,2},{1,3},{2,0},{3,1},{4,6},{5,7},{6,4},{7,5},{8,10},{9,11},{10,... | collective-permute-start | bytes 1105928 | tf_op jit(solution)/shard_map/ppermute | solution.py:341

commit v3 on v2

--- a/solution.py
+++ b/solution.py
@@ -17,6 +17,9 @@
 VMEM = pl.BlockSpec(memory_space=pltpu.VMEM)
 ANY = pl.BlockSpec(memory_space=pl.ANY)
 MIB = 1 << 20
+CUTS = (7, 17, 32)
+NEAR = 12
+EARLY, LATE, PROJ = 24, 16, 8
 
 
 def routes(seq, tp, depth):
@@ -43,7 +46,7 @@
     def by_col(step):
         return flat(lambda s, t: (s ^ 1, t) if s // 2 >= step else (s, t ^ 1))
 
-    table = {("core", i): flat(lambda s, t: (s, t ^ 1)) for i in range(3)}
+    table = {("core", i): flat(lambda s, t: (s, t ^ 1)) for i in range(len(CUTS))}
     for step in range(depth + 1):
         table["col", step] = by_col(step)
         table["even", step] = by_row(0, step)
@@ -71,23 +74,33 @@
         copy.wait()
 
 
-def load_kernel(start, w_hbm, out_ref, sem):
-    width = out_ref.shape[1]
-    copy = pltpu.make_async_copy(w_hbm.at[:, pl.ds(start, width)], out_ref, sem)
-    copy.start()
-    copy.wait()
-
-
-def load_call(weight, start, stop):
-    shape = (weight.shape[0], stop - start)
+def load_kernel(start, w_hbm, *refs):
+    *outs, sems = refs
+    copies = []
+    for i, out in enumerate(outs):
+        width = out.shape[1]
+        source = w_hbm.at[:, pl.ds(start, width)]
+        copies.append(pltpu.make_async_copy(source, out, sems.at[i]))
+        start += width
+    for copy in copies:
+        copy.start()
+    for copy in copies:
+        copy.wait()
+
+
+def load_call(weight, cuts):
+    depth = weight.shape[0]
+    widths = [stop - start for start, stop in zip(cuts, cuts[1:])]
     return pl.pallas_call(
-        functools.partial(load_kernel, start),
-        out_shape=pltpu.VMEM(shape, weight.dtype),
+        functools.partial(load_kernel, cuts[0]),
+        out_shape=[pltpu.VMEM((depth, width), weight.dtype) for width in widths],
         in_specs=[ANY],
-        out_specs=VMEM,
-        scratch_shapes=[pltpu.SemaphoreType.DMA],
+        out_specs=[VMEM] * len(widths),
+        scratch_shapes=[pltpu.SemaphoreType.DMA((len(widths),))],
         cost_estimate=pl.CostEstimate(
-            flops=0, transcendentals=0, bytes_accessed=2 * shape[0] * shape[1]
+            flops=0,
+            transcendentals=0,
+            bytes_accessed=2 * depth * (cuts[-1] - cuts[0]),
         ),
         compiler_params=pltpu.CompilerParams(vmem_limit_bytes=MIB),
         name="load",
@@ -98,10 +111,17 @@
     return pltpu.with_memory_space_constraint(x, pltpu.HBM)
 
 
-def query_doc(docs_t_ref, me):
-    docs = docs_t_ref[...]
-    lane = lax.broadcasted_iota(jnp.int32, docs.shape, 1)
-    return jnp.sum(jnp.where(lane == me, docs, 0.0), axis=1, keepdims=True)
+def query_doc(docs_ref, me):
+    docs = docs_ref[...]
+    own = lax.broadcasted_iota(jnp.int32, (docs.shape[0], HD), 0) == me
+    column = lax.dot_general(
+        docs,
+        own.astype(jnp.float32),
+        (((0,), (0,)), ((), ())),
+        precision=lax.Precision.HIGHEST,
+        preferred_element_type=jnp.float32,
+    )
+    return column[:, :1]
 
 
 def key_doc(docs_ref, block, me):
@@ -122,10 +142,10 @@
 
 
 def early_kernel(kv_local, group, count, step, *refs):
-    q_ref, docs_ref, docs_t_ref = refs[:3]
-    blocks = refs[3 : 3 + count]
-    acc_ref, top_ref, sum_ref = refs[3 + count : 6 + count]
-    bias_ref, s_ref, p_ref = refs[6 + count :]
+    q_ref, docs_ref = refs[:2]
+    blocks = refs[2 : 2 + count]
+    acc_ref, top_ref, sum_ref = refs[2 + count : 5 + count]
+    bias_ref, s_ref, p_ref = refs[5 + count :]
     tokens = q_ref.shape[0]
     stacked = group * tokens
     me = lax.axis_index("seq")
@@ -134,7 +154,7 @@
     for i in range(count):
         block = me - i if i % 2 == 0 else (row - i // 2) * 2 + 1 - col
         docs.append(key_doc(docs_ref, block, me))
-    allowed = query_doc(docs_t_ref, me) == jnp.concatenate(docs, axis=1)
+    allowed = query_doc(docs_ref, me) == jnp.concatenate(docs, axis=1)
     key_at = lax.broadcasted_iota(jnp.int32, (tokens, count * tokens), 1)
     query_at = lax.broadcasted_iota(jnp.int32, (tokens, count * tokens), 0)
     allowed = allowed & ((key_at <= query_at) | (key_at >= tokens))
@@ -159,13 +179,13 @@
         )
 
 
-def project(context_ref, w_ref, start, width, send_ref, keep_ref, part):
+def project(context_ref, w_ref, send_ref, keep_ref, part):
     step = 256
-    for c in range(0, width, step):
+    for c in range(0, w_ref.shape[1], step):
         at = pl.ds(c, step)
         rows = jnp.dot(
             context_ref[...],
-            w_ref[:, pl.ds(start + c, step)],
+            w_ref[:, at],
             preferred_element_type=jnp.float32,
         ).astype(jnp.bfloat16)
         for i in range(rows.shape[0] // (2 * part)):
@@ -175,15 +195,15 @@
 
 
 def late_kernel(kv_local, group, part, depth, *refs):
-    q_ref, docs_ref, docs_t_ref, block, acc_ref, top_ref, sum_ref, w_ref = refs[:8]
-    out_ref, send_ref, keep_ref, context_ref = refs[8:]
+    q_ref, docs_ref, block, acc_ref, top_ref, sum_ref, w_ref = refs[:7]
+    out_ref, send_ref, keep_ref, context_ref = refs[7:]
     tokens = q_ref.shape[0]
     stacked = group * tokens
     me, rank = lax.axis_index("seq"), lax.axis_index("tp")
     chips = lax.axis_size("tp") // 2
     far = (me // 2 - depth) * 2 + 1 - me % 2
     bias = jnp.where(
-        query_doc(docs_t_ref, me) == key_doc(docs_ref, far, me), 0.0, -jnp.inf
+        query_doc(docs_ref, me) == key_doc(docs_ref, far, me), 0.0, -jnp.inf
     )
     for h in range(kv_local):
         keys = block[:, pl.ds(h * HD, HD)]
@@ -211,30 +231,35 @@
             first = pl.multiple_of((base + core) * part, 8)
             out_ref[pl.ds(at, part), :] = context_ref[pl.ds(first, part), :]
             at += part
-    project(out_ref, w_ref, 0, send_ref.shape[1], send_ref, keep_ref, part)
-
-
-def project_kernel(part, start, context_ref, w_ref, send_ref, keep_ref):
-    width = send_ref.shape[1]
-    project(context_ref, w_ref, start, width, send_ref, keep_ref, part)
-
-
-def project_call(context, weight, start, width, part):
+    project(out_ref, w_ref, send_ref, keep_ref, part)
+
+
+def project_kernel(part, context_ref, *refs):
+    *weights, send_ref, keep_ref = refs
+    start = 0
+    for w_ref in weights:
+        cols = pl.ds(start, w_ref.shape[1])
+        project(context_ref, w_ref, send_ref.at[:, cols], keep_ref.at[:, cols], part)
+        start += w_ref.shape[1]
+
+
+def project_call(context, weights, part):
     tokens, depth = context.shape
+    width = sum(weight.shape[1] for weight in weights)
     out = jax.ShapeDtypeStruct((tokens // 2, width), jnp.bfloat16)
     return pl.pallas_call(
-        functools.partial(project_kernel, part, start),
+        functools.partial(project_kernel, part),
         out_shape=(out, out),
-        in_specs=[VMEM, VMEM],
+        in_specs=[VMEM] * (1 + len(weights)),
         out_specs=(VMEM, VMEM),
         cost_estimate=pl.CostEstimate(
             flops=2 * tokens * depth * width,
             transcendentals=0,
             bytes_accessed=2 * depth * width,
         ),
-        compiler_params=pltpu.CompilerParams(vmem_limit_bytes=8 * MIB),
+        compiler_params=pltpu.CompilerParams(vmem_limit_bytes=PROJ * MIB),
         name="project_rest",
-    )(context, weight)
+    )(context, *weights)
 
 
 def layer(query_rows, key_rows, value_rows, document_ids, output_weight):
@@ -264,14 +289,15 @@
         name="join",
     )(in_hbm(key_rows), in_hbm(value_rows))
     docs = document_ids.astype(jnp.float32).reshape(seq, tokens)
-    docs_t = docs.T
-    cuts = [model * 7 // 32, model * 17 // 32, model]
+    cuts = [model * n // 32 for n in (0, *CUTS)]
+    near = model * NEAR // 32
     weight = in_hbm(output_weight)
-    near_weight = load_call(weight, 0, cuts[1])
-    far_weight = load_call(weight, cuts[1], model)
+    first, *middle = load_call(weight, (0, cuts[1], near))
+    *rest, last = load_call(weight, (near, *cuts[2:]))
+    weights = [[first], middle + rest, [last]]
     even, odd = send(own, "even", 1), send(own, "odd", 1)
     blocks = [own, send(own, "col", 0)]
-    even, odd, docs, docs_t = lax.optimization_barrier((even, odd, docs, docs_t))
+    even, odd, docs = lax.optimization_barrier((even, odd, docs))
     for distance in range(1, depth + 1):
         blocks.append(jnp.where(odd_row, even, odd))
         if distance < depth:
@@ -288,7 +314,7 @@
     acc, top, total = pl.pallas_call(
         functools.partial(early_kernel, kv_local, group, count, 32),
         out_shape=(state, state, state),
-        in_specs=[VMEM] * (3 + count),
+        in_specs=[VMEM] * (2 + count),
         out_specs=(VMEM,) * 3,
         scratch_shapes=[
             pltpu.VMEM((tokens, count * tokens), jnp.float32),
@@ -300,35 +326,31 @@
             transcendentals=tokens * tokens * count * width // HD,
             bytes_accessed=4 * tokens * width,
         ),
-        compiler_params=pltpu.CompilerParams(vmem_limit_bytes=24 * MIB),
+        compiler_params=pltpu.CompilerParams(vmem_limit_bytes=EARLY * MIB),
         name="attend_early",
-    )(query_rows, docs, docs_t, *blocks)
-
-    out = jax.ShapeDtypeStruct((tokens // 2, cuts[0]), jnp.bfloat16)
+    )(query_rows, docs, *blocks)
+
+    out = jax.ShapeDtypeStruct((tokens // 2, cuts[1]), jnp.bfloat16)
     context, sent, kept = pl.pallas_call(
         functools.partial(late_kernel, kv_local, group, part, depth),
         out_shape=(jax.ShapeDtypeStruct((tokens, width), jnp.bfloat16), out, out),
-        in_specs=[VMEM] * 8,
+        in_specs=[VMEM] * 7,
         out_specs=(VMEM, VMEM, VMEM),
         scratch_shapes=[pltpu.VMEM((tokens, width), jnp.bfloat16)],
         cost_estimate=pl.CostEstimate(
-            flops=4 * tokens * tokens * width + 2 * tokens * width * cuts[0],
+            flops=4 * tokens * tokens * width + 2 * tokens * width * cuts[1],
             transcendentals=tokens * tokens * width // HD,
-            bytes_accessed=4 * tokens * width + 2 * width * cuts[0],
+            bytes_accessed=4 * tokens * width + 2 * width * cuts[1],
         ),
-        compiler_params=pltpu.CompilerParams(vmem_limit_bytes=16 * MIB),
+        compiler_params=pltpu.CompilerParams(vmem_limit_bytes=LATE * MIB),
         name="attend_late",
-    )(query_rows, docs, docs_t, last_block, acc, top, total, near_weight)
+    )(query_rows, docs, last_block, acc, top, total, first)
 
     pieces = []
     remote = (chips - 1) * part
-    for i, stop in enumerate(cuts):
+    for i, weight in enumerate(weights):
         if i:
-            from_weight = near_weight if i == 1 else far_weight
-            start = cuts[0] if i == 1 else 0
-            sent, kept = project_call(
-                context, from_weight, start, stop - cuts[i - 1], part
-            )
+            sent, kept = project_call(context, weight, part)
         received = send(sent, "core", i)
         moved = (
             kept[:remote].astype(jnp.float32) + received[:remote].astype(jnp.float32)

time: 54.5 us -> 55.7 us (1.022)
  starting transfers between devices: 9.97 us -> 11.5 us
    ppermute x10, starting transfers between devices: 7.24 us -> 8.78 us  [send(): return lax.ppermute(x, AXES, route[name, step])]
where the time goes in v3:
time: 55.7 us; the launch traced here: 55.6 us
  waiting for transfers between devices  24.7 us (44%)
  Pallas kernels  17 us (31%)
  starting transfers between devices  11.5 us (21%)
  other arithmetic  2.17 us (4%)
    ppermute x3, waiting for transfers between devices, layer(): lax.ppermute(moved[at:at + part], AXES, y_route(seq, tp, distance))  16.9 us
    ppermute x10, starting transfers between devices, send(): return lax.ppermute(x, AXES, route[name, step])  8.78 us
    ppermute x10, waiting for transfers between devices, send(): return lax.ppermute(x, AXES, route[name, step])  7.76 us
    pallas_call x2, Pallas kernels, load_call(): pl.pallas_call(functools.partial(load_kernel, cuts[0]), out_shape=[pltpu....  6.94 us
    pallas_call x1, Pallas kernels, layer(): pl.pallas_call(functools.partial(early_kernel, kv_local, group, count, 32...  3.7 us
    pallas_call x2, Pallas kernels, project_call(): pl.pallas_call(functools.partial(project_kernel, part), out_shape=(out, o...  2.93 us
    ppermute x3, starting transfers between devices, layer(): lax.ppermute(moved[at:at + part], AXES, y_route(seq, tp, distance))  2.73 us
    pallas_call x1, Pallas kernels, layer(): pl.pallas_call(functools.partial(late_kernel, kv_local, group, part, dept...  2.42 us
  transfers between devices with their start and end apart: 13, of which 7 were waited for; matrix products, arithmetic and copies ran while one was open for 2% of the time, Pallas kernels for 24%

profile of v3, /device:TPU:20, one launch (start us, length us, event | category | flops | bytes accessed | tf_op | source)
XLA Modules:
  0.0 55.6 jit_solution(11667489277587025148)
XLA Ops:
  0.0 1.0 %join.1.refs_2_ = bf16[192,512]{1,0:T(8,128)(2,1)S(1)} custom-call(bf16[192,256]{1,0:T(8,128)(2,1)} %k_ref.1, bf16[192,256]{1,0:T(8,128)(2,1)} %v_ref.1), custom_call_target="tpu_custom_call" | custom-call | tf_op jit(solution)/shard_map/join/pallas_call | solution.py:282
  1.0 0.5 collective-permute-start.1
  1.5 1.2 %collective-permute-start = (bf16[192,512]{1,0:T(8,128)(2,1)S(1)}, bf16[192,512]{1,0:T(8,128)(2,1)S(1)}, u32[]{:S(2)}, u32[]{:S(2)}) collective-permute-start(bf16[192,512]{1,0:T(8,128)(2,1)S(1)} %join.1.refs_2_), channel_id=1, source_target_pairs={{0,8},{1,9},{2,10},{3,11},{4,12},{5,13},{6,14},{7,15},{8,0},{9,1},... | collective-permute-start | bytes 589832 | tf_op jit(solution)/shard_map/ppermute | solution.py:280
  2.7 1.5 %collective-permute-start.5 = (bf16[192,512]{1,0:T(8,128)(2,1)S(1)}, bf16[192,512]{1,0:T(8,128)(2,1)S(1)}, u32[]{:S(2)}, u32[]{:S(2)}) collective-permute-start(bf16[192,512]{1,0:T(8,128)(2,1)S(1)} %join.1.refs_2_), channel_id=1, source_target_pairs={{0,4},{1,5},{2,6},{3,7},{4,0},{5,1},{6,2},{7,3},{8,12},{9,13},{10,... | collective-permute-start | bytes 589832 | tf_op jit(solution)/shard_map/ppermute | solution.py:280
  4.2 0.7 %convert_element_type.66 = f32[1536]{0:T(1024)S(1)} convert(s32[1536]{0:T(1024)} %param.8) | non-fusion elementwise | flops 1536 | bytes 12288 | tf_op jit(solution)/shard_map/convert_element_type | solution.py:291
  4.9 0.1 reshape.3.refs_1_
  5.0 2.7 %collective-permute-done.1 = bf16[192,512]{1,0:T(8,128)(2,1)S(1)} collective-permute-done((bf16[192,512]{1,0:T(8,128)(2,1)S(1)}, bf16[192,512]{1,0:T(8,128)(2,1)S(1)}, u32[]{:S(2)}, u32[]{:S(2)}) %collective-permute-start.1) | collective-permute-done | bytes 196640 | tf_op jit(solution)/shard_map/ppermute | solution.py:280
  7.7 0.5 collective-permute-done
  8.2 1.7 %collective-permute-start.2 = (bf16[192,512]{1,0:T(8,128)(2,1)S(1)}, bf16[192,512]{1,0:T(8,128)(2,1)S(1)}, u32[]{:S(2)}, u32[]{:S(2)}) collective-permute-start(bf16[192,512]{1,0:T(8,128)(2,1)S(1)} %collective-permute-done.1), channel_id=1, source_target_pairs={{0,1},{1,0},{2,3},{3,2},{4,5},{5,4},{6,7},{7,6},{8,9},{9,8},{10,11... | collective-permute-start | bytes 589832 | tf_op jit(solution)/shard_map/ppermute | solution.py:280
  9.9 0.0 collective-permute-start.3
  10.0 1.6 %collective-permute-start.6 = (bf16[192,512]{1,0:T(8,128)(2,1)S(1)}, bf16[192,512]{1,0:T(8,128)(2,1)S(1)}, u32[]{:S(2)}, u32[]{:S(2)}) collective-permute-start(bf16[192,512]{1,0:T(8,128)(2,1)S(1)} %broadcast_select_fusion.refs_4_), channel_id=1, source_target_pairs={{0,1},{1,0},{2,3},{3,2},{4,5},{5,4},{6,7},{7,6},{8,12},{9,13},{10,... | collective-permute-start | bytes 589832 | tf_op jit(solution)/shard_map/ppermute | solution.py:280
  11.5 3.0 %collective-permute-done.2 = bf16[192,512]{1,0:T(8,128)(2,1)S(1)} collective-permute-done((bf16[192,512]{1,0:T(8,128)(2,1)S(1)}, bf16[192,512]{1,0:T(8,128)(2,1)S(1)}, u32[]{:S(2)}, u32[]{:S(2)}) %collective-permute-start.2) | collective-permute-done | bytes 196640 | tf_op jit(solution)/shard_map/ppermute | solution.py:280
  14.6 1.5 %collective-permute-done.3 = bf16[192,512]{1,0:T(8,128)(2,1)S(1)} collective-permute-done((bf16[192,512]{1,0:T(8,128)(2,1)S(1)}, bf16[192,512]{1,0:T(8,128)(2,1)S(1)}, u32[]{:S(2)}, u32[]{:S(2)}) %collective-permute-start.3) | collective-permute-done | bytes 196640 | tf_op jit(solution)/shard_map/ppermute | solution.py:280
  16.1 0.0 copy-start
  16.1 1.6 %collective-permute-start.4 = (bf16[192,512]{1,0:T(8,128)(2,1)S(1)}, bf16[192,512]{1,0:T(8,128)(2,1)S(1)}, u32[]{:S(2)}, u32[]{:S(2)}) collective-permute-start(bf16[192,512]{1,0:T(8,128)(2,1)S(1)} %broadcast_select_fusion.1.refs_6_), channel_id=1, source_target_pairs={{0,1},{1,0},{2,3},{3,2},{4,5},{5,4},{6,7},{7,6},{8,9},{9,8},{10,11... | collective-permute-start | bytes 589832 | tf_op jit(solution)/shard_map/ppermute | solution.py:280
  17.6 2.9 %load.2 = (bf16[1024,1792]{1,0:T(8,128)(2,1)S(1)}, bf16[1024,1280]{1,0:T(8,128)(2,1)S(1)}) custom-call(bf16[1024,8192]{1,0:T(8,128)(2,1)} %w_hbm.3), custom_call_target="tpu_custom_call" | custom-call | bytes 6291456 | tf_op jit(solution)/shard_map/load/pallas_call | solution.py:94
  20.5 0.0 collective-permute-done.5.refs_3_
  20.5 0.0 collective-permute-done.6.refs_5_
  20.5 0.0 copy-done
  20.5 3.7 %attend_early.1 = (f32[1536,128]{1,0:T(8,128)S(1)}, f32[1536,128]{1,0:T(8,128)S(1)}, f32[1536,128]{1,0:T(8,128)S(1)}) custom-call(bf16[192,1024]{1,0:T(8,128)(2,1)S(1)} %copy-done, f32[8,192]{1,0:T(8,128)S(1)} %reshape.3.refs_1_, bf16[192,512]{1,0:T(8,128)(2,1)S(1)} %join.1.refs_2_, bf16[192,512]{1,0:T(8,128)(2,1)S(1)} %collective-permute-done.5.refs_3_, ...), custom_call_target="tpu_custom_call" | custom-call | flops 754974720 | bytes 786432 | tf_op jit(solution)/shard_map/attend_early/pallas_call | solution.py:314
  24.2 0.0 collective-permute-done.4.refs_2_
  24.3 2.4 %attend_late.1 = (bf16[192,1024]{1,0:T(8,128)(2,1)S(1)}, bf16[96,1792]{1,0:T(8,128)(2,1)S(1)}, bf16[96,1792]{1,0:T(8,128)(2,1)S(1)}) custom-call(bf16[192,1024]{1,0:T(8,128)(2,1)S(1)} %copy-done, f32[8,192]{1,0:T(8,128)S(1)} %reshape.3.refs_1_, bf16[192,512]{1,0:T(8,128)(2,1)S(1)} %collective-permute-done.4.refs_2_, ...), custom_call_target="tpu_custom_call" | custom-call | flops 855638016 | bytes 4456448 | tf_op jit(solution)/shard_map/attend_late/pallas_call | solution.py:334
  26.7 0.1 collective-permute-start.7
  26.8 4.1 %load.3 = (bf16[1024,1280]{1,0:T(8,128)(2,1)S(1)}, bf16[1024,3840]{1,0:T(8,128)(2,1)S(1)}) custom-call(bf16[1024,8192]{1,0:T(8,128)(2,1)} %w_hbm.3), custom_call_target="tpu_custom_call" | custom-call | bytes 10485760 | tf_op jit(solution)/shard_map/load/pallas_call | solution.py:94
  30.8 1.2 %project_rest.2 = (bf16[96,2560]{1,0:T(8,128)(2,1)S(1)}, bf16[96,2560]{1,0:T(8,128)(2,1)S(1)}) custom-call(bf16[192,1024]{1,0:T(8,128)(2,1)S(1)} %get-tuple-element.31.context_ref, bf16[1024,1280]{1,0:T(8,128)(2,1)S(1)} %get-tuple-element.32.refs_0_, bf16[1024,1280]{1,0:T(8,128)(2,1)S(1)} %get-tuple-element.33.refs_1_), custom_call_target="tpu_custom_call" | custom-call | flops 1006632960 | bytes 5242880 | tf_op jit(solution)/shard_map/project_rest/pallas_call | solution.py:250
  32.1 0.6 %collective-permute-start.9 = (bf16[96,2560]{1,0:T(8,128)(2,1)S(1)}, bf16[96,2560]{1,0:T(8,128)(2,1)S(1)}, u32[]{:S(2)}, u32[]{:S(2)}) collective-permute-start(bf16[96,2560]{1,0:T(8,128)(2,1)S(1)} %get-tuple-element.35), channel_id=1, source_target_pairs={{0,1},{1,0},{2,3},{3,2},{4,5},{5,4},{6,7},{7,6},{8,9},{9,8},{10,11... | collective-permute-start | bytes 1474568 | tf_op jit(solution)/shard_map/ppermute | solution.py:280
  32.6 1.7 %project_rest.3 = (bf16[96,3840]{1,0:T(8,128)(2,1)S(1)}, bf16[96,3840]{1,0:T(8,128)(2,1)S(1)}) custom-call(bf16[192,1024]{1,0:T(8,128)(2,1)S(1)} %get-tuple-element.31.context_ref, bf16[1024,3840]{1,0:T(8,128)(2,1)S(1)} %get-tuple-element.36.refs_0_), custom_call_target="tpu_custom_call" | custom-call | flops 1509949440 | bytes 7864320 | tf_op jit(solution)/shard_map/project_rest/pallas_call | solution.py:250
  34.3 0.1 collective-permute-start.11
  34.4 0.0 collective-permute-done.7
  34.5 0.6 %collective-permute-start.8 = (bf16[48,1792]{1,0:T(8,128)(2,1)S(1)}, bf16[48,1792]{1,0:T(8,128)(2,1)S(1)}, u32[]{:S(2)}, u32[]{:S(2)}) collective-permute-start(bf16[48,1792]{1,0:T(8,128)(2,1)S(1)} %add_convert_fusion.5), channel_id=1, source_target_pairs={{0,2},{1,3},{2,0},{3,1},{4,6},{5,7},{6,4},{7,5},{8,10},{9,11},{10,... | collective-permute-start | bytes 516104 | tf_op jit(solution)/shard_map/ppermute | solution.py:363
  35.1 0.0 collective-permute-done.9
  35.1 0.1 add_convert_fusion.3
  35.1 1.6 %collective-permute-start.10 = (bf16[48,2560]{1,0:T(8,128)(2,1)S(1)}, bf16[48,2560]{1,0:T(8,128)(2,1)S(1)}, u32[]{:S(2)}, u32[]{:S(2)}) collective-permute-start(bf16[48,2560]{1,0:T(8,128)(2,1)S(1)} %add_convert_fusion.3), channel_id=1, source_target_pairs={{0,2},{1,3},{2,0},{3,1},{4,6},{5,7},{6,4},{7,5},{8,10},{9,11},{10,... | collective-permute-start | bytes 737288 | tf_op jit(solution)/shard_map/ppermute | solution.py:363
  36.7 5.1 %collective-permute-done.8 = bf16[48,1792]{1,0:T(8,128)(2,1)S(1)} collective-permute-done((bf16[48,1792]{1,0:T(8,128)(2,1)S(1)}, bf16[48,1792]{1,0:T(8,128)(2,1)S(1)}, u32[]{:S(2)}, u32[]{:S(2)}) %collective-permute-start.8) | collective-permute-done | bytes 172064 | tf_op jit(solution)/shard_map/ppermute | solution.py:363
  41.8 0.1 add_convert_fusion.4
  41.9 0.0 collective-permute-done.11
  41.9 0.1 add_convert_fusion.1
  42.0 0.6 %collective-permute-start.12 = (bf16[48,3840]{1,0:T(8,128)(2,1)S(1)}, bf16[48,3840]{1,0:T(8,128)(2,1)S(1)}, u32[]{:S(2)}, u32[]{:S(2)}) collective-permute-start(bf16[48,3840]{1,0:T(8,128)(2,1)S(1)} %add_convert_fusion.1), channel_id=1, source_target_pairs={{0,2},{1,3},{2,0},{3,1},{4,6},{5,7},{6,4},{7,5},{8,10},{9,11},{10,... | collective-permute-start | bytes 1105928 | tf_op jit(solution)/shard_map/ppermute | solution.py:363
  42.5 4.5 %collective-permute-done.10 = bf16[48,2560]{1,0:T(8,128)(2,1)S(1)} collective-permute-done((bf16[48,2560]{1,0:T(8,128)(2,1)S(1)}, bf16[48,2560]{1,0:T(8,128)(2,1)S(1)}, u32[]{:S(2)}, u32[]{:S(2)}) %collective-permute-start.10) | collective-permute-done | bytes 245792 | tf_op jit(solution)/shard_map/ppermute | solution.py:363
  47.1 0.1 add_convert_fusion.2
  47.2 7.3 %collective-permute-done.12 = bf16[48,3840]{1,0:T(8,128)(2,1)S(1)} collective-permute-done((bf16[48,3840]{1,0:T(8,128)(2,1)S(1)}, bf16[48,3840]{1,0:T(8,128)(2,1)S(1)}, u32[]{:S(2)}, u32[]{:S(2)}) %collective-permute-start.12) | collective-permute-done | bytes 368672 | tf_op jit(solution)/shard_map/ppermute | solution.py:363
  54.5 0.1 add_convert_fusion
  54.6 0.9 %pad_maximum_fusion = bf16[48,8192]{1,0:T(8,128)(2,1)} fusion(bf16[48,3840]{1,0:T(8,128)(2,1)S(1)} %add_convert_fusion, bf16[48,2560]{1,0:T(8,128)(2,1)S(1)} %add_convert_fusion.2, bf16[48,1792]{1,0:T(8,128)(2,1)S(1)} %add_convert_fusion.4), kind=kLoop, calls=%fused_computation | loop fusion | flops 2359296 | bytes 1572864 | tf_op jit(solution)/shard_map/concatenate | solution.py:368
  (3 shorter events, 0.1 us)
Async XLA Ops:
  1.0 6.7 %collective-permute-start.1 = (bf16[192,512]{1,0:T(8,128)(2,1)S(1)}, bf16[192,512]{1,0:T(8,128)(2,1)S(1)}, u32[]{:S(2)}, u32[]{:S(2)}) collective-permute-start(bf16[192,512]{1,0:T(8,128)(2,1)S(1)} %join.1.refs_2_), channel_id=1, source_target_pairs={{0,1},{1,0},{2,3},{3,2},{4,5},{5,4},{6,7},{7,6},{8,16},{9,17},{10,... | collective-permute-start | bytes 589832 | tf_op jit(solution)/shard_map/ppermute | solution.py:280
  1.5 6.7 %collective-permute-start = (bf16[192,512]{1,0:T(8,128)(2,1)S(1)}, bf16[192,512]{1,0:T(8,128)(2,1)S(1)}, u32[]{:S(2)}, u32[]{:S(2)}) collective-permute-start(bf16[192,512]{1,0:T(8,128)(2,1)S(1)} %join.1.refs_2_), channel_id=1, source_target_pairs={{0,8},{1,9},{2,10},{3,11},{4,12},{5,13},{6,14},{7,15},{8,0},{9,1},... | collective-permute-start | bytes 589832 | tf_op jit(solution)/shard_map/ppermute | solution.py:280
  2.7 17.8 %collective-permute-start.5 = (bf16[192,512]{1,0:T(8,128)(2,1)S(1)}, bf16[192,512]{1,0:T(8,128)(2,1)S(1)}, u32[]{:S(2)}, u32[]{:S(2)}) collective-permute-start(bf16[192,512]{1,0:T(8,128)(2,1)S(1)} %join.1.refs_2_), channel_id=1, source_target_pairs={{0,4},{1,5},{2,6},{3,7},{4,0},{5,1},{6,2},{7,3},{8,12},{9,13},{10,... | collective-permute-start | bytes 589832 | tf_op jit(solution)/shard_map/ppermute | solution.py:280
  8.2 6.4 %collective-permute-start.2 = (bf16[192,512]{1,0:T(8,128)(2,1)S(1)}, bf16[192,512]{1,0:T(8,128)(2,1)S(1)}, u32[]{:S(2)}, u32[]{:S(2)}) collective-permute-start(bf16[192,512]{1,0:T(8,128)(2,1)S(1)} %collective-permute-done.1), channel_id=1, source_target_pairs={{0,1},{1,0},{2,3},{3,2},{4,5},{5,4},{6,7},{7,6},{8,9},{9,8},{10,11... | collective-permute-start | bytes 589832 | tf_op jit(solution)/shard_map/ppermute | solution.py:280
  9.9 6.1 %collective-permute-start.3 = (bf16[192,512]{1,0:T(8,128)(2,1)S(1)}, bf16[192,512]{1,0:T(8,128)(2,1)S(1)}, u32[]{:S(2)}, u32[]{:S(2)}) collective-permute-start(bf16[192,512]{1,0:T(8,128)(2,1)S(1)} %collective-permute-done), channel_id=1, source_target_pairs={{0,1},{1,0},{2,3},{3,2},{4,5},{5,4},{6,7},{7,6},{8,16},{9,17},{10,... | collective-permute-start | bytes 589832 | tf_op jit(solution)/shard_map/ppermute | solution.py:280
  10.0 10.6 %collective-permute-start.6 = (bf16[192,512]{1,0:T(8,128)(2,1)S(1)}, bf16[192,512]{1,0:T(8,128)(2,1)S(1)}, u32[]{:S(2)}, u32[]{:S(2)}) collective-permute-start(bf16[192,512]{1,0:T(8,128)(2,1)S(1)} %broadcast_select_fusion.refs_4_), channel_id=1, source_target_pairs={{0,1},{1,0},{2,3},{3,2},{4,5},{5,4},{6,7},{7,6},{8,12},{9,13},{10,... | collective-permute-start | bytes 589832 | tf_op jit(solution)/shard_map/ppermute | solution.py:280
  16.1 4.5 %copy-start = (bf16[192,1024]{1,0:T(8,128)(2,1)S(1)}, bf16[192,1024]{1,0:T(8,128)(2,1)}, u32[]{:S(2)}) copy-start(bf16[192,1024]{1,0:T(8,128)(2,1)} %refs_0_.3) | copy-start | bytes 1179652
  16.1 8.2 %collective-permute-start.4 = (bf16[192,512]{1,0:T(8,128)(2,1)S(1)}, bf16[192,512]{1,0:T(8,128)(2,1)S(1)}, u32[]{:S(2)}, u32[]{:S(2)}) collective-permute-start(bf16[192,512]{1,0:T(8,128)(2,1)S(1)} %broadcast_select_fusion.1.refs_6_), channel_id=1, source_target_pairs={{0,1},{1,0},{2,3},{3,2},{4,5},{5,4},{6,7},{7,6},{8,9},{9,8},{10,11... | collective-permute-start | bytes 589832 | tf_op jit(solution)/shard_map/ppermute | solution.py:280
  26.7 7.7 %collective-permute-start.7 = (bf16[96,1792]{1,0:T(8,128)(2,1)S(1)}, bf16[96,1792]{1,0:T(8,128)(2,1)S(1)}, u32[]{:S(2)}, u32[]{:S(2)}) collective-permute-start(bf16[96,1792]{1,0:T(8,128)(2,1)S(1)} %get-tuple-element.30), channel_id=1, source_target_pairs={{0,1},{1,0},{2,3},{3,2},{4,5},{5,4},{6,7},{7,6},{8,9},{9,8},{10,11... | collective-permute-start | bytes 1032200 | tf_op jit(solution)/shard_map/ppermute | solution.py:280
  32.1 3.0 %collective-permute-start.9 = (bf16[96,2560]{1,0:T(8,128)(2,1)S(1)}, bf16[96,2560]{1,0:T(8,128)(2,1)S(1)}, u32[]{:S(2)}, u32[]{:S(2)}) collective-permute-start(bf16[96,2560]{1,0:T(8,128)(2,1)S(1)} %get-tuple-element.35), channel_id=1, source_target_pairs={{0,1},{1,0},{2,3},{3,2},{4,5},{5,4},{6,7},{7,6},{8,9},{9,8},{10,11... | collective-permute-start | bytes 1474568 | tf_op jit(solution)/shard_map/ppermute | solution.py:280
  34.3 7.5 %collective-permute-start.11 = (bf16[96,3840]{1,0:T(8,128)(2,1)S(1)}, bf16[96,3840]{1,0:T(8,128)(2,1)S(1)}, u32[]{:S(2)}, u32[]{:S(2)}) collective-permute-start(bf16[96,3840]{1,0:T(8,128)(2,1)S(1)} %get-tuple-element.38), channel_id=1, source_target_pairs={{0,1},{1,0},{2,3},{3,2},{4,5},{5,4},{6,7},{7,6},{8,9},{9,8},{10,11... | collective-permute-start | bytes 2211848 | tf_op jit(solution)/shard_map/ppermute | solution.py:280
  34.5 7.3 %collective-permute-start.8 = (bf16[48,1792]{1,0:T(8,128)(2,1)S(1)}, bf16[48,1792]{1,0:T(8,128)(2,1)S(1)}, u32[]{:S(2)}, u32[]{:S(2)}) collective-permute-start(bf16[48,1792]{1,0:T(8,128)(2,1)S(1)} %add_convert_fusion.5), channel_id=1, source_target_pairs={{0,2},{1,3},{2,0},{3,1},{4,6},{5,7},{6,4},{7,5},{8,10},{9,11},{10,... | collective-permute-start | bytes 516104 | tf_op jit(solution)/shard_map/ppermute | solution.py:363
  35.1 11.9 %collective-permute-start.10 = (bf16[48,2560]{1,0:T(8,128)(2,1)S(1)}, bf16[48,2560]{1,0:T(8,128)(2,1)S(1)}, u32[]{:S(2)}, u32[]{:S(2)}) collective-permute-start(bf16[48,2560]{1,0:T(8,128)(2,1)S(1)} %add_convert_fusion.3), channel_id=1, source_target_pairs={{0,2},{1,3},{2,0},{3,1},{4,6},{5,7},{6,4},{7,5},{8,10},{9,11},{10,... | collective-permute-start | bytes 737288 | tf_op jit(solution)/shard_map/ppermute | solution.py:363
  42.0 12.5 %collective-permute-start.12 = (bf16[48,3840]{1,0:T(8,128)(2,1)S(1)}, bf16[48,3840]{1,0:T(8,128)(2,1)S(1)}, u32[]{:S(2)}, u32[]{:S(2)}) collective-permute-start(bf16[48,3840]{1,0:T(8,128)(2,1)S(1)} %add_convert_fusion.1), channel_id=1, source_target_pairs={{0,2},{1,3},{2,0},{3,1},{4,6},{5,7},{6,4},{7,5},{8,10},{9,11},{10,... | collective-permute-start | bytes 1105928 | tf_op jit(solution)/shard_map/ppermute | solution.py:363

commit v4 on v3

--- a/solution.py
+++ b/solution.py
@@ -17,7 +17,7 @@
 VMEM = pl.BlockSpec(memory_space=pltpu.VMEM)
 ANY = pl.BlockSpec(memory_space=pl.ANY)
 MIB = 1 << 20
-CUTS = (7, 17, 32)
+CUTS = (7, 17, 24, 32)
 NEAR = 12
 EARLY, LATE, PROJ = 24, 16, 8
 
@@ -293,8 +293,9 @@
     near = model * NEAR // 32
     weight = in_hbm(output_weight)
     first, *middle = load_call(weight, (0, cuts[1], near))
-    *rest, last = load_call(weight, (near, *cuts[2:]))
-    weights = [[first], middle + rest, [last]]
+    *rest, third = load_call(weight, (near, *cuts[2:4]))
+    weights = [[first], middle + rest, [third]]
+    weights.append(load_call(weight, cuts[3:]))
     even, odd = send(own, "even", 1), send(own, "odd", 1)
     blocks = [own, send(own, "col", 0)]
     even, odd, docs = lax.optimization_barrier((even, odd, docs))

time: 55.7 us -> 56.1 us (level)
  the two profiles are of different devices: /device:TPU:20 before, /device:TPU:12 now
where the time goes in v4:
time: 56.1 us; the launch traced here: 55.9 us
  waiting for transfers between devices  21.3 us (38%)
  Pallas kernels  18.1 us (32%)
  starting transfers between devices  14 us (25%)
  other arithmetic  2.19 us (4%)
    ppermute x4, waiting for transfers between devices, layer(): lax.ppermute(moved[at:at + part], AXES, y_route(seq, tp, distance))  15.3 us
    ppermute x11, starting transfers between devices, send(): return lax.ppermute(x, AXES, route[name, step])  9.64 us
    pallas_call x3, Pallas kernels, load_call(): pl.pallas_call(functools.partial(load_kernel, cuts[0]), out_shape=[pltpu....  7.97 us
    ppermute x11, waiting for transfers between devices, send(): return lax.ppermute(x, AXES, route[name, step])  6.08 us
    ppermute x4, starting transfers between devices, layer(): lax.ppermute(moved[at:at + part], AXES, y_route(seq, tp, distance))  4.31 us
    pallas_call x1, Pallas kernels, layer(): pl.pallas_call(functools.partial(early_kernel, kv_local, group, count, 32...  3.7 us
    pallas_call x3, Pallas kernels, project_call(): pl.pallas_call(functools.partial(project_kernel, part), out_shape=(out, o...  3.17 us
    pallas_call x1, Pallas kernels, layer(): pl.pallas_call(functools.partial(late_kernel, kv_local, group, part, dept...  2.34 us
  transfers between devices with their start and end apart: 15, of which 7 were waited for; matrix products, arithmetic and copies ran while one was open for 2% of the time, Pallas kernels for 27%

profile of v4, /device:TPU:12, one launch (start us, length us, event | category | flops | bytes accessed | tf_op | source)
XLA Modules:
  0.0 55.9 jit_solution(16934948442116973763)
XLA Ops:
  0.0 1.0 %join.1.refs_2_ = bf16[192,512]{1,0:T(8,128)(2,1)S(1)} custom-call(bf16[192,256]{1,0:T(8,128)(2,1)} %k_ref.1, bf16[192,256]{1,0:T(8,128)(2,1)} %v_ref.1), custom_call_target="tpu_custom_call" | custom-call | tf_op jit(solution)/shard_map/join/pallas_call | solution.py:282
  1.0 0.5 collective-permute-start
  1.5 2.7 %collective-permute-start.1 = (bf16[192,512]{1,0:T(8,128)(2,1)S(1)}, bf16[192,512]{1,0:T(8,128)(2,1)S(1)}, u32[]{:S(2)}, u32[]{:S(2)}) collective-permute-start(bf16[192,512]{1,0:T(8,128)(2,1)S(1)} %join.1.refs_2_), channel_id=1, source_target_pairs={{0,1},{1,0},{2,3},{3,2},{4,5},{5,4},{6,7},{7,6},{8,16},{9,17},{10,... | collective-permute-start | bytes 589832 | tf_op jit(solution)/shard_map/ppermute | solution.py:280
  4.2 1.5 %collective-permute-start.5 = (bf16[192,512]{1,0:T(8,128)(2,1)S(1)}, bf16[192,512]{1,0:T(8,128)(2,1)S(1)}, u32[]{:S(2)}, u32[]{:S(2)}) collective-permute-start(bf16[192,512]{1,0:T(8,128)(2,1)S(1)} %join.1.refs_2_), channel_id=1, source_target_pairs={{0,4},{1,5},{2,6},{3,7},{4,0},{5,1},{6,2},{7,3},{8,12},{9,13},{10,... | collective-permute-start | bytes 589832 | tf_op jit(solution)/shard_map/ppermute | solution.py:280
  5.7 0.7 %convert_element_type.87 = f32[1536]{0:T(1024)S(1)} convert(s32[1536]{0:T(1024)} %param.8) | non-fusion elementwise | flops 1536 | bytes 12288 | tf_op jit(solution)/shard_map/convert_element_type | solution.py:291
  6.4 0.1 reshape.3.refs_1_
  6.4 1.2 %collective-permute-done = bf16[192,512]{1,0:T(8,128)(2,1)S(1)} collective-permute-done((bf16[192,512]{1,0:T(8,128)(2,1)S(1)}, bf16[192,512]{1,0:T(8,128)(2,1)S(1)}, u32[]{:S(2)}, u32[]{:S(2)}) %collective-permute-start) | collective-permute-done | bytes 196640 | tf_op jit(solution)/shard_map/ppermute | solution.py:280
  7.7 1.1 %collective-permute-done.1 = bf16[192,512]{1,0:T(8,128)(2,1)S(1)} collective-permute-done((bf16[192,512]{1,0:T(8,128)(2,1)S(1)}, bf16[192,512]{1,0:T(8,128)(2,1)S(1)}, u32[]{:S(2)}, u32[]{:S(2)}) %collective-permute-start.1) | collective-permute-done | bytes 196640 | tf_op jit(solution)/shard_map/ppermute | solution.py:280
  8.8 0.0 collective-permute-start.2
  8.8 2.0 %collective-permute-start.3 = (bf16[192,512]{1,0:T(8,128)(2,1)S(1)}, bf16[192,512]{1,0:T(8,128)(2,1)S(1)}, u32[]{:S(2)}, u32[]{:S(2)}) collective-permute-start(bf16[192,512]{1,0:T(8,128)(2,1)S(1)} %collective-permute-done), channel_id=1, source_target_pairs={{0,1},{1,0},{2,3},{3,2},{4,5},{5,4},{6,7},{7,6},{8,16},{9,17},{10,... | collective-permute-start | bytes 589832 | tf_op jit(solution)/shard_map/ppermute | solution.py:280
  10.9 1.6 %collective-permute-start.6 = (bf16[192,512]{1,0:T(8,128)(2,1)S(1)}, bf16[192,512]{1,0:T(8,128)(2,1)S(1)}, u32[]{:S(2)}, u32[]{:S(2)}) collective-permute-start(bf16[192,512]{1,0:T(8,128)(2,1)S(1)} %broadcast_select_fusion.refs_4_), channel_id=1, source_target_pairs={{0,1},{1,0},{2,3},{3,2},{4,5},{5,4},{6,7},{7,6},{8,12},{9,13},{10,... | collective-permute-start | bytes 589832 | tf_op jit(solution)/shard_map/ppermute | solution.py:280
  12.4 0.0 collective-permute-done.2
  12.4 3.7 %collective-permute-done.3 = bf16[192,512]{1,0:T(8,128)(2,1)S(1)} collective-permute-done((bf16[192,512]{1,0:T(8,128)(2,1)S(1)}, bf16[192,512]{1,0:T(8,128)(2,1)S(1)}, u32[]{:S(2)}, u32[]{:S(2)}) %collective-permute-start.3) | collective-permute-done | bytes 196640 | tf_op jit(solution)/shard_map/ppermute | solution.py:280
  16.1 0.0 copy-start
  16.2 0.1 collective-permute-start.4
  16.2 2.9 %load.3 = (bf16[1024,1792]{1,0:T(8,128)(2,1)S(1)}, bf16[1024,1280]{1,0:T(8,128)(2,1)S(1)}) custom-call(bf16[1024,8192]{1,0:T(8,128)(2,1)} %w_hbm.5), custom_call_target="tpu_custom_call" | custom-call | bytes 6291456 | tf_op jit(solution)/shard_map/load/pallas_call | solution.py:94
  19.2 0.0 collective-permute-done.5.refs_3_
  19.2 0.0 collective-permute-done.6.refs_5_
  19.2 3.7 %attend_early.1 = (f32[1536,128]{1,0:T(8,128)S(1)}, f32[1536,128]{1,0:T(8,128)S(1)}, f32[1536,128]{1,0:T(8,128)S(1)}) custom-call(bf16[192,1024]{1,0:T(8,128)(2,1)S(1)} %copy-done, f32[8,192]{1,0:T(8,128)S(1)} %reshape.3.refs_1_, bf16[192,512]{1,0:T(8,128)(2,1)S(1)} %join.1.refs_2_, bf16[192,512]{1,0:T(8,128)(2,1)S(1)} %collective-permute-done.5.refs_3_, ...), custom_call_target="tpu_custom_call" | custom-call | flops 754974720 | bytes 786432 | tf_op jit(solution)/shard_map/attend_early/pallas_call | solution.py:315
  22.9 0.0 collective-permute-done.4.refs_2_
  22.9 2.3 %attend_late.1 = (bf16[192,1024]{1,0:T(8,128)(2,1)S(1)}, bf16[96,1792]{1,0:T(8,128)(2,1)S(1)}, bf16[96,1792]{1,0:T(8,128)(2,1)S(1)}) custom-call(bf16[192,1024]{1,0:T(8,128)(2,1)S(1)} %copy-done, f32[8,192]{1,0:T(8,128)S(1)} %reshape.3.refs_1_, bf16[192,512]{1,0:T(8,128)(2,1)S(1)} %collective-permute-done.4.refs_2_, ...), custom_call_target="tpu_custom_call" | custom-call | flops 855638016 | bytes 4456448 | tf_op jit(solution)/shard_map/attend_late/pallas_call | solution.py:335
  25.3 0.5 collective-permute-start.7
  25.8 2.9 %load.4 = (bf16[1024,1280]{1,0:T(8,128)(2,1)S(1)}, bf16[1024,1792]{1,0:T(8,128)(2,1)S(1)}) custom-call(bf16[1024,8192]{1,0:T(8,128)(2,1)} %w_hbm.5), custom_call_target="tpu_custom_call" | custom-call | bytes 6291456 | tf_op jit(solution)/shard_map/load/pallas_call | solution.py:94
  28.7 2.2 %load.5.refs_0_ = bf16[1024,2048]{1,0:T(8,128)(2,1)S(1)} custom-call(bf16[1024,8192]{1,0:T(8,128)(2,1)} %w_hbm.5), custom_call_target="tpu_custom_call" | custom-call | bytes 4194304 | tf_op jit(solution)/shard_map/load/pallas_call | solution.py:94
  30.9 1.2 %project_rest.3 = (bf16[96,2560]{1,0:T(8,128)(2,1)S(1)}, bf16[96,2560]{1,0:T(8,128)(2,1)S(1)}) custom-call(bf16[192,1024]{1,0:T(8,128)(2,1)S(1)} %get-tuple-element.33.context_ref, bf16[1024,1280]{1,0:T(8,128)(2,1)S(1)} %get-tuple-element.34.refs_0_, bf16[1024,1280]{1,0:T(8,128)(2,1)S(1)} %get-tuple-element.35.refs_1_), custom_call_target="tpu_custom_call" | custom-call | flops 1006632960 | bytes 5242880 | tf_op jit(solution)/shard_map/project_rest/pallas_call | solution.py:250
  32.1 0.1 collective-permute-start.9
  32.2 0.9 %project_rest.4 = (bf16[96,1792]{1,0:T(8,128)(2,1)S(1)}, bf16[96,1792]{1,0:T(8,128)(2,1)S(1)}) custom-call(bf16[192,1024]{1,0:T(8,128)(2,1)S(1)} %get-tuple-element.33.context_ref, bf16[1024,1792]{1,0:T(8,128)(2,1)S(1)} %get-tuple-element.38.refs_0_), custom_call_target="tpu_custom_call" | custom-call | flops 704643072 | bytes 3670016 | tf_op jit(solution)/shard_map/project_rest/pallas_call | solution.py:250
  33.1 0.5 collective-permute-start.11
  33.7 1.0 %project_rest.5 = (bf16[96,2048]{1,0:T(8,128)(2,1)S(1)}, bf16[96,2048]{1,0:T(8,128)(2,1)S(1)}) custom-call(bf16[192,1024]{1,0:T(8,128)(2,1)S(1)} %get-tuple-element.33.context_ref, bf16[1024,2048]{1,0:T(8,128)(2,1)S(1)} %load.5.refs_0_), custom_call_target="tpu_custom_call" | custom-call | flops 805306368 | bytes 4194304 | tf_op jit(solution)/shard_map/project_rest/pallas_call | solution.py:250
  34.7 0.1 collective-permute-start.13
  34.8 0.0 collective-permute-done.7
  34.8 0.6 %collective-permute-start.8 = (bf16[48,1792]{1,0:T(8,128)(2,1)S(1)}, bf16[48,1792]{1,0:T(8,128)(2,1)S(1)}, u32[]{:S(2)}, u32[]{:S(2)}) collective-permute-start(bf16[48,1792]{1,0:T(8,128)(2,1)S(1)} %add_convert_fusion.7), channel_id=1, source_target_pairs={{0,2},{1,3},{2,0},{3,1},{4,6},{5,7},{6,4},{7,5},{8,10},{9,11},{10,... | collective-permute-start | bytes 516104 | tf_op jit(solution)/shard_map/ppermute | solution.py:364
  35.4 0.0 collective-permute-done.11
  35.5 1.6 %collective-permute-start.12 = (bf16[48,1792]{1,0:T(8,128)(2,1)S(1)}, bf16[48,1792]{1,0:T(8,128)(2,1)S(1)}, u32[]{:S(2)}, u32[]{:S(2)}) collective-permute-start(bf16[48,1792]{1,0:T(8,128)(2,1)S(1)} %add_convert_fusion.5), channel_id=1, source_target_pairs={{0,2},{1,3},{2,0},{3,1},{4,6},{5,7},{6,4},{7,5},{8,10},{9,11},{10,... | collective-permute-start | bytes 516104 | tf_op jit(solution)/shard_map/ppermute | solution.py:364
  37.1 0.0 collective-permute-done.13
  37.1 0.6 %collective-permute-start.14 = (bf16[48,2048]{1,0:T(8,128)(2,1)S(1)}, bf16[48,2048]{1,0:T(8,128)(2,1)S(1)}, u32[]{:S(2)}, u32[]{:S(2)}) collective-permute-start(bf16[48,2048]{1,0:T(8,128)(2,1)S(1)} %add_convert_fusion.3), channel_id=1, source_target_pairs={{0,2},{1,3},{2,0},{3,1},{4,6},{5,7},{6,4},{7,5},{8,10},{9,11},{10,... | collective-permute-start | bytes 589832 | tf_op jit(solution)/shard_map/ppermute | solution.py:364
  37.7 0.0 collective-permute-done.9
  37.7 0.1 add_convert_fusion.1
  37.8 1.6 %collective-permute-start.10 = (bf16[48,2560]{1,0:T(8,128)(2,1)S(1)}, bf16[48,2560]{1,0:T(8,128)(2,1)S(1)}, u32[]{:S(2)}, u32[]{:S(2)}) collective-permute-start(bf16[48,2560]{1,0:T(8,128)(2,1)S(1)} %add_convert_fusion.1), channel_id=1, source_target_pairs={{0,2},{1,3},{2,0},{3,1},{4,6},{5,7},{6,4},{7,5},{8,10},{9,11},{10,... | collective-permute-start | bytes 737288 | tf_op jit(solution)/shard_map/ppermute | solution.py:364
  39.3 2.8 %collective-permute-done.8 = bf16[48,1792]{1,0:T(8,128)(2,1)S(1)} collective-permute-done((bf16[48,1792]{1,0:T(8,128)(2,1)S(1)}, bf16[48,1792]{1,0:T(8,128)(2,1)S(1)}, u32[]{:S(2)}, u32[]{:S(2)}) %collective-permute-start.8) | collective-permute-done | bytes 172064 | tf_op jit(solution)/shard_map/ppermute | solution.py:364
  42.2 0.1 add_convert_fusion.6
  42.2 3.6 %collective-permute-done.12 = bf16[48,1792]{1,0:T(8,128)(2,1)S(1)} collective-permute-done((bf16[48,1792]{1,0:T(8,128)(2,1)S(1)}, bf16[48,1792]{1,0:T(8,128)(2,1)S(1)}, u32[]{:S(2)}, u32[]{:S(2)}) %collective-permute-start.12) | collective-permute-done | bytes 172064 | tf_op jit(solution)/shard_map/ppermute | solution.py:364
  45.8 0.1 add_convert_fusion.4
  45.9 4.1 %collective-permute-done.14 = bf16[48,2048]{1,0:T(8,128)(2,1)S(1)} collective-permute-done((bf16[48,2048]{1,0:T(8,128)(2,1)S(1)}, bf16[48,2048]{1,0:T(8,128)(2,1)S(1)}, u32[]{:S(2)}, u32[]{:S(2)}) %collective-permute-start.14) | collective-permute-done | bytes 196640 | tf_op jit(solution)/shard_map/ppermute | solution.py:364
  50.1 0.1 add_convert_fusion.2
  50.1 4.7 %collective-permute-done.10 = bf16[48,2560]{1,0:T(8,128)(2,1)S(1)} collective-permute-done((bf16[48,2560]{1,0:T(8,128)(2,1)S(1)}, bf16[48,2560]{1,0:T(8,128)(2,1)S(1)}, u32[]{:S(2)}, u32[]{:S(2)}) %collective-permute-start.10) | collective-permute-done | bytes 245792 | tf_op jit(solution)/shard_map/ppermute | solution.py:364
  54.8 0.1 add_convert_fusion
  54.9 0.9 %pad_maximum_fusion = bf16[48,8192]{1,0:T(8,128)(2,1)} fusion(bf16[48,2048]{1,0:T(8,128)(2,1)S(1)} %add_convert_fusion.2, bf16[48,1792]{1,0:T(8,128)(2,1)S(1)} %add_convert_fusion.4, bf16[48,2560]{1,0:T(8,128)(2,1)S(1)} %add_convert_fusion, bf16[48,1792]{1,0:T(8,128)(2,1)S(1)} %add_convert_fusion.6), kind=kLoop, calls=%fused_computation | loop fusion | flops 3145728 | bytes 1572864 | tf_op jit(solution)/shard_map/concatenate | solution.py:369
  (6 shorter events, 0.2 us)
Async XLA Ops:
  1.0 6.7 %collective-permute-start = (bf16[192,512]{1,0:T(8,128)(2,1)S(1)}, bf16[192,512]{1,0:T(8,128)(2,1)S(1)}, u32[]{:S(2)}, u32[]{:S(2)}) collective-permute-start(bf16[192,512]{1,0:T(8,128)(2,1)S(1)} %join.1.refs_2_), channel_id=1, source_target_pairs={{0,8},{1,9},{2,10},{3,11},{4,12},{5,13},{6,14},{7,15},{8,0},{9,1},... | collective-permute-start | bytes 589832 | tf_op jit(solution)/shard_map/ppermute | solution.py:280
  1.5 7.3 %collective-permute-start.1 = (bf16[192,512]{1,0:T(8,128)(2,1)S(1)}, bf16[192,512]{1,0:T(8,128)(2,1)S(1)}, u32[]{:S(2)}, u32[]{:S(2)}) collective-permute-start(bf16[192,512]{1,0:T(8,128)(2,1)S(1)} %join.1.refs_2_), channel_id=1, source_target_pairs={{0,1},{1,0},{2,3},{3,2},{4,5},{5,4},{6,7},{7,6},{8,16},{9,17},{10,... | collective-permute-start | bytes 589832 | tf_op jit(solution)/shard_map/ppermute | solution.py:280
  4.2 15.0 %collective-permute-start.5 = (bf16[192,512]{1,0:T(8,128)(2,1)S(1)}, bf16[192,512]{1,0:T(8,128)(2,1)S(1)}, u32[]{:S(2)}, u32[]{:S(2)}) collective-permute-start(bf16[192,512]{1,0:T(8,128)(2,1)S(1)} %join.1.refs_2_), channel_id=1, source_target_pairs={{0,4},{1,5},{2,6},{3,7},{4,0},{5,1},{6,2},{7,3},{8,12},{9,13},{10,... | collective-permute-start | bytes 589832 | tf_op jit(solution)/shard_map/ppermute | solution.py:280
  8.8 3.6 %collective-permute-start.2 = (bf16[192,512]{1,0:T(8,128)(2,1)S(1)}, bf16[192,512]{1,0:T(8,128)(2,1)S(1)}, u32[]{:S(2)}, u32[]{:S(2)}) collective-permute-start(bf16[192,512]{1,0:T(8,128)(2,1)S(1)} %collective-permute-done.1), channel_id=1, source_target_pairs={{0,1},{1,0},{2,3},{3,2},{4,5},{5,4},{6,7},{7,6},{8,9},{9,8},{10,11... | collective-permute-start | bytes 589832 | tf_op jit(solution)/shard_map/ppermute | solution.py:280
  8.8 7.3 %collective-permute-start.3 = (bf16[192,512]{1,0:T(8,128)(2,1)S(1)}, bf16[192,512]{1,0:T(8,128)(2,1)S(1)}, u32[]{:S(2)}, u32[]{:S(2)}) collective-permute-start(bf16[192,512]{1,0:T(8,128)(2,1)S(1)} %collective-permute-done), channel_id=1, source_target_pairs={{0,1},{1,0},{2,3},{3,2},{4,5},{5,4},{6,7},{7,6},{8,16},{9,17},{10,... | collective-permute-start | bytes 589832 | tf_op jit(solution)/shard_map/ppermute | solution.py:280
  10.9 8.3 %collective-permute-start.6 = (bf16[192,512]{1,0:T(8,128)(2,1)S(1)}, bf16[192,512]{1,0:T(8,128)(2,1)S(1)}, u32[]{:S(2)}, u32[]{:S(2)}) collective-permute-start(bf16[192,512]{1,0:T(8,128)(2,1)S(1)} %broadcast_select_fusion.refs_4_), channel_id=1, source_target_pairs={{0,1},{1,0},{2,3},{3,2},{4,5},{5,4},{6,7},{7,6},{8,12},{9,13},{10,... | collective-permute-start | bytes 589832 | tf_op jit(solution)/shard_map/ppermute | solution.py:280
  16.1 3.0 %copy-start = (bf16[192,1024]{1,0:T(8,128)(2,1)S(1)}, bf16[192,1024]{1,0:T(8,128)(2,1)}, u32[]{:S(2)}) copy-start(bf16[192,1024]{1,0:T(8,128)(2,1)} %refs_0_.3) | copy-start | bytes 1179652
  16.2 6.7 %collective-permute-start.4 = (bf16[192,512]{1,0:T(8,128)(2,1)S(1)}, bf16[192,512]{1,0:T(8,128)(2,1)S(1)}, u32[]{:S(2)}, u32[]{:S(2)}) collective-permute-start(bf16[192,512]{1,0:T(8,128)(2,1)S(1)} %broadcast_select_fusion.1.refs_6_), channel_id=1, source_target_pairs={{0,1},{1,0},{2,3},{3,2},{4,5},{5,4},{6,7},{7,6},{8,9},{9,8},{10,11... | collective-permute-start | bytes 589832 | tf_op jit(solution)/shard_map/ppermute | solution.py:280
  25.3 9.5 %collective-permute-start.7 = (bf16[96,1792]{1,0:T(8,128)(2,1)S(1)}, bf16[96,1792]{1,0:T(8,128)(2,1)S(1)}, u32[]{:S(2)}, u32[]{:S(2)}) collective-permute-start(bf16[96,1792]{1,0:T(8,128)(2,1)S(1)} %get-tuple-element.32), channel_id=1, source_target_pairs={{0,1},{1,0},{2,3},{3,2},{4,5},{5,4},{6,7},{7,6},{8,9},{9,8},{10,11... | collective-permute-start | bytes 1032200 | tf_op jit(solution)/shard_map/ppermute | solution.py:280
  32.1 5.6 %collective-permute-start.9 = (bf16[96,2560]{1,0:T(8,128)(2,1)S(1)}, bf16[96,2560]{1,0:T(8,128)(2,1)S(1)}, u32[]{:S(2)}, u32[]{:S(2)}) collective-permute-start(bf16[96,2560]{1,0:T(8,128)(2,1)S(1)} %get-tuple-element.37), channel_id=1, source_target_pairs={{0,1},{1,0},{2,3},{3,2},{4,5},{5,4},{6,7},{7,6},{8,9},{9,8},{10,11... | collective-permute-start | bytes 1474568 | tf_op jit(solution)/shard_map/ppermute | solution.py:280
  33.1 2.3 %collective-permute-start.11 = (bf16[96,1792]{1,0:T(8,128)(2,1)S(1)}, bf16[96,1792]{1,0:T(8,128)(2,1)S(1)}, u32[]{:S(2)}, u32[]{:S(2)}) collective-permute-start(bf16[96,1792]{1,0:T(8,128)(2,1)S(1)} %get-tuple-element.40), channel_id=1, source_target_pairs={{0,1},{1,0},{2,3},{3,2},{4,5},{5,4},{6,7},{7,6},{8,9},{9,8},{10,11... | collective-permute-start | bytes 1032200 | tf_op jit(solution)/shard_map/ppermute | solution.py:280
  34.7 2.4 %collective-permute-start.13 = (bf16[96,2048]{1,0:T(8,128)(2,1)S(1)}, bf16[96,2048]{1,0:T(8,128)(2,1)S(1)}, u32[]{:S(2)}, u32[]{:S(2)}) collective-permute-start(bf16[96,2048]{1,0:T(8,128)(2,1)S(1)} %get-tuple-element.42), channel_id=1, source_target_pairs={{0,1},{1,0},{2,3},{3,2},{4,5},{5,4},{6,7},{7,6},{8,9},{9,8},{10,11... | collective-permute-start | bytes 1179656 | tf_op jit(solution)/shard_map/ppermute | solution.py:280
  34.8 7.3 %collective-permute-start.8 = (bf16[48,1792]{1,0:T(8,128)(2,1)S(1)}, bf16[48,1792]{1,0:T(8,128)(2,1)S(1)}, u32[]{:S(2)}, u32[]{:S(2)}) collective-permute-start(bf16[48,1792]{1,0:T(8,128)(2,1)S(1)} %add_convert_fusion.7), channel_id=1, source_target_pairs={{0,2},{1,3},{2,0},{3,1},{4,6},{5,7},{6,4},{7,5},{8,10},{9,11},{10,... | collective-permute-start | bytes 516104 | tf_op jit(solution)/shard_map/ppermute | solution.py:364
  35.5 10.4 %collective-permute-start.12 = (bf16[48,1792]{1,0:T(8,128)(2,1)S(1)}, bf16[48,1792]{1,0:T(8,128)(2,1)S(1)}, u32[]{:S(2)}, u32[]{:S(2)}) collective-permute-start(bf16[48,1792]{1,0:T(8,128)(2,1)S(1)} %add_convert_fusion.5), channel_id=1, source_target_pairs={{0,2},{1,3},{2,0},{3,1},{4,6},{5,7},{6,4},{7,5},{8,10},{9,11},{10,... | collective-permute-start | bytes 516104 | tf_op jit(solution)/shard_map/ppermute | solution.py:364
  37.1 12.9 %collective-permute-start.14 = (bf16[48,2048]{1,0:T(8,128)(2,1)S(1)}, bf16[48,2048]{1,0:T(8,128)(2,1)S(1)}, u32[]{:S(2)}, u32[]{:S(2)}) collective-permute-start(bf16[48,2048]{1,0:T(8,128)(2,1)S(1)} %add_convert_fusion.3), channel_id=1, source_target_pairs={{0,2},{1,3},{2,0},{3,1},{4,6},{5,7},{6,4},{7,5},{8,10},{9,11},{10,... | collective-permute-start | bytes 589832 | tf_op jit(solution)/shard_map/ppermute | solution.py:364
  37.8 17.1 %collective-permute-start.10 = (bf16[48,2560]{1,0:T(8,128)(2,1)S(1)}, bf16[48,2560]{1,0:T(8,128)(2,1)S(1)}, u32[]{:S(2)}, u32[]{:S(2)}) collective-permute-start(bf16[48,2560]{1,0:T(8,128)(2,1)S(1)} %add_convert_fusion.1), channel_id=1, source_target_pairs={{0,2},{1,3},{2,0},{3,1},{4,6},{5,7},{6,4},{7,5},{8,10},{9,11},{10,... | collective-permute-start | bytes 737288 | tf_op jit(solution)/shard_map/ppermute | solution.py:364

commit v5 on v4

--- a/solution.py
+++ b/solution.py
@@ -46,7 +46,7 @@
     def by_col(step):
         return flat(lambda s, t: (s ^ 1, t) if s // 2 >= step else (s, t ^ 1))
 
-    table = {("core", i): flat(lambda s, t: (s, t ^ 1)) for i in range(len(CUTS))}
+    table = {("core", i): flat(lambda s, t: (s, t ^ 1)) for i in range(len(CUTS) + 1)}
     for step in range(depth + 1):
         table["col", step] = by_col(step)
         table["even", step] = by_row(0, step)
@@ -179,16 +179,17 @@
         )
 
 
-def project(context_ref, w_ref, send_ref, keep_ref, part):
+def project(context_ref, first, w_ref, send_ref, keep_ref, part):
     step = 256
+    count = keep_ref.shape[0] // part
     for c in range(0, w_ref.shape[1], step):
         at = pl.ds(c, step)
         rows = jnp.dot(
-            context_ref[...],
+            context_ref[pl.ds(first, 2 * count * part), :],
             w_ref[:, at],
             preferred_element_type=jnp.float32,
         ).astype(jnp.bfloat16)
-        for i in range(rows.shape[0] // (2 * part)):
+        for i in range(count):
             into = pl.ds(i * part, part)
             keep_ref[into, at] = rows[2 * i * part : (2 * i + 1) * part]
             send_ref[into, at] = rows[(2 * i + 1) * part : (2 * i + 2) * part]
@@ -231,35 +232,81 @@
             first = pl.multiple_of((base + core) * part, 8)
             out_ref[pl.ds(at, part), :] = context_ref[pl.ds(first, part), :]
             at += part
-    project(out_ref, w_ref, send_ref, keep_ref, part)
-
-
-def project_kernel(part, context_ref, *refs):
+    project(out_ref, 0, w_ref, send_ref, keep_ref, part)
+
+
+def project_kernel(part, first, context_ref, *refs):
     *weights, send_ref, keep_ref = refs
     start = 0
     for w_ref in weights:
         cols = pl.ds(start, w_ref.shape[1])
-        project(context_ref, w_ref, send_ref.at[:, cols], keep_ref.at[:, cols], part)
+        send, keep = send_ref.at[:, cols], keep_ref.at[:, cols]
+        project(context_ref, first, w_ref, send, keep, part)
         start += w_ref.shape[1]
 
 
-def project_call(context, weights, part):
-    tokens, depth = context.shape
+def project_call(context, weights, part, first, rows):
+    depth = context.shape[1]
     width = sum(weight.shape[1] for weight in weights)
-    out = jax.ShapeDtypeStruct((tokens // 2, width), jnp.bfloat16)
+    out = jax.ShapeDtypeStruct((rows // 2, width), jnp.bfloat16)
     return pl.pallas_call(
-        functools.partial(project_kernel, part),
+        functools.partial(project_kernel, part, first),
         out_shape=(out, out),
         in_specs=[VMEM] * (1 + len(weights)),
         out_specs=(VMEM, VMEM),
         cost_estimate=pl.CostEstimate(
-            flops=2 * tokens * depth * width,
+            flops=2 * rows * depth * width,
             transcendentals=0,
             bytes_accessed=2 * depth * width,
         ),
         compiler_params=pltpu.CompilerParams(vmem_limit_bytes=PROJ * MIB),
         name="project_rest",
     )(context, *weights)
+
+
+def finish_kernel(starts, kept_ref, received_ref, *refs):
+    n = len(starts)
+    *arrived, out_hbm = refs[: -n - 1]
+    chunks, sems = refs[-n - 1 : -1], refs[-1]
+    each = len(arrived) // n
+    copies = []
+    for i, start in enumerate(starts):
+        cols = pl.ds(start, chunks[i].shape[1])
+        total = kept_ref[:, cols].astype(jnp.float32)
+        total = total + received_ref[:, cols].astype(jnp.float32)
+        for ref in arrived[i * each : (i + 1) * each]:
+            total = total + ref[...].astype(jnp.float32)
+        chunks[i][...] = total.astype(jnp.bfloat16)
+        copies.append(pltpu.make_async_copy(chunks[i], out_hbm.at[:, cols], sems.at[i]))
+        copies[-1].start()
+    for copy in copies:
+        copy.wait()
+
+
+def finish_call(kept, received, arrived, starts, out=None):
+    flat = [block for blocks in arrived for block in blocks]
+    n = len(starts)
+    kernel = functools.partial(finish_kernel, starts)
+    if out is not None:
+
+        def kernel(kept_ref, received_ref, *refs):
+            blocks, rest = refs[: len(flat)], refs[len(flat) + 1 :]
+            finish_kernel(starts, kept_ref, received_ref, *blocks, *rest)
+
+    return pl.pallas_call(
+        kernel,
+        out_shape=jax.ShapeDtypeStruct(kept.shape, kept.dtype),
+        in_specs=[VMEM] * (2 + len(flat)) + [ANY] * (out is not None),
+        out_specs=ANY,
+        scratch_shapes=[pltpu.VMEM(blocks[0].shape, kept.dtype) for blocks in arrived]
+        + [pltpu.SemaphoreType.DMA((n,))],
+        input_output_aliases={} if out is None else {2 + len(flat): 0},
+        cost_estimate=pl.CostEstimate(
+            flops=4 * kept.size, transcendentals=0, bytes_accessed=4 * kept.size
+        ),
+        compiler_params=pltpu.CompilerParams(vmem_limit_bytes=4 * MIB),
+        name="finish",
+    )(kept, received, *flat, *([] if out is None else [out]))
 
 
 def layer(query_rows, key_rows, value_rows, document_ids, output_weight):
@@ -331,7 +378,8 @@
         name="attend_early",
     )(query_rows, docs, *blocks)
 
-    out = jax.ShapeDtypeStruct((tokens // 2, cuts[1]), jnp.bfloat16)
+    remote = (chips - 1) * part
+    out = jax.ShapeDtypeStruct((remote, cuts[1]), jnp.bfloat16)
     context, sent, kept = pl.pallas_call(
         functools.partial(late_kernel, kv_local, group, part, depth),
         out_shape=(jax.ShapeDtypeStruct((tokens, width), jnp.bfloat16), out, out),
@@ -347,26 +395,25 @@
         name="attend_late",
     )(query_rows, docs, last_block, acc, top, total, first)
 
-    pieces = []
-    remote = (chips - 1) * part
+    arrived = []
     for i, weight in enumerate(weights):
         if i:
-            sent, kept = project_call(context, weight, part)
+            sent, kept = project_call(context, weight, part, 0, 2 * remote)
         received = send(sent, "core", i)
-        moved = (
-            kept[:remote].astype(jnp.float32) + received[:remote].astype(jnp.float32)
-        ).astype(jnp.bfloat16)
-        piece = kept[remote:].astype(jnp.float32) + received[remote:].astype(
-            jnp.float32
-        )
+        moved = kept.astype(jnp.float32) + received.astype(jnp.float32)
+        moved = moved.astype(jnp.bfloat16)
+        arrived.append([])
         for distance in range(1, chips):
             at = (distance - 1) * part
-            arrived = lax.ppermute(
+            block = lax.ppermute(
                 moved[at : at + part], AXES, y_route(seq, tp, distance)
             )
-            piece = piece + arrived.astype(jnp.float32)
-        pieces.append(piece.astype(jnp.bfloat16))
-    return jnp.concatenate(pieces, axis=1)
+            arrived[-1].append(block)
+    every = [weight for weights_of in weights for weight in weights_of]
+    sent, kept = project_call(context, every, part, 2 * remote, 2 * part)
+    received = send(sent, "core", len(CUTS))
+    out = finish_call(kept, received, arrived[:-1], cuts[:-2])
+    return finish_call(kept, received, arrived[-1:], cuts[-2:-1], out)
 
 
 def solution(mesh):

time: 56.1 us -> 59.1 us (1.053)
  the two profiles are of different devices: /device:TPU:12 before, /device:TPU:20 now
where the time goes in v5:
time: 59.1 us; the launch traced here: 58.9 us
  waiting for transfers between devices  23.7 us (40%)
  Pallas kernels  21.8 us (37%)
  starting transfers between devices  12.2 us (21%)
  other arithmetic  0.94 us (2%)
    ppermute x4, waiting for transfers between devices, layer(): block = lax.ppermute(moved[at:at + part], AXES, y_route(seq, tp, distance))  15.5 us
    ppermute x12, waiting for transfers between devices, send(): return lax.ppermute(x, AXES, route[name, step])  8.2 us
    pallas_call x3, Pallas kernels, load_call(): pl.pallas_call(functools.partial(load_kernel, cuts[0]), out_shape=[pltpu....  7.99 us
    ppermute x12, starting transfers between devices, send(): return lax.ppermute(x, AXES, route[name, step])  7.89 us
    pallas_call x4, Pallas kernels, project_call(): pl.pallas_call(functools.partial(project_kernel, part, first), out_shape=...  5.24 us
    ppermute x4, starting transfers between devices, layer(): block = lax.ppermute(moved[at:at + part], AXES, y_route(seq, tp, distance))  4.31 us
    pallas_call x1, Pallas kernels, layer(): pl.pallas_call(functools.partial(early_kernel, kv_local, group, count, 32...  3.7 us
    pallas_call x1, Pallas kernels, layer(): pl.pallas_call(functools.partial(late_kernel, kv_local, group, part, dept...  2.21 us
  transfers between devices with their start and end apart: 16, of which 6 were waited for; matrix products, arithmetic and copies ran while one was open for 2% of the time, Pallas kernels for 30%

profile of v5, /device:TPU:20, one launch (start us, length us, event | category | flops | bytes accessed | tf_op | source)
XLA Modules:
  0.0 58.9 jit_solution(9418708698587819587)
XLA Ops:
  0.0 1.0 %join.1.refs_2_ = bf16[192,512]{1,0:T(8,128)(2,1)S(1)} custom-call(bf16[192,256]{1,0:T(8,128)(2,1)} %k_ref.1, bf16[192,256]{1,0:T(8,128)(2,1)} %v_ref.1), custom_call_target="tpu_custom_call" | custom-call | tf_op jit(solution)/shard_map/join/pallas_call | solution.py:329
  1.0 1.6 %collective-permute-start = (bf16[192,512]{1,0:T(8,128)(2,1)S(1)}, bf16[192,512]{1,0:T(8,128)(2,1)S(1)}, u32[]{:S(2)}, u32[]{:S(2)}) collective-permute-start(bf16[192,512]{1,0:T(8,128)(2,1)S(1)} %join.1.refs_2_), channel_id=1, source_target_pairs={{0,8},{1,9},{2,10},{3,11},{4,12},{5,13},{6,14},{7,15},{8,0},{9,1},... | collective-permute-start | bytes 589832 | tf_op jit(solution)/shard_map/ppermute | solution.py:327
  2.6 0.0 collective-permute-start.1
  2.6 1.5 %collective-permute-start.5 = (bf16[192,512]{1,0:T(8,128)(2,1)S(1)}, bf16[192,512]{1,0:T(8,128)(2,1)S(1)}, u32[]{:S(2)}, u32[]{:S(2)}) collective-permute-start(bf16[192,512]{1,0:T(8,128)(2,1)S(1)} %join.1.refs_2_), channel_id=1, source_target_pairs={{0,4},{1,5},{2,6},{3,7},{4,0},{5,1},{6,2},{7,3},{8,12},{9,13},{10,... | collective-permute-start | bytes 589832 | tf_op jit(solution)/shard_map/ppermute | solution.py:327
  4.1 0.7 %convert_element_type.39 = f32[1536]{0:T(1024)S(1)} convert(s32[1536]{0:T(1024)} %param.8) | non-fusion elementwise | flops 1536 | bytes 12288 | tf_op jit(solution)/shard_map/convert_element_type | solution.py:338
  4.8 0.1 reshape.3.refs_1_
  4.9 2.8 %collective-permute-done = bf16[192,512]{1,0:T(8,128)(2,1)S(1)} collective-permute-done((bf16[192,512]{1,0:T(8,128)(2,1)S(1)}, bf16[192,512]{1,0:T(8,128)(2,1)S(1)}, u32[]{:S(2)}, u32[]{:S(2)}) %collective-permute-start) | collective-permute-done | bytes 196640 | tf_op jit(solution)/shard_map/ppermute | solution.py:327
  7.7 1.3 %collective-permute-done.1 = bf16[192,512]{1,0:T(8,128)(2,1)S(1)} collective-permute-done((bf16[192,512]{1,0:T(8,128)(2,1)S(1)}, bf16[192,512]{1,0:T(8,128)(2,1)S(1)}, u32[]{:S(2)}, u32[]{:S(2)}) %collective-permute-start.1) | collective-permute-done | bytes 196640 | tf_op jit(solution)/shard_map/ppermute | solution.py:327
  9.0 0.3 collective-permute-start.2
  9.3 0.0 collective-permute-start.3
  9.3 1.6 %collective-permute-start.6 = (bf16[192,512]{1,0:T(8,128)(2,1)S(1)}, bf16[192,512]{1,0:T(8,128)(2,1)S(1)}, u32[]{:S(2)}, u32[]{:S(2)}) collective-permute-start(bf16[192,512]{1,0:T(8,128)(2,1)S(1)} %broadcast_select_fusion.refs_4_), channel_id=1, source_target_pairs={{0,1},{1,0},{2,3},{3,2},{4,5},{5,4},{6,7},{7,6},{8,12},{9,13},{10,... | collective-permute-start | bytes 589832 | tf_op jit(solution)/shard_map/ppermute | solution.py:327
  10.8 3.8 %collective-permute-done.2 = bf16[192,512]{1,0:T(8,128)(2,1)S(1)} collective-permute-done((bf16[192,512]{1,0:T(8,128)(2,1)S(1)}, bf16[192,512]{1,0:T(8,128)(2,1)S(1)}, u32[]{:S(2)}, u32[]{:S(2)}) %collective-permute-start.2) | collective-permute-done | bytes 196640 | tf_op jit(solution)/shard_map/ppermute | solution.py:327
  14.6 0.3 collective-permute-done.3
  15.0 1.6 %collective-permute-start.4 = (bf16[192,512]{1,0:T(8,128)(2,1)S(1)}, bf16[192,512]{1,0:T(8,128)(2,1)S(1)}, u32[]{:S(2)}, u32[]{:S(2)}) collective-permute-start(bf16[192,512]{1,0:T(8,128)(2,1)S(1)} %broadcast_select_fusion.1.refs_6_), channel_id=1, source_target_pairs={{0,1},{1,0},{2,3},{3,2},{4,5},{5,4},{6,7},{7,6},{8,9},{9,8},{10,11... | collective-permute-start | bytes 589832 | tf_op jit(solution)/shard_map/ppermute | solution.py:327
  16.5 2.9 %load.3 = (bf16[1024,1792]{1,0:T(8,128)(2,1)S(1)}, bf16[1024,1280]{1,0:T(8,128)(2,1)S(1)}) custom-call(bf16[1024,8192]{1,0:T(8,128)(2,1)} %w_hbm.5), custom_call_target="tpu_custom_call" | custom-call | bytes 6291456 | tf_op jit(solution)/shard_map/load/pallas_call | solution.py:94
  19.4 2.9 %load.4 = (bf16[1024,1280]{1,0:T(8,128)(2,1)S(1)}, bf16[1024,1792]{1,0:T(8,128)(2,1)S(1)}) custom-call(bf16[1024,8192]{1,0:T(8,128)(2,1)} %w_hbm.5), custom_call_target="tpu_custom_call" | custom-call | bytes 6291456 | tf_op jit(solution)/shard_map/load/pallas_call | solution.py:94
  22.3 0.0 copy-start
  22.3 2.2 %load.5.refs_4_.refs_0_ = bf16[1024,2048]{1,0:T(8,128)(2,1)S(1)} custom-call(bf16[1024,8192]{1,0:T(8,128)(2,1)} %w_hbm.5), custom_call_target="tpu_custom_call" | custom-call | bytes 4194304 | tf_op jit(solution)/shard_map/load/pallas_call | solution.py:94
  24.5 0.0 collective-permute-done.5.refs_3_
  24.5 0.0 collective-permute-done.6.refs_5_
  24.6 3.7 %attend_early.1 = (f32[1536,128]{1,0:T(8,128)S(1)}, f32[1536,128]{1,0:T(8,128)S(1)}, f32[1536,128]{1,0:T(8,128)S(1)}) custom-call(bf16[192,1024]{1,0:T(8,128)(2,1)S(1)} %copy-done, f32[8,192]{1,0:T(8,128)S(1)} %reshape.3.refs_1_, bf16[192,512]{1,0:T(8,128)(2,1)S(1)} %join.1.refs_2_, bf16[192,512]{1,0:T(8,128)(2,1)S(1)} %collective-permute-done.5.refs_3_, ...), custom_call_target="tpu_custom_call" | custom-call | flops 754974720 | bytes 786432 | tf_op jit(solution)/shard_map/attend_early/pallas_call | solution.py:362
  28.3 0.0 collective-permute-done.4.refs_2_
  28.3 2.2 %attend_late.1 = (bf16[192,1024]{1,0:T(8,128)(2,1)S(1)}, bf16[48,1792]{1,0:T(8,128)(2,1)S(1)}, bf16[48,1792]{1,0:T(8,128)(2,1)S(1)}) custom-call(bf16[192,1024]{1,0:T(8,128)(2,1)S(1)} %copy-done, f32[8,192]{1,0:T(8,128)S(1)} %reshape.3.refs_1_, bf16[192,512]{1,0:T(8,128)(2,1)S(1)} %collective-permute-done.4.refs_2_, ...), custom_call_target="tpu_custom_call" | custom-call | flops 855638016 | bytes 4456448 | tf_op jit(solution)/shard_map/attend_late/pallas_call | solution.py:383
  30.5 0.1 collective-permute-start.10
  30.6 2.8 %project_rest.4 = (bf16[48,8192]{1,0:T(8,128)(2,1)S(1)}, bf16[48,8192]{1,0:T(8,128)(2,1)S(1)}) custom-call(bf16[192,1024]{1,0:T(8,128)(2,1)S(1)} %get-tuple-element.33.context_ref, bf16[1024,1792]{1,0:T(8,128)(2,1)S(1)} %get-tuple-element.32.refs_6_.refs_0_, bf16[1024,1280]{1,0:T(8,128)(2,1)S(1)} %get-tuple-element.34.refs_1_.refs_0_, ...), custom_call_target="tpu_custom_call" | custom-call | flops 1610612736 | bytes 16777216 | tf_op jit(solution)/shard_map/project_rest/pallas_call | solution.py:252
  33.3 0.6 collective-permute-start.7
  33.9 0.8 %project_rest.5 = (bf16[48,2048]{1,0:T(8,128)(2,1)S(1)}, bf16[48,2048]{1,0:T(8,128)(2,1)S(1)}) custom-call(bf16[192,1024]{1,0:T(8,128)(2,1)S(1)} %get-tuple-element.33.context_ref, bf16[1024,2048]{1,0:T(8,128)(2,1)S(1)} %load.5.refs_4_.refs_0_), custom_call_target="tpu_custom_call" | custom-call | flops 402653184 | bytes 4194304 | tf_op jit(solution)/shard_map/project_rest/pallas_call | solution.py:252
  34.7 0.1 collective-permute-start.8
  34.8 1.0 %project_rest.6 = (bf16[48,2560]{1,0:T(8,128)(2,1)S(1)}, bf16[48,2560]{1,0:T(8,128)(2,1)S(1)}) custom-call(bf16[192,1024]{1,0:T(8,128)(2,1)S(1)} %get-tuple-element.33.context_ref, bf16[1024,1280]{1,0:T(8,128)(2,1)S(1)} %get-tuple-element.34.refs_1_.refs_0_, bf16[1024,1280]{1,0:T(8,128)(2,1)S(1)} %get-tuple-element.35.refs_2_.refs_1_), custom_call_target="tpu_custom_call" | custom-call | flops 503316480 | bytes 5242880 | tf_op jit(solution)/shard_map/project_rest/pallas_call | solution.py:252
  35.8 0.6 collective-permute-start.12
  36.3 0.7 %project_rest.7 = (bf16[48,1792]{1,0:T(8,128)(2,1)S(1)}, bf16[48,1792]{1,0:T(8,128)(2,1)S(1)}) custom-call(bf16[192,1024]{1,0:T(8,128)(2,1)S(1)} %get-tuple-element.33.context_ref, bf16[1024,1792]{1,0:T(8,128)(2,1)S(1)} %get-tuple-element.36.refs_3_.refs_0_), custom_call_target="tpu_custom_call" | custom-call | flops 352321536 | bytes 3670016 | tf_op jit(solution)/shard_map/project_rest/pallas_call | solution.py:252
  37.0 0.1 collective-permute-start.14
  37.1 0.0 collective-permute-done.10
  37.2 0.6 collective-permute-start.11
  37.7 0.0 collective-permute-done.8
  37.7 0.1 add_convert_fusion.1
  37.8 1.6 %collective-permute-start.9 = (bf16[48,2048]{1,0:T(8,128)(2,1)S(1)}, bf16[48,2048]{1,0:T(8,128)(2,1)S(1)}, u32[]{:S(2)}, u32[]{:S(2)}) collective-permute-start(bf16[48,2048]{1,0:T(8,128)(2,1)S(1)} %add_convert_fusion.1), channel_id=1, source_target_pairs={{0,2},{1,3},{2,0},{3,1},{4,6},{5,7},{6,4},{7,5},{8,10},{9,11},{10,... | collective-permute-start | bytes 589832 | tf_op jit(solution)/shard_map/ppermute | solution.py:408
  39.4 0.0 collective-permute-done.12
  39.4 0.1 add_convert_fusion
  39.5 0.6 collective-permute-start.13
  40.0 0.0 collective-permute-done.14
  40.1 1.6 %collective-permute-start.15 = (bf16[48,1792]{1,0:T(8,128)(2,1)S(1)}, bf16[48,1792]{1,0:T(8,128)(2,1)S(1)}, u32[]{:S(2)}, u32[]{:S(2)}) collective-permute-start(bf16[48,1792]{1,0:T(8,128)(2,1)S(1)} %add_convert_fusion.2), channel_id=1, source_target_pairs={{0,2},{1,3},{2,0},{3,1},{4,6},{5,7},{6,4},{7,5},{8,10},{9,11},{10,... | collective-permute-start | bytes 516104 | tf_op jit(solution)/shard_map/ppermute | solution.py:408
  41.7 2.8 %collective-permute-done.11.refs_0_ = bf16[48,1792]{1,0:T(8,128)(2,1)S(1)} collective-permute-done((bf16[48,1792]{1,0:T(8,128)(2,1)S(1)}, bf16[48,1792]{1,0:T(8,128)(2,1)S(1)}, u32[]{:S(2)}, u32[]{:S(2)}) %collective-permute-start.11) | collective-permute-done | bytes 172064 | tf_op jit(solution)/shard_map/ppermute | solution.py:408
  44.5 12.7 %collective-permute-done.15.refs_2_ = bf16[48,1792]{1,0:T(8,128)(2,1)S(1)} collective-permute-done((bf16[48,1792]{1,0:T(8,128)(2,1)S(1)}, bf16[48,1792]{1,0:T(8,128)(2,1)S(1)}, u32[]{:S(2)}, u32[]{:S(2)}) %collective-permute-start.15) | collective-permute-done | bytes 172064 | tf_op jit(solution)/shard_map/ppermute | solution.py:408
  57.2 0.0 collective-permute-done.7.received_ref
  57.2 0.9 %finish.2.refs_1_ = bf16[48,8192]{1,0:T(8,128)(2,1)} custom-call(bf16[48,8192]{1,0:T(8,128)(2,1)S(1)} %get-tuple-element.37.kept_ref, bf16[48,8192]{1,0:T(8,128)(2,1)S(1)} %collective-permute-done.7.received_ref, bf16[48,1792]{1,0:T(8,128)(2,1)S(1)} %collective-permute-done.11.refs_0_, bf16[48,2560]{1,0:T(8,128)(2,1)S(1)} %collective-permute-done.13.refs_1_, ...), custom_call_target="tpu_custom_call" | custom-call | flops 1572864 | bytes 1572864 | tf_op jit(solution)/shard_map/finish/pallas_call | solution.py:296
  58.1 0.0 collective-permute-done.9.refs_0_
  58.1 0.8 %finish.3 = bf16[48,8192]{1,0:T(8,128)(2,1)} custom-call(bf16[48,8192]{1,0:T(8,128)(2,1)S(1)} %get-tuple-element.37.kept_ref, bf16[48,8192]{1,0:T(8,128)(2,1)S(1)} %collective-permute-done.7.received_ref, bf16[48,2048]{1,0:T(8,128)(2,1)S(1)} %collective-permute-done.9.refs_0_, bf16[48,8192]{1,0:T(8,128)(2,1)} %finish.2.refs_1_), custom_call_target="tpu_custom_call", output_to_operand_aliasing={{}: (3, {})} | custom-call | flops 1572864 | bytes 1572864 | tf_op jit(solution)/shard_map/finish/pallas_call | solution.py:296
  (6 shorter events, 0.1 us)
Async XLA Ops:
  1.0 6.7 %collective-permute-start = (bf16[192,512]{1,0:T(8,128)(2,1)S(1)}, bf16[192,512]{1,0:T(8,128)(2,1)S(1)}, u32[]{:S(2)}, u32[]{:S(2)}) collective-permute-start(bf16[192,512]{1,0:T(8,128)(2,1)S(1)} %join.1.refs_2_), channel_id=1, source_target_pairs={{0,8},{1,9},{2,10},{3,11},{4,12},{5,13},{6,14},{7,15},{8,0},{9,1},... | collective-permute-start | bytes 589832 | tf_op jit(solution)/shard_map/ppermute | solution.py:327
  2.6 6.4 %collective-permute-start.1 = (bf16[192,512]{1,0:T(8,128)(2,1)S(1)}, bf16[192,512]{1,0:T(8,128)(2,1)S(1)}, u32[]{:S(2)}, u32[]{:S(2)}) collective-permute-start(bf16[192,512]{1,0:T(8,128)(2,1)S(1)} %join.1.refs_2_), channel_id=1, source_target_pairs={{0,1},{1,0},{2,3},{3,2},{4,5},{5,4},{6,7},{7,6},{8,16},{9,17},{10,... | collective-permute-start | bytes 589832 | tf_op jit(solution)/shard_map/ppermute | solution.py:327
  2.6 21.9 %collective-permute-start.5 = (bf16[192,512]{1,0:T(8,128)(2,1)S(1)}, bf16[192,512]{1,0:T(8,128)(2,1)S(1)}, u32[]{:S(2)}, u32[]{:S(2)}) collective-permute-start(bf16[192,512]{1,0:T(8,128)(2,1)S(1)} %join.1.refs_2_), channel_id=1, source_target_pairs={{0,4},{1,5},{2,6},{3,7},{4,0},{5,1},{6,2},{7,3},{8,12},{9,13},{10,... | collective-permute-start | bytes 589832 | tf_op jit(solution)/shard_map/ppermute | solution.py:327
  9.0 5.7 %collective-permute-start.2 = (bf16[192,512]{1,0:T(8,128)(2,1)S(1)}, bf16[192,512]{1,0:T(8,128)(2,1)S(1)}, u32[]{:S(2)}, u32[]{:S(2)}) collective-permute-start(bf16[192,512]{1,0:T(8,128)(2,1)S(1)} %collective-permute-done.1), channel_id=1, source_target_pairs={{0,1},{1,0},{2,3},{3,2},{4,5},{5,4},{6,7},{7,6},{8,9},{9,8},{10,11... | collective-permute-start | bytes 589832 | tf_op jit(solution)/shard_map/ppermute | solution.py:327
  9.3 5.7 %collective-permute-start.3 = (bf16[192,512]{1,0:T(8,128)(2,1)S(1)}, bf16[192,512]{1,0:T(8,128)(2,1)S(1)}, u32[]{:S(2)}, u32[]{:S(2)}) collective-permute-start(bf16[192,512]{1,0:T(8,128)(2,1)S(1)} %collective-permute-done), channel_id=1, source_target_pairs={{0,1},{1,0},{2,3},{3,2},{4,5},{5,4},{6,7},{7,6},{8,16},{9,17},{10,... | collective-permute-start | bytes 589832 | tf_op jit(solution)/shard_map/ppermute | solution.py:327
  9.3 15.3 %collective-permute-start.6 = (bf16[192,512]{1,0:T(8,128)(2,1)S(1)}, bf16[192,512]{1,0:T(8,128)(2,1)S(1)}, u32[]{:S(2)}, u32[]{:S(2)}) collective-permute-start(bf16[192,512]{1,0:T(8,128)(2,1)S(1)} %broadcast_select_fusion.refs_4_), channel_id=1, source_target_pairs={{0,1},{1,0},{2,3},{3,2},{4,5},{5,4},{6,7},{7,6},{8,12},{9,13},{10,... | collective-permute-start | bytes 589832 | tf_op jit(solution)/shard_map/ppermute | solution.py:327
  15.0 13.3 %collective-permute-start.4 = (bf16[192,512]{1,0:T(8,128)(2,1)S(1)}, bf16[192,512]{1,0:T(8,128)(2,1)S(1)}, u32[]{:S(2)}, u32[]{:S(2)}) collective-permute-start(bf16[192,512]{1,0:T(8,128)(2,1)S(1)} %broadcast_select_fusion.1.refs_6_), channel_id=1, source_target_pairs={{0,1},{1,0},{2,3},{3,2},{4,5},{5,4},{6,7},{7,6},{8,9},{9,8},{10,11... | collective-permute-start | bytes 589832 | tf_op jit(solution)/shard_map/ppermute | solution.py:327
  22.3 2.3 %copy-start = (bf16[192,1024]{1,0:T(8,128)(2,1)S(1)}, bf16[192,1024]{1,0:T(8,128)(2,1)}, u32[]{:S(2)}) copy-start(bf16[192,1024]{1,0:T(8,128)(2,1)} %refs_0_.3) | copy-start | bytes 1179652
  30.5 6.6 %collective-permute-start.10 = (bf16[48,1792]{1,0:T(8,128)(2,1)S(1)}, bf16[48,1792]{1,0:T(8,128)(2,1)S(1)}, u32[]{:S(2)}, u32[]{:S(2)}) collective-permute-start(bf16[48,1792]{1,0:T(8,128)(2,1)S(1)} %get-tuple-element.42), channel_id=1, source_target_pairs={{0,1},{1,0},{2,3},{3,2},{4,5},{5,4},{6,7},{7,6},{8,9},{9,8},{10,11... | collective-permute-start | bytes 516104 | tf_op jit(solution)/shard_map/ppermute | solution.py:327
  33.3 23.8 %collective-permute-start.7 = (bf16[48,8192]{1,0:T(8,128)(2,1)S(1)}, bf16[48,8192]{1,0:T(8,128)(2,1)S(1)}, u32[]{:S(2)}, u32[]{:S(2)}) collective-permute-start(bf16[48,8192]{1,0:T(8,128)(2,1)S(1)} %get-tuple-element.38), channel_id=1, source_target_pairs={{0,1},{1,0},{2,3},{3,2},{4,5},{5,4},{6,7},{7,6},{8,9},{9,8},{10,11... | collective-permute-start | bytes 2359304 | tf_op jit(solution)/shard_map/ppermute | solution.py:327
  34.7 3.0 %collective-permute-start.8 = (bf16[48,2048]{1,0:T(8,128)(2,1)S(1)}, bf16[48,2048]{1,0:T(8,128)(2,1)S(1)}, u32[]{:S(2)}, u32[]{:S(2)}) collective-permute-start(bf16[48,2048]{1,0:T(8,128)(2,1)S(1)} %get-tuple-element.40), channel_id=1, source_target_pairs={{0,1},{1,0},{2,3},{3,2},{4,5},{5,4},{6,7},{7,6},{8,9},{9,8},{10,11... | collective-permute-start | bytes 589832 | tf_op jit(solution)/shard_map/ppermute | solution.py:327
  35.8 3.6 %collective-permute-start.12 = (bf16[48,2560]{1,0:T(8,128)(2,1)S(1)}, bf16[48,2560]{1,0:T(8,128)(2,1)S(1)}, u32[]{:S(2)}, u32[]{:S(2)}) collective-permute-start(bf16[48,2560]{1,0:T(8,128)(2,1)S(1)} %get-tuple-element.44), channel_id=1, source_target_pairs={{0,1},{1,0},{2,3},{3,2},{4,5},{5,4},{6,7},{7,6},{8,9},{9,8},{10,11... | collective-permute-start | bytes 737288 | tf_op jit(solution)/shard_map/ppermute | solution.py:327
  37.0 3.0 %collective-permute-start.14 = (bf16[48,1792]{1,0:T(8,128)(2,1)S(1)}, bf16[48,1792]{1,0:T(8,128)(2,1)S(1)}, u32[]{:S(2)}, u32[]{:S(2)}) collective-permute-start(bf16[48,1792]{1,0:T(8,128)(2,1)S(1)} %get-tuple-element.46), channel_id=1, source_target_pairs={{0,1},{1,0},{2,3},{3,2},{4,5},{5,4},{6,7},{7,6},{8,9},{9,8},{10,11... | collective-permute-start | bytes 516104 | tf_op jit(solution)/shard_map/ppermute | solution.py:327
  37.2 7.3 %collective-permute-start.11 = (bf16[48,1792]{1,0:T(8,128)(2,1)S(1)}, bf16[48,1792]{1,0:T(8,128)(2,1)S(1)}, u32[]{:S(2)}, u32[]{:S(2)}) collective-permute-start(bf16[48,1792]{1,0:T(8,128)(2,1)S(1)} %add_convert_fusion.3), channel_id=1, source_target_pairs={{0,2},{1,3},{2,0},{3,1},{4,6},{5,7},{6,4},{7,5},{8,10},{9,11},{10,... | collective-permute-start | bytes 516104 | tf_op jit(solution)/shard_map/ppermute | solution.py:408
  37.8 20.3 %collective-permute-start.9 = (bf16[48,2048]{1,0:T(8,128)(2,1)S(1)}, bf16[48,2048]{1,0:T(8,128)(2,1)S(1)}, u32[]{:S(2)}, u32[]{:S(2)}) collective-permute-start(bf16[48,2048]{1,0:T(8,128)(2,1)S(1)} %add_convert_fusion.1), channel_id=1, source_target_pairs={{0,2},{1,3},{2,0},{3,1},{4,6},{5,7},{6,4},{7,5},{8,10},{9,11},{10,... | collective-permute-start | bytes 589832 | tf_op jit(solution)/shard_map/ppermute | solution.py:408
  39.5 17.7 %collective-permute-start.13 = (bf16[48,2560]{1,0:T(8,128)(2,1)S(1)}, bf16[48,2560]{1,0:T(8,128)(2,1)S(1)}, u32[]{:S(2)}, u32[]{:S(2)}) collective-permute-start(bf16[48,2560]{1,0:T(8,128)(2,1)S(1)} %add_convert_fusion), channel_id=1, source_target_pairs={{0,2},{1,3},{2,0},{3,1},{4,6},{5,7},{6,4},{7,5},{8,10},{9,11},{10,... | collective-permute-start | bytes 737288 | tf_op jit(solution)/shard_map/ppermute | solution.py:408
  40.1 17.1 %collective-permute-start.15 = (bf16[48,1792]{1,0:T(8,128)(2,1)S(1)}, bf16[48,1792]{1,0:T(8,128)(2,1)S(1)}, u32[]{:S(2)}, u32[]{:S(2)}) collective-permute-start(bf16[48,1792]{1,0:T(8,128)(2,1)S(1)} %add_convert_fusion.2), channel_id=1, source_target_pairs={{0,2},{1,3},{2,0},{3,1},{4,6},{5,7},{6,4},{7,5},{8,10},{9,11},{10,... | collective-permute-start | bytes 516104 | tf_op jit(solution)/shard_map/ppermute | solution.py:408

commit v6 on v5

--- a/solution.py
+++ b/solution.py
@@ -63,11 +63,13 @@
 
 
 def join_kernel(k_ref, v_ref, out_ref, sems):
-    width = k_ref.shape[1]
-    copies = [
-        pltpu.make_async_copy(k_ref, out_ref.at[:, pl.ds(0, width)], sems.at[0]),
-        pltpu.make_async_copy(v_ref, out_ref.at[:, pl.ds(width, width)], sems.at[1]),
-    ]
+    copies = []
+    for h in range(k_ref.shape[1] // HD):
+        for i, ref in enumerate((k_ref, v_ref)):
+            at = 2 * h + i
+            into = out_ref.at[:, pl.ds(at * HD, HD)]
+            source = ref.at[:, pl.ds(h * HD, HD)]
+            copies.append(pltpu.make_async_copy(source, into, sems.at[at]))
     for copy in copies:
         copy.start()
     for copy in copies:
@@ -160,7 +162,8 @@
     allowed = allowed & ((key_at <= query_at) | (key_at >= tokens))
     bias_ref[...] = jnp.where(allowed, 0.0, -jnp.inf)
     for h in range(kv_local):
-        keys = jnp.concatenate([b[:, pl.ds(h * HD, HD)] for b in blocks], axis=0)
+        cols = pl.ds(2 * h * HD, HD)
+        keys = jnp.concatenate([b[:, cols] for b in blocks], axis=0)
         s_ref[...] = scores_of(stack(q_ref, h, group), keys)
         for r in range(0, stacked, step):
             at = pl.ds(r, step)
@@ -172,32 +175,36 @@
             p_ref[at, :] = weight.astype(jnp.bfloat16)
             top_ref[into, :] = jnp.broadcast_to(top, (step, HD))
             sum_ref[into, :] = jnp.broadcast_to(total, (step, HD))
-        cols = pl.ds((kv_local + h) * HD, HD)
+        cols = pl.ds((2 * h + 1) * HD, HD)
         values = jnp.concatenate([b[:, cols] for b in blocks], axis=0)
         acc_ref[pl.ds(h * stacked, stacked), :] = jnp.dot(
             p_ref[...], values, preferred_element_type=jnp.float32
         )
 
 
-def project(context_ref, first, w_ref, send_ref, keep_ref, part):
+def project(context_ref, first, w_ref, send_ref, keep_ref, part, top=0, more_ref=None):
     step = 256
     count = keep_ref.shape[0] // part
     for c in range(0, w_ref.shape[1], step):
         at = pl.ds(c, step)
         rows = jnp.dot(
             context_ref[pl.ds(first, 2 * count * part), :],
-            w_ref[:, at],
+            w_ref[pl.ds(top, context_ref.shape[1]), at],
             preferred_element_type=jnp.float32,
-        ).astype(jnp.bfloat16)
+        )
+        if more_ref is not None:
+            rows = rows + more_ref[:, at]
+        rows = rows.astype(jnp.bfloat16)
         for i in range(count):
             into = pl.ds(i * part, part)
             keep_ref[into, at] = rows[2 * i * part : (2 * i + 1) * part]
             send_ref[into, at] = rows[(2 * i + 1) * part : (2 * i + 2) * part]
 
 
-def late_kernel(kv_local, group, part, depth, *refs):
+def late_kernel(h, kv_local, group, part, depth, *refs):
     q_ref, docs_ref, block, acc_ref, top_ref, sum_ref, w_ref = refs[:7]
-    out_ref, send_ref, keep_ref, context_ref = refs[7:]
+    context_ref, here_ref = refs[-2:]
+    refs = refs[7:-2]
     tokens = q_ref.shape[0]
     stacked = group * tokens
     me, rank = lax.axis_index("seq"), lax.axis_index("tp")
@@ -206,33 +213,51 @@
     bias = jnp.where(
         query_doc(docs_ref, me) == key_doc(docs_ref, far, me), 0.0, -jnp.inf
     )
-    for h in range(kv_local):
-        keys = block[:, pl.ds(h * HD, HD)]
-        values = block[:, pl.ds((kv_local + h) * HD, HD)]
-        scores = scores_of(stack(q_ref, h, group), keys)
-        scores = scores * SCALE + jnp.concatenate([bias] * group, axis=0)
-        at = pl.ds(h * stacked, stacked)
-        old = top_ref[at, :]
-        new = jnp.maximum(old[:, :1], jnp.max(scores, axis=-1, keepdims=True))
-        weight = jnp.exp2(scores - new)
-        rescale = jnp.exp2(old - new)
-        total = sum_ref[at, :] * rescale + jnp.sum(weight, axis=-1, keepdims=True)
-        added = jnp.dot(
-            weight.astype(jnp.bfloat16), values, preferred_element_type=jnp.float32
-        )
-        context = (acc_ref[at, :] * rescale + added) / total
-        context = context.astype(jnp.bfloat16)
-        for g in range(group):
-            cols = pl.ds((h * group + g) * HD, HD)
-            context_ref[:, cols] = context[g * tokens : (g + 1) * tokens]
+    keys, values = block[:, pl.ds(0, HD)], block[:, pl.ds(HD, HD)]
+    scores = scores_of(stack(q_ref, h, group), keys)
+    scores = scores * SCALE + jnp.concatenate([bias] * group, axis=0)
+    at = pl.ds(h * stacked, stacked)
+    old = top_ref[at, :]
+    new = jnp.maximum(old[:, :1], jnp.max(scores, axis=-1, keepdims=True))
+    weight = jnp.exp2(scores - new)
+    rescale = jnp.exp2(old - new)
+    total = sum_ref[at, :] * rescale + jnp.sum(weight, axis=-1, keepdims=True)
+    added = jnp.dot(
+        weight.astype(jnp.bfloat16), values, preferred_element_type=jnp.float32
+    )
+    context = (acc_ref[at, :] * rescale + added) / total
+    context = context.astype(jnp.bfloat16)
+    for g in range(group):
+        rows = context[g * tokens : (g + 1) * tokens]
+        context_ref[:, pl.ds(g * HD, HD)] = rows
     at = 0
     for distance in range(1, chips + 1):
         base = lax.rem(rank // 2 + distance, chips) * 2
         for core in (rank % 2, 1 - rank % 2):
             first = pl.multiple_of((base + core) * part, 8)
-            out_ref[pl.ds(at, part), :] = context_ref[pl.ds(first, part), :]
+            here_ref[pl.ds(at, part), :] = context_ref[pl.ds(first, part), :]
             at += part
-    project(out_ref, 0, w_ref, send_ref, keep_ref, part)
+    depth_of = group * HD
+    top = h * depth_of
+    more_ref, before_ref = refs[:2] if h else (None, None)
+    if h < kv_local - 1:
+        part_ref, out_ref = refs[-2:]
+        rows = part_ref.shape[0]
+        step = 256
+        for c in range(0, w_ref.shape[1], step):
+            cols = pl.ds(c, step)
+            product = jnp.dot(
+                here_ref[pl.ds(0, rows), :],
+                w_ref[pl.ds(top, depth_of), cols],
+                preferred_element_type=jnp.float32,
+            )
+            part_ref[:, cols] = product if more_ref is None else product + more_ref[:, cols]
+    else:
+        send_ref, keep_ref, out_ref = refs[-3:]
+        project(here_ref, 0, w_ref, send_ref, keep_ref, part, top, more_ref)
+    out_ref[:, pl.ds(top, depth_of)] = here_ref[...]
+    if h:
+        out_ref[:, pl.ds(0, top)] = before_ref[...]
 
 
 def project_kernel(part, first, context_ref, *refs):
@@ -331,7 +356,7 @@
         out_shape=pltpu.VMEM((tokens, 2 * kv_local * HD), jnp.bfloat16),
         in_specs=[ANY, ANY],
         out_specs=VMEM,
-        scratch_shapes=[pltpu.SemaphoreType.DMA((2,))],
+        scratch_shapes=[pltpu.SemaphoreType.DMA((2 * kv_local,))],
         compiler_params=pltpu.CompilerParams(vmem_limit_bytes=2 * MIB),
         name="join",
     )(in_hbm(key_rows), in_hbm(value_rows))
@@ -353,13 +378,17 @@
                 send(odd, "even", distance + 1),
                 send(even, "odd", distance + 1),
             )
-        blocks.append(send(blocks[-1], "col", distance))
-    last_block = blocks.pop()
+        if distance < depth:
+            blocks.append(send(blocks[-1], "col", distance))
+    last_blocks = []
+    for h in range(kv_local):
+        piece = blocks[-1][:, 2 * h * HD : 2 * (h + 1) * HD]
+        last_blocks.append(lax.ppermute(piece, AXES, route["col", depth]))
     count = len(blocks)
 
     stacked = group * tokens
     state = jax.ShapeDtypeStruct((kv_local * stacked, HD), jnp.float32)
-    acc, top, total = pl.pallas_call(
+    early = pl.pallas_call(
         functools.partial(early_kernel, kv_local, group, count, 32),
         out_shape=(state, state, state),
         in_specs=[VMEM] * (2 + count),
@@ -376,24 +405,35 @@
         ),
         compiler_params=pltpu.CompilerParams(vmem_limit_bytes=EARLY * MIB),
         name="attend_early",
-    )(query_rows, docs, *blocks)
+    )
+    acc, top, total = early(query_rows, docs, *blocks)
 
     remote = (chips - 1) * part
     out = jax.ShapeDtypeStruct((remote, cuts[1]), jnp.bfloat16)
-    context, sent, kept = pl.pallas_call(
-        functools.partial(late_kernel, kv_local, group, part, depth),
-        out_shape=(jax.ShapeDtypeStruct((tokens, width), jnp.bfloat16), out, out),
-        in_specs=[VMEM] * 7,
-        out_specs=(VMEM, VMEM, VMEM),
-        scratch_shapes=[pltpu.VMEM((tokens, width), jnp.bfloat16)],
-        cost_estimate=pl.CostEstimate(
-            flops=4 * tokens * tokens * width + 2 * tokens * width * cuts[1],
-            transcendentals=tokens * tokens * width // HD,
-            bytes_accessed=4 * tokens * width + 2 * width * cuts[1],
-        ),
-        compiler_params=pltpu.CompilerParams(vmem_limit_bytes=LATE * MIB),
-        name="attend_late",
-    )(query_rows, docs, last_block, acc, top, total, first)
+    share = group * HD
+    so_far = ()
+    for h, last_block in enumerate(last_blocks):
+        context_shape = jax.ShapeDtypeStruct((tokens, (h + 1) * share), jnp.bfloat16)
+        if h < kv_local - 1:
+            product = jax.ShapeDtypeStruct((2 * remote, cuts[1]), jnp.float32)
+            shapes = (product, context_shape)
+        else:
+            shapes = (out, out, context_shape)
+        so_far = pl.pallas_call(
+            functools.partial(late_kernel, h, kv_local, group, part, depth),
+            out_shape=shapes,
+            in_specs=[VMEM] * (7 + len(so_far)),
+            out_specs=(VMEM,) * len(shapes),
+            scratch_shapes=[pltpu.VMEM((tokens, share), jnp.bfloat16)] * 2,
+            cost_estimate=pl.CostEstimate(
+                flops=4 * tokens * tokens * share + 4 * remote * share * cuts[1],
+                transcendentals=tokens * tokens * group,
+                bytes_accessed=4 * tokens * share + 2 * share * cuts[1],
+            ),
+            compiler_params=pltpu.CompilerParams(vmem_limit_bytes=LATE * MIB),
+            name="attend_late",
+        )(query_rows, docs, last_block, acc, top, total, first, *so_far)
+    sent, kept, context = so_far
 
     arrived = []
     for i, weight in enumerate(weights):

time: 59.1 us -> 60.3 us (1.020)
  the two profiles are of different devices: /device:TPU:20 before, /device:TPU:22 now
where the time goes in v6:
time: 60.3 us; the launch traced here: 60.1 us
  waiting for transfers between devices  25.6 us (42%)
  Pallas kernels  22.4 us (37%)
  starting transfers between devices  10.8 us (18%)
  other arithmetic  0.94 us (2%)
    ppermute x4, waiting for transfers between devices, layer(): block = lax.ppermute(moved[at:at + part], AXES, y_route(seq, tp, distance))  15.5 us
    ppermute x11, waiting for transfers between devices, send(): return lax.ppermute(x, AXES, route[name, step])  10.1 us
    pallas_call x3, Pallas kernels, load_call(): pl.pallas_call(functools.partial(load_kernel, cuts[0]), out_shape=[pltpu....  7.99 us
    pallas_call x4, Pallas kernels, project_call(): pl.pallas_call(functools.partial(project_kernel, part, first), out_shape=...  5.24 us
    ppermute x11, starting transfers between devices, send(): return lax.ppermute(x, AXES, route[name, step])  4.42 us
    ppermute x4, starting transfers between devices, layer(): block = lax.ppermute(moved[at:at + part], AXES, y_route(seq, tp, distance))  4.31 us
    pallas_call x1, Pallas kernels, layer(): acc, top, total = early(query_rows, docs, *blocks)  3.71 us
    pallas_call x2, Pallas kernels, layer(): pl.pallas_call(functools.partial(late_kernel, h, kv_local, group, part, d...  2.92 us
  transfers between devices with their start and end apart: 17, of which 6 were waited for; matrix products, arithmetic and copies ran while one was open for 2% of the time, Pallas kernels for 32%

profile of v6, /device:TPU:22, one launch (start us, length us, event | category | flops | bytes accessed | tf_op | source)
XLA Modules:
  0.0 60.1 jit_solution(11261546190466828207)
XLA Ops:
  0.0 0.9 %join.1.refs_2_ = bf16[192,512]{1,0:T(8,128)(2,1)S(1)} custom-call(bf16[192,256]{1,0:T(8,128)(2,1)} %k_ref.1, bf16[192,256]{1,0:T(8,128)(2,1)} %v_ref.1), custom_call_target="tpu_custom_call" | custom-call | tf_op jit(solution)/shard_map/join/pallas_call | solution.py:354
  0.9 1.6 %collective-permute-start = (bf16[192,512]{1,0:T(8,128)(2,1)S(1)}, bf16[192,512]{1,0:T(8,128)(2,1)S(1)}, u32[]{:S(2)}, u32[]{:S(2)}) collective-permute-start(bf16[192,512]{1,0:T(8,128)(2,1)S(1)} %join.1.refs_2_), channel_id=1, source_target_pairs={{0,8},{1,9},{2,10},{3,11},{4,12},{5,13},{6,14},{7,15},{8,0},{9,1},... | collective-permute-start | bytes 589832 | tf_op jit(solution)/shard_map/ppermute | solution.py:352
  2.6 0.5 collective-permute-start.5
  3.1 0.7 %convert_element_type.39 = f32[1536]{0:T(1024)S(1)} convert(s32[1536]{0:T(1024)} %param.8) | non-fusion elementwise | flops 1536 | bytes 12288 | tf_op jit(solution)/shard_map/convert_element_type | solution.py:363
  3.8 0.1 reshape.3.refs_1_
  3.9 3.8 %collective-permute-done = bf16[192,512]{1,0:T(8,128)(2,1)S(1)} collective-permute-done((bf16[192,512]{1,0:T(8,128)(2,1)S(1)}, bf16[192,512]{1,0:T(8,128)(2,1)S(1)}, u32[]{:S(2)}, u32[]{:S(2)}) %collective-permute-start) | collective-permute-done | bytes 196640 | tf_op jit(solution)/shard_map/ppermute | solution.py:352
  7.6 1.3 %collective-permute-done.1 = bf16[192,512]{1,0:T(8,128)(2,1)S(1)} collective-permute-done((bf16[192,512]{1,0:T(8,128)(2,1)S(1)}, bf16[192,512]{1,0:T(8,128)(2,1)S(1)}, u32[]{:S(2)}, u32[]{:S(2)}) %collective-permute-start.1) | collective-permute-done | bytes 196640 | tf_op jit(solution)/shard_map/ppermute | solution.py:352
  8.9 0.3 collective-permute-start.2
  9.2 0.0 collective-permute-start.3
  9.2 0.6 collective-permute-start.6
  9.8 4.8 %collective-permute-done.2 = bf16[192,512]{1,0:T(8,128)(2,1)S(1)} collective-permute-done((bf16[192,512]{1,0:T(8,128)(2,1)S(1)}, bf16[192,512]{1,0:T(8,128)(2,1)S(1)}, u32[]{:S(2)}, u32[]{:S(2)}) %collective-permute-start.2) | collective-permute-done | bytes 196640 | tf_op jit(solution)/shard_map/ppermute | solution.py:352
  14.6 0.3 collective-permute-done.3
  14.9 0.6 collective-permute-start.7
  15.5 1.5 %collective-permute-start.4 = (bf16[192,256]{1,0:T(8,128)(2,1)S(1)}, bf16[192,256]{1,0:T(8,128)(2,1)S(1)}, u32[]{:S(2)}, u32[]{:S(2)}) collective-permute-start(bf16[192,256]{1,0:T(8,128)(2,1)S(1)} %get-tuple-element.52), channel_id=1, source_target_pairs={{0,1},{1,0},{2,3},{3,2},{4,5},{5,4},{6,7},{7,6},{8,9},{9,8},{10,11... | collective-permute-start | bytes 294920 | tf_op jit(solution)/shard_map/ppermute | solution.py:386
  17.0 2.9 %load.3 = (bf16[1024,1792]{1,0:T(8,128)(2,1)S(1)}, bf16[1024,1280]{1,0:T(8,128)(2,1)S(1)}) custom-call(bf16[1024,8192]{1,0:T(8,128)(2,1)} %w_hbm.5), custom_call_target="tpu_custom_call" | custom-call | bytes 6291456 | tf_op jit(solution)/shard_map/load/pallas_call | solution.py:96
  19.9 2.9 %load.4 = (bf16[1024,1280]{1,0:T(8,128)(2,1)S(1)}, bf16[1024,1792]{1,0:T(8,128)(2,1)S(1)}) custom-call(bf16[1024,8192]{1,0:T(8,128)(2,1)} %w_hbm.5), custom_call_target="tpu_custom_call" | custom-call | bytes 6291456 | tf_op jit(solution)/shard_map/load/pallas_call | solution.py:96
  22.8 0.0 copy-start
  22.8 2.2 %load.5.refs_4_.refs_0_ = bf16[1024,2048]{1,0:T(8,128)(2,1)S(1)} custom-call(bf16[1024,8192]{1,0:T(8,128)(2,1)} %w_hbm.5), custom_call_target="tpu_custom_call" | custom-call | bytes 4194304 | tf_op jit(solution)/shard_map/load/pallas_call | solution.py:96
  25.0 0.0 collective-permute-done.5.refs_3_
  25.0 0.0 collective-permute-done.6.refs_5_
  25.1 3.7 %attend_early.1 = (f32[1536,128]{1,0:T(8,128)S(1)}, f32[1536,128]{1,0:T(8,128)S(1)}, f32[1536,128]{1,0:T(8,128)S(1)}) custom-call(bf16[192,1024]{1,0:T(8,128)(2,1)S(1)} %copy-done, f32[8,192]{1,0:T(8,128)S(1)} %reshape.3.refs_1_, bf16[192,512]{1,0:T(8,128)(2,1)S(1)} %join.1.refs_2_, bf16[192,512]{1,0:T(8,128)(2,1)S(1)} %collective-permute-done.5.refs_3_, ...), custom_call_target="tpu_custom_call" | custom-call | flops 754974720 | bytes 786432 | tf_op jit(solution)/shard_map/attend_early/pallas_call | solution.py:409
  28.8 0.0 collective-permute-done.7.refs_2_
  28.8 1.5 %attend_late.2 = (f32[96,1792]{1,0:T(8,128)S(1)}, bf16[192,512]{1,0:T(8,128)(2,1)S(1)}) custom-call(bf16[192,1024]{1,0:T(8,128)(2,1)S(1)} %copy-done, f32[8,192]{1,0:T(8,128)S(1)} %reshape.3.refs_1_, bf16[192,256]{1,0:T(8,128)(2,1)S(1)} %collective-permute-done.7.refs_2_, f32[1536,128]{1,0:T(8,128)S(1)} %get-tuple-element.31.refs_3_, ...), custom_call_target="tpu_custom_call" | custom-call | flops 251658240 | bytes 2228224 | tf_op jit(solution)/shard_map/attend_late/pallas_call | solution.py:422
  30.3 1.5 %attend_late.3 = (bf16[48,1792]{1,0:T(8,128)(2,1)S(1)}, bf16[48,1792]{1,0:T(8,128)(2,1)S(1)}, bf16[192,1024]{1,0:T(8,128)(2,1)S(1)}) custom-call(bf16[192,1024]{1,0:T(8,128)(2,1)S(1)} %copy-done, f32[8,192]{1,0:T(8,128)S(1)} %reshape.3.refs_1_, bf16[192,256]{1,0:T(8,128)(2,1)S(1)} %collective-permute-done.4.refs_2_, ...), custom_call_target="tpu_custom_call" | custom-call | flops 251658240 | bytes 2228224 | tf_op jit(solution)/shard_map/attend_late/pallas_call | solution.py:422
  31.7 0.1 collective-permute-start.11
  31.8 2.8 %project_rest.4 = (bf16[48,8192]{1,0:T(8,128)(2,1)S(1)}, bf16[48,8192]{1,0:T(8,128)(2,1)S(1)}) custom-call(bf16[192,1024]{1,0:T(8,128)(2,1)S(1)} %get-tuple-element.37.context_ref, bf16[1024,1792]{1,0:T(8,128)(2,1)S(1)} %get-tuple-element.34.refs_6_.refs_0_, bf16[1024,1280]{1,0:T(8,128)(2,1)S(1)} %get-tuple-element.38.refs_1_.refs_0_, ...), custom_call_target="tpu_custom_call" | custom-call | flops 1610612736 | bytes 16777216 | tf_op jit(solution)/shard_map/project_rest/pallas_call | solution.py:277
  34.6 0.6 collective-permute-start.8
  35.1 0.8 %project_rest.5 = (bf16[48,2048]{1,0:T(8,128)(2,1)S(1)}, bf16[48,2048]{1,0:T(8,128)(2,1)S(1)}) custom-call(bf16[192,1024]{1,0:T(8,128)(2,1)S(1)} %get-tuple-element.37.context_ref, bf16[1024,2048]{1,0:T(8,128)(2,1)S(1)} %load.5.refs_4_.refs_0_), custom_call_target="tpu_custom_call" | custom-call | flops 402653184 | bytes 4194304 | tf_op jit(solution)/shard_map/project_rest/pallas_call | solution.py:277
  35.9 0.1 collective-permute-start.9
  36.0 1.0 %project_rest.6 = (bf16[48,2560]{1,0:T(8,128)(2,1)S(1)}, bf16[48,2560]{1,0:T(8,128)(2,1)S(1)}) custom-call(bf16[192,1024]{1,0:T(8,128)(2,1)S(1)} %get-tuple-element.37.context_ref, bf16[1024,1280]{1,0:T(8,128)(2,1)S(1)} %get-tuple-element.38.refs_1_.refs_0_, bf16[1024,1280]{1,0:T(8,128)(2,1)S(1)} %get-tuple-element.39.refs_2_.refs_1_), custom_call_target="tpu_custom_call" | custom-call | flops 503316480 | bytes 5242880 | tf_op jit(solution)/shard_map/project_rest/pallas_call | solution.py:277
  37.0 0.6 collective-permute-start.13
  37.5 0.7 %project_rest.7 = (bf16[48,1792]{1,0:T(8,128)(2,1)S(1)}, bf16[48,1792]{1,0:T(8,128)(2,1)S(1)}) custom-call(bf16[192,1024]{1,0:T(8,128)(2,1)S(1)} %get-tuple-element.37.context_ref, bf16[1024,1792]{1,0:T(8,128)(2,1)S(1)} %get-tuple-element.40.refs_3_.refs_0_), custom_call_target="tpu_custom_call" | custom-call | flops 352321536 | bytes 3670016 | tf_op jit(solution)/shard_map/project_rest/pallas_call | solution.py:277
  38.3 0.1 collective-permute-start.15
  38.3 0.0 collective-permute-done.11
  38.4 0.6 collective-permute-start.12
  39.0 0.0 collective-permute-done.9
  39.0 0.1 add_convert_fusion.1
  39.0 1.6 %collective-permute-start.10 = (bf16[48,2048]{1,0:T(8,128)(2,1)S(1)}, bf16[48,2048]{1,0:T(8,128)(2,1)S(1)}, u32[]{:S(2)}, u32[]{:S(2)}) collective-permute-start(bf16[48,2048]{1,0:T(8,128)(2,1)S(1)} %add_convert_fusion.1), channel_id=1, source_target_pairs={{0,2},{1,3},{2,0},{3,1},{4,6},{5,7},{6,4},{7,5},{8,10},{9,11},{10,... | collective-permute-start | bytes 589832 | tf_op jit(solution)/shard_map/ppermute | solution.py:448
  40.6 0.1 add_convert_fusion
  40.7 0.6 collective-permute-start.14
  41.3 1.6 %collective-permute-start.16 = (bf16[48,1792]{1,0:T(8,128)(2,1)S(1)}, bf16[48,1792]{1,0:T(8,128)(2,1)S(1)}, u32[]{:S(2)}, u32[]{:S(2)}) collective-permute-start(bf16[48,1792]{1,0:T(8,128)(2,1)S(1)} %add_convert_fusion.2), channel_id=1, source_target_pairs={{0,2},{1,3},{2,0},{3,1},{4,6},{5,7},{6,4},{7,5},{8,10},{9,11},{10,... | collective-permute-start | bytes 516104 | tf_op jit(solution)/shard_map/ppermute | solution.py:448
  42.9 2.8 %collective-permute-done.12.refs_0_ = bf16[48,1792]{1,0:T(8,128)(2,1)S(1)} collective-permute-done((bf16[48,1792]{1,0:T(8,128)(2,1)S(1)}, bf16[48,1792]{1,0:T(8,128)(2,1)S(1)}, u32[]{:S(2)}, u32[]{:S(2)}) %collective-permute-start.12) | collective-permute-done | bytes 172064 | tf_op jit(solution)/shard_map/ppermute | solution.py:448
  45.7 12.7 %collective-permute-done.16.refs_2_ = bf16[48,1792]{1,0:T(8,128)(2,1)S(1)} collective-permute-done((bf16[48,1792]{1,0:T(8,128)(2,1)S(1)}, bf16[48,1792]{1,0:T(8,128)(2,1)S(1)}, u32[]{:S(2)}, u32[]{:S(2)}) %collective-permute-start.16) | collective-permute-done | bytes 172064 | tf_op jit(solution)/shard_map/ppermute | solution.py:448
  58.4 0.0 collective-permute-done.14.refs_1_
  58.4 0.0 collective-permute-done.8.received_ref
  58.4 0.9 %finish.2.refs_1_ = bf16[48,8192]{1,0:T(8,128)(2,1)} custom-call(bf16[48,8192]{1,0:T(8,128)(2,1)S(1)} %get-tuple-element.41.kept_ref, bf16[48,8192]{1,0:T(8,128)(2,1)S(1)} %collective-permute-done.8.received_ref, bf16[48,1792]{1,0:T(8,128)(2,1)S(1)} %collective-permute-done.12.refs_0_, bf16[48,2560]{1,0:T(8,128)(2,1)S(1)} %collective-permute-done.14.refs_1_, ...), custom_call_target="tpu_custom_call" | custom-call | flops 1572864 | bytes 1572864 | tf_op jit(solution)/shard_map/finish/pallas_call | solution.py:321
  59.3 0.0 collective-permute-done.10.refs_0_
  59.4 0.8 %finish.3 = bf16[48,8192]{1,0:T(8,128)(2,1)} custom-call(bf16[48,8192]{1,0:T(8,128)(2,1)S(1)} %get-tuple-element.41.kept_ref, bf16[48,8192]{1,0:T(8,128)(2,1)S(1)} %collective-permute-done.8.received_ref, bf16[48,2048]{1,0:T(8,128)(2,1)S(1)} %collective-permute-done.10.refs_0_, bf16[48,8192]{1,0:T(8,128)(2,1)} %finish.2.refs_1_), custom_call_target="tpu_custom_call", output_to_operand_aliasing={{}: (3, {})} | custom-call | flops 1572864 | bytes 1572864 | tf_op jit(solution)/shard_map/finish/pallas_call | solution.py:321
  (10 shorter events, 0.2 us)
Async XLA Ops:
  0.9 6.7 %collective-permute-start = (bf16[192,512]{1,0:T(8,128)(2,1)S(1)}, bf16[192,512]{1,0:T(8,128)(2,1)S(1)}, u32[]{:S(2)}, u32[]{:S(2)}) collective-permute-start(bf16[192,512]{1,0:T(8,128)(2,1)S(1)} %join.1.refs_2_), channel_id=1, source_target_pairs={{0,8},{1,9},{2,10},{3,11},{4,12},{5,13},{6,14},{7,15},{8,0},{9,1},... | collective-permute-start | bytes 589832 | tf_op jit(solution)/shard_map/ppermute | solution.py:352
  2.6 6.4 %collective-permute-start.1 = (bf16[192,512]{1,0:T(8,128)(2,1)S(1)}, bf16[192,512]{1,0:T(8,128)(2,1)S(1)}, u32[]{:S(2)}, u32[]{:S(2)}) collective-permute-start(bf16[192,512]{1,0:T(8,128)(2,1)S(1)} %join.1.refs_2_), channel_id=1, source_target_pairs={{0,1},{1,0},{2,3},{3,2},{4,5},{5,4},{6,7},{7,6},{8,16},{9,17},{10,... | collective-permute-start | bytes 589832 | tf_op jit(solution)/shard_map/ppermute | solution.py:352
  2.6 22.5 %collective-permute-start.5 = (bf16[192,512]{1,0:T(8,128)(2,1)S(1)}, bf16[192,512]{1,0:T(8,128)(2,1)S(1)}, u32[]{:S(2)}, u32[]{:S(2)}) collective-permute-start(bf16[192,512]{1,0:T(8,128)(2,1)S(1)} %join.1.refs_2_), channel_id=1, source_target_pairs={{0,4},{1,5},{2,6},{3,7},{4,0},{5,1},{6,2},{7,3},{8,12},{9,13},{10,... | collective-permute-start | bytes 589832 | tf_op jit(solution)/shard_map/ppermute | solution.py:352
  8.9 5.7 %collective-permute-start.2 = (bf16[192,512]{1,0:T(8,128)(2,1)S(1)}, bf16[192,512]{1,0:T(8,128)(2,1)S(1)}, u32[]{:S(2)}, u32[]{:S(2)}) collective-permute-start(bf16[192,512]{1,0:T(8,128)(2,1)S(1)} %collective-permute-done.1), channel_id=1, source_target_pairs={{0,1},{1,0},{2,3},{3,2},{4,5},{5,4},{6,7},{7,6},{8,9},{9,8},{10,11... | collective-permute-start | bytes 589832 | tf_op jit(solution)/shard_map/ppermute | solution.py:352
  9.2 5.7 %collective-permute-start.3 = (bf16[192,512]{1,0:T(8,128)(2,1)S(1)}, bf16[192,512]{1,0:T(8,128)(2,1)S(1)}, u32[]{:S(2)}, u32[]{:S(2)}) collective-permute-start(bf16[192,512]{1,0:T(8,128)(2,1)S(1)} %collective-permute-done), channel_id=1, source_target_pairs={{0,1},{1,0},{2,3},{3,2},{4,5},{5,4},{6,7},{7,6},{8,16},{9,17},{10,... | collective-permute-start | bytes 589832 | tf_op jit(solution)/shard_map/ppermute | solution.py:352
  9.2 15.8 %collective-permute-start.6 = (bf16[192,512]{1,0:T(8,128)(2,1)S(1)}, bf16[192,512]{1,0:T(8,128)(2,1)S(1)}, u32[]{:S(2)}, u32[]{:S(2)}) collective-permute-start(bf16[192,512]{1,0:T(8,128)(2,1)S(1)} %broadcast_select_fusion.refs_4_), channel_id=1, source_target_pairs={{0,1},{1,0},{2,3},{3,2},{4,5},{5,4},{6,7},{7,6},{8,12},{9,13},{10,... | collective-permute-start | bytes 589832 | tf_op jit(solution)/shard_map/ppermute | solution.py:352
  14.9 13.9 %collective-permute-start.7 = (bf16[192,256]{1,0:T(8,128)(2,1)S(1)}, bf16[192,256]{1,0:T(8,128)(2,1)S(1)}, u32[]{:S(2)}, u32[]{:S(2)}) collective-permute-start(bf16[192,256]{1,0:T(8,128)(2,1)S(1)} %get-tuple-element.51), channel_id=1, source_target_pairs={{0,1},{1,0},{2,3},{3,2},{4,5},{5,4},{6,7},{7,6},{8,9},{9,8},{10,11... | collective-permute-start | bytes 294920 | tf_op jit(solution)/shard_map/ppermute | solution.py:386
  15.5 14.7 %collective-permute-start.4 = (bf16[192,256]{1,0:T(8,128)(2,1)S(1)}, bf16[192,256]{1,0:T(8,128)(2,1)S(1)}, u32[]{:S(2)}, u32[]{:S(2)}) collective-permute-start(bf16[192,256]{1,0:T(8,128)(2,1)S(1)} %get-tuple-element.52), channel_id=1, source_target_pairs={{0,1},{1,0},{2,3},{3,2},{4,5},{5,4},{6,7},{7,6},{8,9},{9,8},{10,11... | collective-permute-start | bytes 294920 | tf_op jit(solution)/shard_map/ppermute | solution.py:386
  22.8 2.3 %copy-start = (bf16[192,1024]{1,0:T(8,128)(2,1)S(1)}, bf16[192,1024]{1,0:T(8,128)(2,1)}, u32[]{:S(2)}) copy-start(bf16[192,1024]{1,0:T(8,128)(2,1)} %refs_0_.5) | copy-start | bytes 1179652
  31.7 6.6 %collective-permute-start.11 = (bf16[48,1792]{1,0:T(8,128)(2,1)S(1)}, bf16[48,1792]{1,0:T(8,128)(2,1)S(1)}, u32[]{:S(2)}, u32[]{:S(2)}) collective-permute-start(bf16[48,1792]{1,0:T(8,128)(2,1)S(1)} %get-tuple-element.46), channel_id=1, source_target_pairs={{0,1},{1,0},{2,3},{3,2},{4,5},{5,4},{6,7},{7,6},{8,9},{9,8},{10,11... | collective-permute-start | bytes 516104 | tf_op jit(solution)/shard_map/ppermute | solution.py:352
  34.6 23.8 %collective-permute-start.8 = (bf16[48,8192]{1,0:T(8,128)(2,1)S(1)}, bf16[48,8192]{1,0:T(8,128)(2,1)S(1)}, u32[]{:S(2)}, u32[]{:S(2)}) collective-permute-start(bf16[48,8192]{1,0:T(8,128)(2,1)S(1)} %get-tuple-element.42), channel_id=1, source_target_pairs={{0,1},{1,0},{2,3},{3,2},{4,5},{5,4},{6,7},{7,6},{8,9},{9,8},{10,11... | collective-permute-start | bytes 2359304 | tf_op jit(solution)/shard_map/ppermute | solution.py:352
  35.9 3.0 %collective-permute-start.9 = (bf16[48,2048]{1,0:T(8,128)(2,1)S(1)}, bf16[48,2048]{1,0:T(8,128)(2,1)S(1)}, u32[]{:S(2)}, u32[]{:S(2)}) collective-permute-start(bf16[48,2048]{1,0:T(8,128)(2,1)S(1)} %get-tuple-element.44), channel_id=1, source_target_pairs={{0,1},{1,0},{2,3},{3,2},{4,5},{5,4},{6,7},{7,6},{8,9},{9,8},{10,11... | collective-permute-start | bytes 589832 | tf_op jit(solution)/shard_map/ppermute | solution.py:352
  37.0 3.6 %collective-permute-start.13 = (bf16[48,2560]{1,0:T(8,128)(2,1)S(1)}, bf16[48,2560]{1,0:T(8,128)(2,1)S(1)}, u32[]{:S(2)}, u32[]{:S(2)}) collective-permute-start(bf16[48,2560]{1,0:T(8,128)(2,1)S(1)} %get-tuple-element.48), channel_id=1, source_target_pairs={{0,1},{1,0},{2,3},{3,2},{4,5},{5,4},{6,7},{7,6},{8,9},{9,8},{10,11... | collective-permute-start | bytes 737288 | tf_op jit(solution)/shard_map/ppermute | solution.py:352
  38.3 3.0 %collective-permute-start.15 = (bf16[48,1792]{1,0:T(8,128)(2,1)S(1)}, bf16[48,1792]{1,0:T(8,128)(2,1)S(1)}, u32[]{:S(2)}, u32[]{:S(2)}) collective-permute-start(bf16[48,1792]{1,0:T(8,128)(2,1)S(1)} %get-tuple-element.50), channel_id=1, source_target_pairs={{0,1},{1,0},{2,3},{3,2},{4,5},{5,4},{6,7},{7,6},{8,9},{9,8},{10,11... | collective-permute-start | bytes 516104 | tf_op jit(solution)/shard_map/ppermute | solution.py:352
  38.4 7.3 %collective-permute-start.12 = (bf16[48,1792]{1,0:T(8,128)(2,1)S(1)}, bf16[48,1792]{1,0:T(8,128)(2,1)S(1)}, u32[]{:S(2)}, u32[]{:S(2)}) collective-permute-start(bf16[48,1792]{1,0:T(8,128)(2,1)S(1)} %add_convert_fusion.3), channel_id=1, source_target_pairs={{0,2},{1,3},{2,0},{3,1},{4,6},{5,7},{6,4},{7,5},{8,10},{9,11},{10,... | collective-permute-start | bytes 516104 | tf_op jit(solution)/shard_map/ppermute | solution.py:448
  39.0 20.3 %collective-permute-start.10 = (bf16[48,2048]{1,0:T(8,128)(2,1)S(1)}, bf16[48,2048]{1,0:T(8,128)(2,1)S(1)}, u32[]{:S(2)}, u32[]{:S(2)}) collective-permute-start(bf16[48,2048]{1,0:T(8,128)(2,1)S(1)} %add_convert_fusion.1), channel_id=1, source_target_pairs={{0,2},{1,3},{2,0},{3,1},{4,6},{5,7},{6,4},{7,5},{8,10},{9,11},{10,... | collective-permute-start | bytes 589832 | tf_op jit(solution)/shard_map/ppermute | solution.py:448
  40.7 17.7 %collective-permute-start.14 = (bf16[48,2560]{1,0:T(8,128)(2,1)S(1)}, bf16[48,2560]{1,0:T(8,128)(2,1)S(1)}, u32[]{:S(2)}, u32[]{:S(2)}) collective-permute-start(bf16[48,2560]{1,0:T(8,128)(2,1)S(1)} %add_convert_fusion), channel_id=1, source_target_pairs={{0,2},{1,3},{2,0},{3,1},{4,6},{5,7},{6,4},{7,5},{8,10},{9,11},{10,... | collective-permute-start | bytes 737288 | tf_op jit(solution)/shard_map/ppermute | solution.py:448
  41.3 17.1 %collective-permute-start.16 = (bf16[48,1792]{1,0:T(8,128)(2,1)S(1)}, bf16[48,1792]{1,0:T(8,128)(2,1)S(1)}, u32[]{:S(2)}, u32[]{:S(2)}) collective-permute-start(bf16[48,1792]{1,0:T(8,128)(2,1)S(1)} %add_convert_fusion.2), channel_id=1, source_target_pairs={{0,2},{1,3},{2,0},{3,1},{4,6},{5,7},{6,4},{7,5},{8,10},{9,11},{10,... | collective-permute-start | bytes 516104 | tf_op jit(solution)/shard_map/ppermute | solution.py:448

commit v7 on v6

--- a/solution.py
+++ b/solution.py
@@ -143,13 +143,16 @@
     )
 
 
+def with_ones(values):
+    return jnp.concatenate([values, jnp.ones_like(values)], axis=1)
+
+
 def early_kernel(kv_local, group, count, step, *refs):
     q_ref, docs_ref = refs[:2]
     blocks = refs[2 : 2 + count]
     acc_ref, top_ref, sum_ref = refs[2 + count : 5 + count]
     bias_ref, s_ref, p_ref = refs[5 + count :]
     tokens = q_ref.shape[0]
-    stacked = group * tokens
     me = lax.axis_index("seq")
     row, col = me // 2, me % 2
     docs = []
@@ -161,25 +164,42 @@
     query_at = lax.broadcasted_iota(jnp.int32, (tokens, count * tokens), 0)
     allowed = allowed & ((key_at <= query_at) | (key_at >= tokens))
     bias_ref[...] = jnp.where(allowed, 0.0, -jnp.inf)
+    keys, values = [], []
     for h in range(kv_local):
-        cols = pl.ds(2 * h * HD, HD)
-        keys = jnp.concatenate([b[:, cols] for b in blocks], axis=0)
-        s_ref[...] = scores_of(stack(q_ref, h, group), keys)
-        for r in range(0, stacked, step):
+        at = pl.ds(2 * h * HD, HD)
+        keys.append(jnp.concatenate([b[:, at] for b in blocks], axis=0))
+        at = pl.ds((2 * h + 1) * HD, HD)
+        values.append(with_ones(jnp.concatenate([b[:, at] for b in blocks], axis=0)))
+
+    def score(head):
+        s_ref[head] = scores_of(q_ref[:, pl.ds(head * HD, HD)], keys[head // group])
+
+    def soften(head):
+        for r in range(0, tokens, step):
             at = pl.ds(r, step)
-            into = pl.ds(h * stacked + r, step)
-            scores = s_ref[at, :] * SCALE + bias_ref[pl.ds(r % tokens, step), :]
+            scores = s_ref[head, at, :] * SCALE + bias_ref[at, :]
             top = jnp.max(scores, axis=-1, keepdims=True)
-            weight = jnp.exp2(scores - top)
-            total = jnp.sum(weight, axis=-1, keepdims=True)
-            p_ref[at, :] = weight.astype(jnp.bfloat16)
+            p_ref[head, at, :] = jnp.exp2(scores - top).astype(jnp.bfloat16)
+            into = pl.ds(head * tokens + r, step)
             top_ref[into, :] = jnp.broadcast_to(top, (step, HD))
-            sum_ref[into, :] = jnp.broadcast_to(total, (step, HD))
-        cols = pl.ds((2 * h + 1) * HD, HD)
-        values = jnp.concatenate([b[:, cols] for b in blocks], axis=0)
-        acc_ref[pl.ds(h * stacked, stacked), :] = jnp.dot(
-            p_ref[...], values, preferred_element_type=jnp.float32
+
+    def add_up(head):
+        both = jnp.dot(
+            p_ref[head], values[head // group], preferred_element_type=jnp.float32
         )
+        into = pl.ds(head * tokens, tokens)
+        acc_ref[into, :] = both[:, :HD]
+        sum_ref[into, :] = both[:, HD:]
+
+    heads = kv_local * group
+    score(0)
+    for head in range(heads):
+        if head + 1 < heads:
+            score(head + 1)
+        soften(head)
+        if head:
+            add_up(head - 1)
+    add_up(heads - 1)
 
 
 def project(context_ref, first, w_ref, send_ref, keep_ref, part, top=0, more_ref=None):
@@ -221,11 +241,13 @@
     new = jnp.maximum(old[:, :1], jnp.max(scores, axis=-1, keepdims=True))
     weight = jnp.exp2(scores - new)
     rescale = jnp.exp2(old - new)
-    total = sum_ref[at, :] * rescale + jnp.sum(weight, axis=-1, keepdims=True)
     added = jnp.dot(
-        weight.astype(jnp.bfloat16), values, preferred_element_type=jnp.float32
-    )
-    context = (acc_ref[at, :] * rescale + added) / total
+        weight.astype(jnp.bfloat16),
+        with_ones(values),
+        preferred_element_type=jnp.float32,
+    )
+    total = sum_ref[at, :] * rescale + added[:, HD:]
+    context = (acc_ref[at, :] * rescale + added[:, :HD]) / total
     context = context.astype(jnp.bfloat16)
     for g in range(group):
         rows = context[g * tokens : (g + 1) * tokens]
@@ -389,14 +411,14 @@
     stacked = group * tokens
     state = jax.ShapeDtypeStruct((kv_local * stacked, HD), jnp.float32)
     early = pl.pallas_call(
-        functools.partial(early_kernel, kv_local, group, count, 32),
+        functools.partial(early_kernel, kv_local, group, count, 64),
         out_shape=(state, state, state),
         in_specs=[VMEM] * (2 + count),
         out_specs=(VMEM,) * 3,
         scratch_shapes=[
             pltpu.VMEM((tokens, count * tokens), jnp.float32),
-            pltpu.VMEM((stacked, count * tokens), jnp.float32),
-            pltpu.VMEM((stacked, count * tokens), jnp.bfloat16),
+            pltpu.VMEM((kv_local * group, tokens, count * tokens), jnp.float32),
+            pltpu.VMEM((kv_local * group, tokens, count * tokens), jnp.bfloat16),
         ],
         cost_estimate=pl.CostEstimate(
             flops=4 * tokens * tokens * count * width,

time: 60.3 us -> 59.2 us (0.982)
  the two profiles are of different devices: /device:TPU:22 before, /device:TPU:16 now
where the time goes in v7:
time: 59.2 us; the launch traced here: 59 us
  waiting for transfers between devices  23.7 us (40%)
  Pallas kernels  21.3 us (36%)
  starting transfers between devices  12.7 us (21%)
  other arithmetic  0.94 us (2%)
    ppermute x4, waiting for transfers between devices, layer(): block = lax.ppermute(moved[at:at + part], AXES, y_route(seq, tp, distance))  15.5 us
    ppermute x11, waiting for transfers between devices, send(): return lax.ppermute(x, AXES, route[name, step])  8.19 us
    pallas_call x3, Pallas kernels, load_call(): pl.pallas_call(functools.partial(load_kernel, cuts[0]), out_shape=[pltpu....  7.99 us
    ppermute x11, starting transfers between devices, send(): return lax.ppermute(x, AXES, route[name, step])  6.33 us
    pallas_call x4, Pallas kernels, project_call(): pl.pallas_call(functools.partial(project_kernel, part, first), out_shape=...  5.24 us
    ppermute x4, starting transfers between devices, layer(): block = lax.ppermute(moved[at:at + part], AXES, y_route(seq, tp, distance))  4.31 us
    pallas_call x2, Pallas kernels, layer(): pl.pallas_call(functools.partial(late_kernel, h, kv_local, group, part, d...  2.85 us
    pallas_call x1, Pallas kernels, layer(): acc, top, total = early(query_rows, docs, *blocks)  2.62 us
  transfers between devices with their start and end apart: 17, of which 6 were waited for; matrix products, arithmetic and copies ran while one was open for 2% of the time, Pallas kernels for 31%

profile of v7, /device:TPU:16, one launch (start us, length us, event | category | flops | bytes accessed | tf_op | source)
XLA Modules:
  0.0 59.0 jit_solution(13326893751778936593)
XLA Ops:
  0.0 0.9 %join.1.refs_2_ = bf16[192,512]{1,0:T(8,128)(2,1)S(1)} custom-call(bf16[192,256]{1,0:T(8,128)(2,1)} %k_ref.1, bf16[192,256]{1,0:T(8,128)(2,1)} %v_ref.1), custom_call_target="tpu_custom_call" | custom-call | tf_op jit(solution)/shard_map/join/pallas_call | solution.py:376
  0.9 1.6 %collective-permute-start = (bf16[192,512]{1,0:T(8,128)(2,1)S(1)}, bf16[192,512]{1,0:T(8,128)(2,1)S(1)}, u32[]{:S(2)}, u32[]{:S(2)}) collective-permute-start(bf16[192,512]{1,0:T(8,128)(2,1)S(1)} %join.1.refs_2_), channel_id=1, source_target_pairs={{0,8},{1,9},{2,10},{3,11},{4,12},{5,13},{6,14},{7,15},{8,0},{9,1},... | collective-permute-start | bytes 589832 | tf_op jit(solution)/shard_map/ppermute | solution.py:374
  2.6 0.0 collective-permute-start.1
  2.6 1.5 %collective-permute-start.5 = (bf16[192,512]{1,0:T(8,128)(2,1)S(1)}, bf16[192,512]{1,0:T(8,128)(2,1)S(1)}, u32[]{:S(2)}, u32[]{:S(2)}) collective-permute-start(bf16[192,512]{1,0:T(8,128)(2,1)S(1)} %join.1.refs_2_), channel_id=1, source_target_pairs={{0,4},{1,5},{2,6},{3,7},{4,0},{5,1},{6,2},{7,3},{8,12},{9,13},{10,... | collective-permute-start | bytes 589832 | tf_op jit(solution)/shard_map/ppermute | solution.py:374
  4.0 0.7 %convert_element_type.39 = f32[1536]{0:T(1024)S(1)} convert(s32[1536]{0:T(1024)} %param.8) | non-fusion elementwise | flops 1536 | bytes 12288 | tf_op jit(solution)/shard_map/convert_element_type | solution.py:385
  4.7 0.1 reshape.3.refs_1_
  4.8 2.8 %collective-permute-done = bf16[192,512]{1,0:T(8,128)(2,1)S(1)} collective-permute-done((bf16[192,512]{1,0:T(8,128)(2,1)S(1)}, bf16[192,512]{1,0:T(8,128)(2,1)S(1)}, u32[]{:S(2)}, u32[]{:S(2)}) %collective-permute-start) | collective-permute-done | bytes 196640 | tf_op jit(solution)/shard_map/ppermute | solution.py:374
  7.6 1.3 %collective-permute-done.1 = bf16[192,512]{1,0:T(8,128)(2,1)S(1)} collective-permute-done((bf16[192,512]{1,0:T(8,128)(2,1)S(1)}, bf16[192,512]{1,0:T(8,128)(2,1)S(1)}, u32[]{:S(2)}, u32[]{:S(2)}) %collective-permute-start.1) | collective-permute-done | bytes 196640 | tf_op jit(solution)/shard_map/ppermute | solution.py:374
  8.9 0.3 collective-permute-start.2
  9.2 0.0 collective-permute-start.3
  9.2 1.6 %collective-permute-start.6 = (bf16[192,512]{1,0:T(8,128)(2,1)S(1)}, bf16[192,512]{1,0:T(8,128)(2,1)S(1)}, u32[]{:S(2)}, u32[]{:S(2)}) collective-permute-start(bf16[192,512]{1,0:T(8,128)(2,1)S(1)} %broadcast_select_fusion.refs_4_), channel_id=1, source_target_pairs={{0,1},{1,0},{2,3},{3,2},{4,5},{5,4},{6,7},{7,6},{8,12},{9,13},{10,... | collective-permute-start | bytes 589832 | tf_op jit(solution)/shard_map/ppermute | solution.py:374
  10.8 3.8 %collective-permute-done.2 = bf16[192,512]{1,0:T(8,128)(2,1)S(1)} collective-permute-done((bf16[192,512]{1,0:T(8,128)(2,1)S(1)}, bf16[192,512]{1,0:T(8,128)(2,1)S(1)}, u32[]{:S(2)}, u32[]{:S(2)}) %collective-permute-start.2) | collective-permute-done | bytes 196640 | tf_op jit(solution)/shard_map/ppermute | solution.py:374
  14.6 0.3 collective-permute-done.3
  14.9 1.6 %collective-permute-start.7 = (bf16[192,256]{1,0:T(8,128)(2,1)S(1)}, bf16[192,256]{1,0:T(8,128)(2,1)S(1)}, u32[]{:S(2)}, u32[]{:S(2)}) collective-permute-start(bf16[192,256]{1,0:T(8,128)(2,1)S(1)} %get-tuple-element.51), channel_id=1, source_target_pairs={{0,1},{1,0},{2,3},{3,2},{4,5},{5,4},{6,7},{7,6},{8,9},{9,8},{10,11... | collective-permute-start | bytes 294920 | tf_op jit(solution)/shard_map/ppermute | solution.py:408
  16.5 0.5 collective-permute-start.4
  17.0 2.9 %load.3 = (bf16[1024,1792]{1,0:T(8,128)(2,1)S(1)}, bf16[1024,1280]{1,0:T(8,128)(2,1)S(1)}) custom-call(bf16[1024,8192]{1,0:T(8,128)(2,1)} %w_hbm.5), custom_call_target="tpu_custom_call" | custom-call | bytes 6291456 | tf_op jit(solution)/shard_map/load/pallas_call | solution.py:96
  19.9 2.9 %load.4 = (bf16[1024,1280]{1,0:T(8,128)(2,1)S(1)}, bf16[1024,1792]{1,0:T(8,128)(2,1)S(1)}) custom-call(bf16[1024,8192]{1,0:T(8,128)(2,1)} %w_hbm.5), custom_call_target="tpu_custom_call" | custom-call | bytes 6291456 | tf_op jit(solution)/shard_map/load/pallas_call | solution.py:96
  22.8 0.0 copy-start
  22.8 2.2 %load.5.refs_4_.refs_0_ = bf16[1024,2048]{1,0:T(8,128)(2,1)S(1)} custom-call(bf16[1024,8192]{1,0:T(8,128)(2,1)} %w_hbm.5), custom_call_target="tpu_custom_call" | custom-call | bytes 4194304 | tf_op jit(solution)/shard_map/load/pallas_call | solution.py:96
  25.0 0.0 collective-permute-done.5.refs_3_
  25.0 0.0 collective-permute-done.6.refs_5_
  25.1 2.6 %attend_early.1 = (f32[1536,128]{1,0:T(8,128)S(1)}, f32[1536,128]{1,0:T(8,128)S(1)}, f32[1536,128]{1,0:T(8,128)S(1)}) custom-call(bf16[192,1024]{1,0:T(8,128)(2,1)S(1)} %copy-done, f32[8,192]{1,0:T(8,128)S(1)} %reshape.3.refs_1_, bf16[192,512]{1,0:T(8,128)(2,1)S(1)} %join.1.refs_2_, bf16[192,512]{1,0:T(8,128)(2,1)S(1)} %collective-permute-done.5.refs_3_, ...), custom_call_target="tpu_custom_call" | custom-call | flops 754974720 | bytes 786432 | tf_op jit(solution)/shard_map/attend_early/pallas_call | solution.py:431
  27.7 0.0 collective-permute-done.7.refs_2_
  27.7 1.4 %attend_late.2 = (f32[96,1792]{1,0:T(8,128)S(1)}, bf16[192,512]{1,0:T(8,128)(2,1)S(1)}) custom-call(bf16[192,1024]{1,0:T(8,128)(2,1)S(1)} %copy-done, f32[8,192]{1,0:T(8,128)S(1)} %reshape.3.refs_1_, bf16[192,256]{1,0:T(8,128)(2,1)S(1)} %collective-permute-done.7.refs_2_, f32[1536,128]{1,0:T(8,128)S(1)} %get-tuple-element.31.refs_3_, ...), custom_call_target="tpu_custom_call" | custom-call | flops 251658240 | bytes 2228224 | tf_op jit(solution)/shard_map/attend_late/pallas_call | solution.py:444
  29.1 1.4 %attend_late.3 = (bf16[48,1792]{1,0:T(8,128)(2,1)S(1)}, bf16[48,1792]{1,0:T(8,128)(2,1)S(1)}, bf16[192,1024]{1,0:T(8,128)(2,1)S(1)}) custom-call(bf16[192,1024]{1,0:T(8,128)(2,1)S(1)} %copy-done, f32[8,192]{1,0:T(8,128)S(1)} %reshape.3.refs_1_, bf16[192,256]{1,0:T(8,128)(2,1)S(1)} %collective-permute-done.4.refs_2_, ...), custom_call_target="tpu_custom_call" | custom-call | flops 251658240 | bytes 2228224 | tf_op jit(solution)/shard_map/attend_late/pallas_call | solution.py:444
  30.6 0.1 collective-permute-start.11
  30.7 2.8 %project_rest.4 = (bf16[48,8192]{1,0:T(8,128)(2,1)S(1)}, bf16[48,8192]{1,0:T(8,128)(2,1)S(1)}) custom-call(bf16[192,1024]{1,0:T(8,128)(2,1)S(1)} %get-tuple-element.37.context_ref, bf16[1024,1792]{1,0:T(8,128)(2,1)S(1)} %get-tuple-element.34.refs_6_.refs_0_, bf16[1024,1280]{1,0:T(8,128)(2,1)S(1)} %get-tuple-element.38.refs_1_.refs_0_, ...), custom_call_target="tpu_custom_call" | custom-call | flops 1610612736 | bytes 16777216 | tf_op jit(solution)/shard_map/project_rest/pallas_call | solution.py:299
  33.4 0.6 collective-permute-start.8
  34.0 0.8 %project_rest.5 = (bf16[48,2048]{1,0:T(8,128)(2,1)S(1)}, bf16[48,2048]{1,0:T(8,128)(2,1)S(1)}) custom-call(bf16[192,1024]{1,0:T(8,128)(2,1)S(1)} %get-tuple-element.37.context_ref, bf16[1024,2048]{1,0:T(8,128)(2,1)S(1)} %load.5.refs_4_.refs_0_), custom_call_target="tpu_custom_call" | custom-call | flops 402653184 | bytes 4194304 | tf_op jit(solution)/shard_map/project_rest/pallas_call | solution.py:299
  34.8 0.1 collective-permute-start.9
  34.9 1.0 %project_rest.6 = (bf16[48,2560]{1,0:T(8,128)(2,1)S(1)}, bf16[48,2560]{1,0:T(8,128)(2,1)S(1)}) custom-call(bf16[192,1024]{1,0:T(8,128)(2,1)S(1)} %get-tuple-element.37.context_ref, bf16[1024,1280]{1,0:T(8,128)(2,1)S(1)} %get-tuple-element.38.refs_1_.refs_0_, bf16[1024,1280]{1,0:T(8,128)(2,1)S(1)} %get-tuple-element.39.refs_2_.refs_1_), custom_call_target="tpu_custom_call" | custom-call | flops 503316480 | bytes 5242880 | tf_op jit(solution)/shard_map/project_rest/pallas_call | solution.py:299
  35.8 0.6 collective-permute-start.13
  36.4 0.7 %project_rest.7 = (bf16[48,1792]{1,0:T(8,128)(2,1)S(1)}, bf16[48,1792]{1,0:T(8,128)(2,1)S(1)}) custom-call(bf16[192,1024]{1,0:T(8,128)(2,1)S(1)} %get-tuple-element.37.context_ref, bf16[1024,1792]{1,0:T(8,128)(2,1)S(1)} %get-tuple-element.40.refs_3_.refs_0_), custom_call_target="tpu_custom_call" | custom-call | flops 352321536 | bytes 3670016 | tf_op jit(solution)/shard_map/project_rest/pallas_call | solution.py:299
  37.1 0.1 collective-permute-start.15
  37.2 1.6 %collective-permute-start.12 = (bf16[48,1792]{1,0:T(8,128)(2,1)S(1)}, bf16[48,1792]{1,0:T(8,128)(2,1)S(1)}, u32[]{:S(2)}, u32[]{:S(2)}) collective-permute-start(bf16[48,1792]{1,0:T(8,128)(2,1)S(1)} %add_convert_fusion.3), channel_id=1, source_target_pairs={{0,2},{1,3},{2,0},{3,1},{4,6},{5,7},{6,4},{7,5},{8,10},{9,11},{10,... | collective-permute-start | bytes 516104 | tf_op jit(solution)/shard_map/ppermute | solution.py:470
  38.8 0.0 collective-permute-done.9
  38.8 0.1 add_convert_fusion.1
  38.9 0.6 collective-permute-start.10
  39.5 0.1 add_convert_fusion
  39.5 1.6 %collective-permute-start.14 = (bf16[48,2560]{1,0:T(8,128)(2,1)S(1)}, bf16[48,2560]{1,0:T(8,128)(2,1)S(1)}, u32[]{:S(2)}, u32[]{:S(2)}) collective-permute-start(bf16[48,2560]{1,0:T(8,128)(2,1)S(1)} %add_convert_fusion), channel_id=1, source_target_pairs={{0,2},{1,3},{2,0},{3,1},{4,6},{5,7},{6,4},{7,5},{8,10},{9,11},{10,... | collective-permute-start | bytes 737288 | tf_op jit(solution)/shard_map/ppermute | solution.py:470
  41.2 0.6 collective-permute-start.16
  41.7 2.8 %collective-permute-done.12.refs_0_ = bf16[48,1792]{1,0:T(8,128)(2,1)S(1)} collective-permute-done((bf16[48,1792]{1,0:T(8,128)(2,1)S(1)}, bf16[48,1792]{1,0:T(8,128)(2,1)S(1)}, u32[]{:S(2)}, u32[]{:S(2)}) %collective-permute-start.12) | collective-permute-done | bytes 172064 | tf_op jit(solution)/shard_map/ppermute | solution.py:470
  44.6 12.7 %collective-permute-done.16.refs_2_ = bf16[48,1792]{1,0:T(8,128)(2,1)S(1)} collective-permute-done((bf16[48,1792]{1,0:T(8,128)(2,1)S(1)}, bf16[48,1792]{1,0:T(8,128)(2,1)S(1)}, u32[]{:S(2)}, u32[]{:S(2)}) %collective-permute-start.16) | collective-permute-done | bytes 172064 | tf_op jit(solution)/shard_map/ppermute | solution.py:470
  57.2 0.0 collective-permute-done.14.refs_1_
  57.2 0.0 collective-permute-done.8.received_ref
  57.3 0.9 %finish.2.refs_1_ = bf16[48,8192]{1,0:T(8,128)(2,1)} custom-call(bf16[48,8192]{1,0:T(8,128)(2,1)S(1)} %get-tuple-element.41.kept_ref, bf16[48,8192]{1,0:T(8,128)(2,1)S(1)} %collective-permute-done.8.received_ref, bf16[48,1792]{1,0:T(8,128)(2,1)S(1)} %collective-permute-done.12.refs_0_, bf16[48,2560]{1,0:T(8,128)(2,1)S(1)} %collective-permute-done.14.refs_1_, ...), custom_call_target="tpu_custom_call" | custom-call | flops 1572864 | bytes 1572864 | tf_op jit(solution)/shard_map/finish/pallas_call | solution.py:343
  58.2 0.0 collective-permute-done.10.refs_0_
  58.2 0.8 %finish.3 = bf16[48,8192]{1,0:T(8,128)(2,1)} custom-call(bf16[48,8192]{1,0:T(8,128)(2,1)S(1)} %get-tuple-element.41.kept_ref, bf16[48,8192]{1,0:T(8,128)(2,1)S(1)} %collective-permute-done.8.received_ref, bf16[48,2048]{1,0:T(8,128)(2,1)S(1)} %collective-permute-done.10.refs_0_, bf16[48,8192]{1,0:T(8,128)(2,1)} %finish.2.refs_1_), custom_call_target="tpu_custom_call", output_to_operand_aliasing={{}: (3, {})} | custom-call | flops 1572864 | bytes 1572864 | tf_op jit(solution)/shard_map/finish/pallas_call | solution.py:343
  (10 shorter events, 0.2 us)
Async XLA Ops:
  0.9 6.7 %collective-permute-start = (bf16[192,512]{1,0:T(8,128)(2,1)S(1)}, bf16[192,512]{1,0:T(8,128)(2,1)S(1)}, u32[]{:S(2)}, u32[]{:S(2)}) collective-permute-start(bf16[192,512]{1,0:T(8,128)(2,1)S(1)} %join.1.refs_2_), channel_id=1, source_target_pairs={{0,8},{1,9},{2,10},{3,11},{4,12},{5,13},{6,14},{7,15},{8,0},{9,1},... | collective-permute-start | bytes 589832 | tf_op jit(solution)/shard_map/ppermute | solution.py:374
  2.6 6.4 %collective-permute-start.1 = (bf16[192,512]{1,0:T(8,128)(2,1)S(1)}, bf16[192,512]{1,0:T(8,128)(2,1)S(1)}, u32[]{:S(2)}, u32[]{:S(2)}) collective-permute-start(bf16[192,512]{1,0:T(8,128)(2,1)S(1)} %join.1.refs_2_), channel_id=1, source_target_pairs={{0,1},{1,0},{2,3},{3,2},{4,5},{5,4},{6,7},{7,6},{8,16},{9,17},{10,... | collective-permute-start | bytes 589832 | tf_op jit(solution)/shard_map/ppermute | solution.py:374
  2.6 22.5 %collective-permute-start.5 = (bf16[192,512]{1,0:T(8,128)(2,1)S(1)}, bf16[192,512]{1,0:T(8,128)(2,1)S(1)}, u32[]{:S(2)}, u32[]{:S(2)}) collective-permute-start(bf16[192,512]{1,0:T(8,128)(2,1)S(1)} %join.1.refs_2_), channel_id=1, source_target_pairs={{0,4},{1,5},{2,6},{3,7},{4,0},{5,1},{6,2},{7,3},{8,12},{9,13},{10,... | collective-permute-start | bytes 589832 | tf_op jit(solution)/shard_map/ppermute | solution.py:374
  8.9 5.7 %collective-permute-start.2 = (bf16[192,512]{1,0:T(8,128)(2,1)S(1)}, bf16[192,512]{1,0:T(8,128)(2,1)S(1)}, u32[]{:S(2)}, u32[]{:S(2)}) collective-permute-start(bf16[192,512]{1,0:T(8,128)(2,1)S(1)} %collective-permute-done.1), channel_id=1, source_target_pairs={{0,1},{1,0},{2,3},{3,2},{4,5},{5,4},{6,7},{7,6},{8,9},{9,8},{10,11... | collective-permute-start | bytes 589832 | tf_op jit(solution)/shard_map/ppermute | solution.py:374
  9.2 5.7 %collective-permute-start.3 = (bf16[192,512]{1,0:T(8,128)(2,1)S(1)}, bf16[192,512]{1,0:T(8,128)(2,1)S(1)}, u32[]{:S(2)}, u32[]{:S(2)}) collective-permute-start(bf16[192,512]{1,0:T(8,128)(2,1)S(1)} %collective-permute-done), channel_id=1, source_target_pairs={{0,1},{1,0},{2,3},{3,2},{4,5},{5,4},{6,7},{7,6},{8,16},{9,17},{10,... | collective-permute-start | bytes 589832 | tf_op jit(solution)/shard_map/ppermute | solution.py:374
  9.2 15.8 %collective-permute-start.6 = (bf16[192,512]{1,0:T(8,128)(2,1)S(1)}, bf16[192,512]{1,0:T(8,128)(2,1)S(1)}, u32[]{:S(2)}, u32[]{:S(2)}) collective-permute-start(bf16[192,512]{1,0:T(8,128)(2,1)S(1)} %broadcast_select_fusion.refs_4_), channel_id=1, source_target_pairs={{0,1},{1,0},{2,3},{3,2},{4,5},{5,4},{6,7},{7,6},{8,12},{9,13},{10,... | collective-permute-start | bytes 589832 | tf_op jit(solution)/shard_map/ppermute | solution.py:374
  14.9 12.8 %collective-permute-start.7 = (bf16[192,256]{1,0:T(8,128)(2,1)S(1)}, bf16[192,256]{1,0:T(8,128)(2,1)S(1)}, u32[]{:S(2)}, u32[]{:S(2)}) collective-permute-start(bf16[192,256]{1,0:T(8,128)(2,1)S(1)} %get-tuple-element.51), channel_id=1, source_target_pairs={{0,1},{1,0},{2,3},{3,2},{4,5},{5,4},{6,7},{7,6},{8,9},{9,8},{10,11... | collective-permute-start | bytes 294920 | tf_op jit(solution)/shard_map/ppermute | solution.py:408
  16.5 12.7 %collective-permute-start.4 = (bf16[192,256]{1,0:T(8,128)(2,1)S(1)}, bf16[192,256]{1,0:T(8,128)(2,1)S(1)}, u32[]{:S(2)}, u32[]{:S(2)}) collective-permute-start(bf16[192,256]{1,0:T(8,128)(2,1)S(1)} %get-tuple-element.52), channel_id=1, source_target_pairs={{0,1},{1,0},{2,3},{3,2},{4,5},{5,4},{6,7},{7,6},{8,9},{9,8},{10,11... | collective-permute-start | bytes 294920 | tf_op jit(solution)/shard_map/ppermute | solution.py:408
  22.8 2.3 %copy-start = (bf16[192,1024]{1,0:T(8,128)(2,1)S(1)}, bf16[192,1024]{1,0:T(8,128)(2,1)}, u32[]{:S(2)}) copy-start(bf16[192,1024]{1,0:T(8,128)(2,1)} %refs_0_.5) | copy-start | bytes 1179652
  30.6 6.6 %collective-permute-start.11 = (bf16[48,1792]{1,0:T(8,128)(2,1)S(1)}, bf16[48,1792]{1,0:T(8,128)(2,1)S(1)}, u32[]{:S(2)}, u32[]{:S(2)}) collective-permute-start(bf16[48,1792]{1,0:T(8,128)(2,1)S(1)} %get-tuple-element.46), channel_id=1, source_target_pairs={{0,1},{1,0},{2,3},{3,2},{4,5},{5,4},{6,7},{7,6},{8,9},{9,8},{10,11... | collective-permute-start | bytes 516104 | tf_op jit(solution)/shard_map/ppermute | solution.py:374
  33.4 23.8 %collective-permute-start.8 = (bf16[48,8192]{1,0:T(8,128)(2,1)S(1)}, bf16[48,8192]{1,0:T(8,128)(2,1)S(1)}, u32[]{:S(2)}, u32[]{:S(2)}) collective-permute-start(bf16[48,8192]{1,0:T(8,128)(2,1)S(1)} %get-tuple-element.42), channel_id=1, source_target_pairs={{0,1},{1,0},{2,3},{3,2},{4,5},{5,4},{6,7},{7,6},{8,9},{9,8},{10,11... | collective-permute-start | bytes 2359304 | tf_op jit(solution)/shard_map/ppermute | solution.py:374
  34.8 4.0 %collective-permute-start.9 = (bf16[48,2048]{1,0:T(8,128)(2,1)S(1)}, bf16[48,2048]{1,0:T(8,128)(2,1)S(1)}, u32[]{:S(2)}, u32[]{:S(2)}) collective-permute-start(bf16[48,2048]{1,0:T(8,128)(2,1)S(1)} %get-tuple-element.44), channel_id=1, source_target_pairs={{0,1},{1,0},{2,3},{3,2},{4,5},{5,4},{6,7},{7,6},{8,9},{9,8},{10,11... | collective-permute-start | bytes 589832 | tf_op jit(solution)/shard_map/ppermute | solution.py:374
  35.8 3.6 %collective-permute-start.13 = (bf16[48,2560]{1,0:T(8,128)(2,1)S(1)}, bf16[48,2560]{1,0:T(8,128)(2,1)S(1)}, u32[]{:S(2)}, u32[]{:S(2)}) collective-permute-start(bf16[48,2560]{1,0:T(8,128)(2,1)S(1)} %get-tuple-element.48), channel_id=1, source_target_pairs={{0,1},{1,0},{2,3},{3,2},{4,5},{5,4},{6,7},{7,6},{8,9},{9,8},{10,11... | collective-permute-start | bytes 737288 | tf_op jit(solution)/shard_map/ppermute | solution.py:374
  37.1 4.0 %collective-permute-start.15 = (bf16[48,1792]{1,0:T(8,128)(2,1)S(1)}, bf16[48,1792]{1,0:T(8,128)(2,1)S(1)}, u32[]{:S(2)}, u32[]{:S(2)}) collective-permute-start(bf16[48,1792]{1,0:T(8,128)(2,1)S(1)} %get-tuple-element.50), channel_id=1, source_target_pairs={{0,1},{1,0},{2,3},{3,2},{4,5},{5,4},{6,7},{7,6},{8,9},{9,8},{10,11... | collective-permute-start | bytes 516104 | tf_op jit(solution)/shard_map/ppermute | solution.py:374
  37.2 7.3 %collective-permute-start.12 = (bf16[48,1792]{1,0:T(8,128)(2,1)S(1)}, bf16[48,1792]{1,0:T(8,128)(2,1)S(1)}, u32[]{:S(2)}, u32[]{:S(2)}) collective-permute-start(bf16[48,1792]{1,0:T(8,128)(2,1)S(1)} %add_convert_fusion.3), channel_id=1, source_target_pairs={{0,2},{1,3},{2,0},{3,1},{4,6},{5,7},{6,4},{7,5},{8,10},{9,11},{10,... | collective-permute-start | bytes 516104 | tf_op jit(solution)/shard_map/ppermute | solution.py:470
  38.9 19.3 %collective-permute-start.10 = (bf16[48,2048]{1,0:T(8,128)(2,1)S(1)}, bf16[48,2048]{1,0:T(8,128)(2,1)S(1)}, u32[]{:S(2)}, u32[]{:S(2)}) collective-permute-start(bf16[48,2048]{1,0:T(8,128)(2,1)S(1)} %add_convert_fusion.1), channel_id=1, source_target_pairs={{0,2},{1,3},{2,0},{3,1},{4,6},{5,7},{6,4},{7,5},{8,10},{9,11},{10,... | collective-permute-start | bytes 589832 | tf_op jit(solution)/shard_map/ppermute | solution.py:470
  39.5 17.7 %collective-permute-start.14 = (bf16[48,2560]{1,0:T(8,128)(2,1)S(1)}, bf16[48,2560]{1,0:T(8,128)(2,1)S(1)}, u32[]{:S(2)}, u32[]{:S(2)}) collective-permute-start(bf16[48,2560]{1,0:T(8,128)(2,1)S(1)} %add_convert_fusion), channel_id=1, source_target_pairs={{0,2},{1,3},{2,0},{3,1},{4,6},{5,7},{6,4},{7,5},{8,10},{9,11},{10,... | collective-permute-start | bytes 737288 | tf_op jit(solution)/shard_map/ppermute | solution.py:470
  41.2 16.1 %collective-permute-start.16 = (bf16[48,1792]{1,0:T(8,128)(2,1)S(1)}, bf16[48,1792]{1,0:T(8,128)(2,1)S(1)}, u32[]{:S(2)}, u32[]{:S(2)}) collective-permute-start(bf16[48,1792]{1,0:T(8,128)(2,1)S(1)} %add_convert_fusion.2), channel_id=1, source_target_pairs={{0,2},{1,3},{2,0},{3,1},{4,6},{5,7},{6,4},{7,5},{8,10},{9,11},{10,... | collective-permute-start | bytes 516104 | tf_op jit(solution)/shard_map/ppermute | solution.py:470

commit v8 on v7

--- a/solution.py
+++ b/solution.py
@@ -17,7 +17,7 @@
 VMEM = pl.BlockSpec(memory_space=pltpu.VMEM)
 ANY = pl.BlockSpec(memory_space=pl.ANY)
 MIB = 1 << 20
-CUTS = (7, 17, 24, 32)
+CUTS = (5, 15, 25, 32)
 NEAR = 12
 EARLY, LATE, PROJ = 24, 16, 8
 
@@ -129,12 +129,6 @@
 def key_doc(docs_ref, block, me):
     row = docs_ref[pl.ds(jnp.maximum(block, 0), 1), :]
     return jnp.where((block >= 0) & (block <= me), row, -1.0)
-
-
-def stack(q_ref, h, group):
-    return jnp.concatenate(
-        [q_ref[:, pl.ds((h * group + g) * HD, HD)] for g in range(group)], axis=0
-    )
 
 
 def scores_of(queries, keys):
@@ -221,37 +215,48 @@
             send_ref[into, at] = rows[(2 * i + 1) * part : (2 * i + 2) * part]
 
 
-def late_kernel(h, kv_local, group, part, depth, *refs):
+def late_kernel(h, kv_local, group, part, depth, step, *refs):
     q_ref, docs_ref, block, acc_ref, top_ref, sum_ref, w_ref = refs[:7]
-    context_ref, here_ref = refs[-2:]
-    refs = refs[7:-2]
+    context_ref, here_ref, bias_ref, s_ref, p_ref, rescale_ref = refs[-6:]
+    refs = refs[7:-6]
     tokens = q_ref.shape[0]
-    stacked = group * tokens
     me, rank = lax.axis_index("seq"), lax.axis_index("tp")
     chips = lax.axis_size("tp") // 2
     far = (me // 2 - depth) * 2 + 1 - me % 2
-    bias = jnp.where(
+    bias_ref[...] = jnp.where(
         query_doc(docs_ref, me) == key_doc(docs_ref, far, me), 0.0, -jnp.inf
     )
-    keys, values = block[:, pl.ds(0, HD)], block[:, pl.ds(HD, HD)]
-    scores = scores_of(stack(q_ref, h, group), keys)
-    scores = scores * SCALE + jnp.concatenate([bias] * group, axis=0)
-    at = pl.ds(h * stacked, stacked)
-    old = top_ref[at, :]
-    new = jnp.maximum(old[:, :1], jnp.max(scores, axis=-1, keepdims=True))
-    weight = jnp.exp2(scores - new)
-    rescale = jnp.exp2(old - new)
-    added = jnp.dot(
-        weight.astype(jnp.bfloat16),
-        with_ones(values),
-        preferred_element_type=jnp.float32,
-    )
-    total = sum_ref[at, :] * rescale + added[:, HD:]
-    context = (acc_ref[at, :] * rescale + added[:, :HD]) / total
-    context = context.astype(jnp.bfloat16)
+    keys, values = block[:, pl.ds(0, HD)], with_ones(block[:, pl.ds(HD, HD)])
+
+    def score(g):
+        cols = pl.ds((h * group + g) * HD, HD)
+        s_ref[g] = scores_of(q_ref[:, cols], keys)
+
+    def soften(g):
+        for r in range(0, tokens, step):
+            at = pl.ds(r, step)
+            scores = s_ref[g, at, :] * SCALE + bias_ref[at, :]
+            old = top_ref[pl.ds((h * group + g) * tokens + r, step), :]
+            new = jnp.maximum(old, jnp.max(scores, axis=-1, keepdims=True))
+            p_ref[g, at, :] = jnp.exp2(scores - new[:, :1]).astype(jnp.bfloat16)
+            rescale_ref[g, at, :] = jnp.exp2(old - new)
+
+    def add_up(g):
+        at = pl.ds((h * group + g) * tokens, tokens)
+        added = jnp.dot(p_ref[g], values, preferred_element_type=jnp.float32)
+        rescale = rescale_ref[g]
+        total = sum_ref[at, :] * rescale + added[:, HD:]
+        context = (acc_ref[at, :] * rescale + added[:, :HD]) / total
+        context_ref[:, pl.ds(g * HD, HD)] = context.astype(jnp.bfloat16)
+
+    score(0)
     for g in range(group):
-        rows = context[g * tokens : (g + 1) * tokens]
-        context_ref[:, pl.ds(g * HD, HD)] = rows
+        if g + 1 < group:
+            score(g + 1)
+        soften(g)
+        if g:
+            add_up(g - 1)
+    add_up(group - 1)
     at = 0
     for distance in range(1, chips + 1):
         base = lax.rem(rank // 2 + distance, chips) * 2
@@ -442,11 +447,18 @@
         else:
             shapes = (out, out, context_shape)
         so_far = pl.pallas_call(
-            functools.partial(late_kernel, h, kv_local, group, part, depth),
+            functools.partial(late_kernel, h, kv_local, group, part, depth, 64),
             out_shape=shapes,
             in_specs=[VMEM] * (7 + len(so_far)),
             out_specs=(VMEM,) * len(shapes),
-            scratch_shapes=[pltpu.VMEM((tokens, share), jnp.bfloat16)] * 2,
+            scratch_shapes=[
+                pltpu.VMEM((tokens, share), jnp.bfloat16),
+                pltpu.VMEM((tokens, share), jnp.bfloat16),
+                pltpu.VMEM((tokens, tokens), jnp.float32),
+                pltpu.VMEM((group, tokens, tokens), jnp.float32),
+                pltpu.VMEM((group, tokens, tokens), jnp.bfloat16),
+                pltpu.VMEM((group, tokens, HD), jnp.float32),
+            ],
             cost_estimate=pl.CostEstimate(
                 flops=4 * tokens * tokens * share + 4 * remote * share * cuts[1],
                 transcendentals=tokens * tokens * group,

time: 59.2 us -> 59.4 us (level)
  transfers between devices with their start and end apart: 17 -> 17, of which waited for: 6 -> 5; matrix products, arithmetic and copies ran while one was open for 2% -> 2% of each run, Pallas kernels for 31% -> 30%
where the time goes in v8:
time: 59.4 us; the launch traced here: 59.1 us
  waiting for transfers between devices  23.7 us (40%)
  Pallas kernels  21.5 us (36%)
  starting transfers between devices  12.7 us (21%)
  other arithmetic  0.95 us (2%)
    ppermute x4, waiting for transfers between devices, layer(): block = lax.ppermute(moved[at:at + part], AXES, y_route(seq, tp, distance))  15.5 us
    ppermute x11, waiting for transfers between devices, send(): return lax.ppermute(x, AXES, route[name, step])  8.19 us
    pallas_call x3, Pallas kernels, load_call(): pl.pallas_call(functools.partial(load_kernel, cuts[0]), out_shape=[pltpu....  7.96 us
    ppermute x11, starting transfers between devices, send(): return lax.ppermute(x, AXES, route[name, step])  6.33 us
    pallas_call x4, Pallas kernels, project_call(): pl.pallas_call(functools.partial(project_kernel, part, first), out_shape=...  5.66 us
    ppermute x4, starting transfers between devices, layer(): block = lax.ppermute(moved[at:at + part], AXES, y_route(seq, tp, distance))  4.31 us
    pallas_call x2, Pallas kernels, layer(): pl.pallas_call(functools.partial(late_kernel, h, kv_local, group, part, d...  2.7 us
    pallas_call x1, Pallas kernels, layer(): acc, top, total = early(query_rows, docs, *blocks)  2.62 us
  transfers between devices with their start and end apart: 17, of which 5 were waited for; matrix products, arithmetic and copies ran while one was open for 2% of the time, Pallas kernels for 30%

profile of v8, /device:TPU:16, one launch (start us, length us, event | category | flops | bytes accessed | tf_op | source)
XLA Modules:
  0.0 59.1 jit_solution(10018840128130431187)
XLA Ops:
  0.0 0.9 %join.1.refs_2_ = bf16[192,512]{1,0:T(8,128)(2,1)S(1)} custom-call(bf16[192,256]{1,0:T(8,128)(2,1)} %k_ref.1, bf16[192,256]{1,0:T(8,128)(2,1)} %v_ref.1), custom_call_target="tpu_custom_call" | custom-call | tf_op jit(solution)/shard_map/join/pallas_call | solution.py:381
  0.9 1.6 %collective-permute-start = (bf16[192,512]{1,0:T(8,128)(2,1)S(1)}, bf16[192,512]{1,0:T(8,128)(2,1)S(1)}, u32[]{:S(2)}, u32[]{:S(2)}) collective-permute-start(bf16[192,512]{1,0:T(8,128)(2,1)S(1)} %join.1.refs_2_), channel_id=1, source_target_pairs={{0,8},{1,9},{2,10},{3,11},{4,12},{5,13},{6,14},{7,15},{8,0},{9,1},... | collective-permute-start | bytes 589832 | tf_op jit(solution)/shard_map/ppermute | solution.py:379
  2.6 0.0 collective-permute-start.1
  2.6 1.5 %collective-permute-start.5 = (bf16[192,512]{1,0:T(8,128)(2,1)S(1)}, bf16[192,512]{1,0:T(8,128)(2,1)S(1)}, u32[]{:S(2)}, u32[]{:S(2)}) collective-permute-start(bf16[192,512]{1,0:T(8,128)(2,1)S(1)} %join.1.refs_2_), channel_id=1, source_target_pairs={{0,4},{1,5},{2,6},{3,7},{4,0},{5,1},{6,2},{7,3},{8,12},{9,13},{10,... | collective-permute-start | bytes 589832 | tf_op jit(solution)/shard_map/ppermute | solution.py:379
  4.0 0.7 %convert_element_type.39 = f32[1536]{0:T(1024)S(1)} convert(s32[1536]{0:T(1024)} %param.8) | non-fusion elementwise | flops 1536 | bytes 12288 | tf_op jit(solution)/shard_map/convert_element_type | solution.py:390
  4.7 0.1 reshape.3.refs_1_
  4.8 2.8 %collective-permute-done = bf16[192,512]{1,0:T(8,128)(2,1)S(1)} collective-permute-done((bf16[192,512]{1,0:T(8,128)(2,1)S(1)}, bf16[192,512]{1,0:T(8,128)(2,1)S(1)}, u32[]{:S(2)}, u32[]{:S(2)}) %collective-permute-start) | collective-permute-done | bytes 196640 | tf_op jit(solution)/shard_map/ppermute | solution.py:379
  7.6 1.3 %collective-permute-done.1 = bf16[192,512]{1,0:T(8,128)(2,1)S(1)} collective-permute-done((bf16[192,512]{1,0:T(8,128)(2,1)S(1)}, bf16[192,512]{1,0:T(8,128)(2,1)S(1)}, u32[]{:S(2)}, u32[]{:S(2)}) %collective-permute-start.1) | collective-permute-done | bytes 196640 | tf_op jit(solution)/shard_map/ppermute | solution.py:379
  8.9 0.3 collective-permute-start.2
  9.2 0.0 collective-permute-start.3
  9.2 1.6 %collective-permute-start.6 = (bf16[192,512]{1,0:T(8,128)(2,1)S(1)}, bf16[192,512]{1,0:T(8,128)(2,1)S(1)}, u32[]{:S(2)}, u32[]{:S(2)}) collective-permute-start(bf16[192,512]{1,0:T(8,128)(2,1)S(1)} %broadcast_select_fusion.refs_4_), channel_id=1, source_target_pairs={{0,1},{1,0},{2,3},{3,2},{4,5},{5,4},{6,7},{7,6},{8,12},{9,13},{10,... | collective-permute-start | bytes 589832 | tf_op jit(solution)/shard_map/ppermute | solution.py:379
  10.8 3.8 %collective-permute-done.2 = bf16[192,512]{1,0:T(8,128)(2,1)S(1)} collective-permute-done((bf16[192,512]{1,0:T(8,128)(2,1)S(1)}, bf16[192,512]{1,0:T(8,128)(2,1)S(1)}, u32[]{:S(2)}, u32[]{:S(2)}) %collective-permute-start.2) | collective-permute-done | bytes 196640 | tf_op jit(solution)/shard_map/ppermute | solution.py:379
  14.6 0.3 collective-permute-done.3
  14.9 1.6 %collective-permute-start.7 = (bf16[192,256]{1,0:T(8,128)(2,1)S(1)}, bf16[192,256]{1,0:T(8,128)(2,1)S(1)}, u32[]{:S(2)}, u32[]{:S(2)}) collective-permute-start(bf16[192,256]{1,0:T(8,128)(2,1)S(1)} %get-tuple-element.51), channel_id=1, source_target_pairs={{0,1},{1,0},{2,3},{3,2},{4,5},{5,4},{6,7},{7,6},{8,9},{9,8},{10,11... | collective-permute-start | bytes 294920 | tf_op jit(solution)/shard_map/ppermute | solution.py:413
  16.5 0.5 collective-permute-start.4
  17.0 2.9 %load.3 = (bf16[1024,1280]{1,0:T(8,128)(2,1)S(1)}, bf16[1024,1792]{1,0:T(8,128)(2,1)S(1)}) custom-call(bf16[1024,8192]{1,0:T(8,128)(2,1)} %w_hbm.5), custom_call_target="tpu_custom_call" | custom-call | bytes 6291456 | tf_op jit(solution)/shard_map/load/pallas_call | solution.py:96
  19.9 3.0 %load.4 = (bf16[1024,768]{1,0:T(8,128)(2,1)S(1)}, bf16[1024,2560]{1,0:T(8,128)(2,1)S(1)}) custom-call(bf16[1024,8192]{1,0:T(8,128)(2,1)} %w_hbm.5), custom_call_target="tpu_custom_call" | custom-call | bytes 6815744 | tf_op jit(solution)/shard_map/load/pallas_call | solution.py:96
  22.9 0.0 copy-start
  22.9 2.1 %load.5.refs_4_.refs_0_ = bf16[1024,1792]{1,0:T(8,128)(2,1)S(1)} custom-call(bf16[1024,8192]{1,0:T(8,128)(2,1)} %w_hbm.5), custom_call_target="tpu_custom_call" | custom-call | bytes 3670016 | tf_op jit(solution)/shard_map/load/pallas_call | solution.py:96
  25.0 0.0 collective-permute-done.5.refs_3_
  25.0 0.0 collective-permute-done.6.refs_5_
  25.0 2.6 %attend_early.1 = (f32[1536,128]{1,0:T(8,128)S(1)}, f32[1536,128]{1,0:T(8,128)S(1)}, f32[1536,128]{1,0:T(8,128)S(1)}) custom-call(bf16[192,1024]{1,0:T(8,128)(2,1)S(1)} %copy-done, f32[8,192]{1,0:T(8,128)S(1)} %reshape.3.refs_1_, bf16[192,512]{1,0:T(8,128)(2,1)S(1)} %join.1.refs_2_, bf16[192,512]{1,0:T(8,128)(2,1)S(1)} %collective-permute-done.5.refs_3_, ...), custom_call_target="tpu_custom_call" | custom-call | flops 754974720 | bytes 786432 | tf_op jit(solution)/shard_map/attend_early/pallas_call | solution.py:436
  27.7 0.0 collective-permute-done.7.refs_2_
  27.7 1.4 %attend_late.2 = (f32[96,1280]{1,0:T(8,128)S(1)}, bf16[192,512]{1,0:T(8,128)(2,1)S(1)}) custom-call(bf16[192,1024]{1,0:T(8,128)(2,1)S(1)} %copy-done, f32[8,192]{1,0:T(8,128)S(1)} %reshape.3.refs_1_, bf16[192,256]{1,0:T(8,128)(2,1)S(1)} %collective-permute-done.7.refs_2_, f32[1536,128]{1,0:T(8,128)S(1)} %get-tuple-element.31.refs_3_, ...), custom_call_target="tpu_custom_call" | custom-call | flops 201326592 | bytes 1703936 | tf_op jit(solution)/shard_map/attend_late/pallas_call | solution.py:449
  29.0 0.0 collective-permute-done.4.refs_2_
  29.0 1.4 %attend_late.3 = (bf16[48,1280]{1,0:T(8,128)(2,1)S(1)}, bf16[48,1280]{1,0:T(8,128)(2,1)S(1)}, bf16[192,1024]{1,0:T(8,128)(2,1)S(1)}) custom-call(bf16[192,1024]{1,0:T(8,128)(2,1)S(1)} %copy-done, f32[8,192]{1,0:T(8,128)S(1)} %reshape.3.refs_1_, bf16[192,256]{1,0:T(8,128)(2,1)S(1)} %collective-permute-done.4.refs_2_, ...), custom_call_target="tpu_custom_call" | custom-call | flops 201326592 | bytes 1703936 | tf_op jit(solution)/shard_map/attend_late/pallas_call | solution.py:449
  30.4 0.8 %project_rest.5 = (bf16[48,1792]{1,0:T(8,128)(2,1)S(1)}, bf16[48,1792]{1,0:T(8,128)(2,1)S(1)}) custom-call(bf16[192,1024]{1,0:T(8,128)(2,1)S(1)} %get-tuple-element.37.context_ref, bf16[1024,1792]{1,0:T(8,128)(2,1)S(1)} %load.5.refs_4_.refs_0_), custom_call_target="tpu_custom_call" | custom-call | flops 352321536 | bytes 3670016 | tf_op jit(solution)/shard_map/project_rest/pallas_call | solution.py:304
  31.1 0.1 collective-permute-start.9
  31.2 2.9 %project_rest.4 = (bf16[48,8192]{1,0:T(8,128)(2,1)S(1)}, bf16[48,8192]{1,0:T(8,128)(2,1)S(1)}) custom-call(bf16[192,1024]{1,0:T(8,128)(2,1)S(1)} %get-tuple-element.37.context_ref, bf16[1024,1280]{1,0:T(8,128)(2,1)S(1)} %get-tuple-element.34.refs_6_.refs_0_, bf16[1024,1792]{1,0:T(8,128)(2,1)S(1)} %get-tuple-element.38.refs_1_.refs_0_, ...), custom_call_target="tpu_custom_call" | custom-call | flops 1610612736 | bytes 16777216 | tf_op jit(solution)/shard_map/project_rest/pallas_call | solution.py:304
  34.1 0.6 collective-permute-start.8
  34.7 0.1 collective-permute-start.11
  34.8 1.0 %project_rest.6 = (bf16[48,2560]{1,0:T(8,128)(2,1)S(1)}, bf16[48,2560]{1,0:T(8,128)(2,1)S(1)}) custom-call(bf16[192,1024]{1,0:T(8,128)(2,1)S(1)} %get-tuple-element.37.context_ref, bf16[1024,1792]{1,0:T(8,128)(2,1)S(1)} %get-tuple-element.38.refs_1_.refs_0_, bf16[1024,768]{1,0:T(8,128)(2,1)S(1)} %get-tuple-element.39.refs_2_.refs_1_), custom_call_target="tpu_custom_call" | custom-call | flops 503316480 | bytes 5242880 | tf_op jit(solution)/shard_map/project_rest/pallas_call | solution.py:304
  35.8 0.5 collective-permute-start.13
  36.3 1.0 %project_rest.7 = (bf16[48,2560]{1,0:T(8,128)(2,1)S(1)}, bf16[48,2560]{1,0:T(8,128)(2,1)S(1)}) custom-call(bf16[192,1024]{1,0:T(8,128)(2,1)S(1)} %get-tuple-element.37.context_ref, bf16[1024,2560]{1,0:T(8,128)(2,1)S(1)} %get-tuple-element.40.refs_3_.refs_0_), custom_call_target="tpu_custom_call" | custom-call | flops 503316480 | bytes 5242880 | tf_op jit(solution)/shard_map/project_rest/pallas_call | solution.py:304
  37.3 0.1 collective-permute-start.15
  37.4 0.0 collective-permute-done.9
  37.5 1.6 %collective-permute-start.10 = (bf16[48,1792]{1,0:T(8,128)(2,1)S(1)}, bf16[48,1792]{1,0:T(8,128)(2,1)S(1)}, u32[]{:S(2)}, u32[]{:S(2)}) collective-permute-start(bf16[48,1792]{1,0:T(8,128)(2,1)S(1)} %add_convert_fusion.2), channel_id=1, source_target_pairs={{0,2},{1,3},{2,0},{3,1},{4,6},{5,7},{6,4},{7,5},{8,10},{9,11},{10,... | collective-permute-start | bytes 516104 | tf_op jit(solution)/shard_map/ppermute | solution.py:482
  39.1 0.0 collective-permute-done.13
  39.1 0.1 add_convert_fusion.1
  39.1 0.6 collective-permute-start.14
  39.7 0.0 collective-permute-done.15
  39.7 0.1 add_convert_fusion
  39.8 1.6 %collective-permute-start.16 = (bf16[48,2560]{1,0:T(8,128)(2,1)S(1)}, bf16[48,2560]{1,0:T(8,128)(2,1)S(1)}, u32[]{:S(2)}, u32[]{:S(2)}) collective-permute-start(bf16[48,2560]{1,0:T(8,128)(2,1)S(1)} %add_convert_fusion), channel_id=1, source_target_pairs={{0,2},{1,3},{2,0},{3,1},{4,6},{5,7},{6,4},{7,5},{8,10},{9,11},{10,... | collective-permute-start | bytes 737288 | tf_op jit(solution)/shard_map/ppermute | solution.py:482
  41.4 0.6 collective-permute-start.12
  42.0 15.4 %collective-permute-done.12.refs_0_ = bf16[48,1280]{1,0:T(8,128)(2,1)S(1)} collective-permute-done((bf16[48,1280]{1,0:T(8,128)(2,1)S(1)}, bf16[48,1280]{1,0:T(8,128)(2,1)S(1)}, u32[]{:S(2)}, u32[]{:S(2)}) %collective-permute-start.12) | collective-permute-done | bytes 122912 | tf_op jit(solution)/shard_map/ppermute | solution.py:482
  57.4 0.9 %finish.2.refs_1_ = bf16[48,8192]{1,0:T(8,128)(2,1)} custom-call(bf16[48,8192]{1,0:T(8,128)(2,1)S(1)} %get-tuple-element.41.kept_ref, bf16[48,8192]{1,0:T(8,128)(2,1)S(1)} %collective-permute-done.8.received_ref, bf16[48,1280]{1,0:T(8,128)(2,1)S(1)} %collective-permute-done.12.refs_0_, bf16[48,2560]{1,0:T(8,128)(2,1)S(1)} %collective-permute-done.14.refs_1_, ...), custom_call_target="tpu_custom_call" | custom-call | flops 1572864 | bytes 1572864 | tf_op jit(solution)/shard_map/finish/pallas_call | solution.py:348
  58.4 0.0 collective-permute-done.10.refs_0_
  58.4 0.7 %finish.3 = bf16[48,8192]{1,0:T(8,128)(2,1)} custom-call(bf16[48,8192]{1,0:T(8,128)(2,1)S(1)} %get-tuple-element.41.kept_ref, bf16[48,8192]{1,0:T(8,128)(2,1)S(1)} %collective-permute-done.8.received_ref, bf16[48,1792]{1,0:T(8,128)(2,1)S(1)} %collective-permute-done.10.refs_0_, bf16[48,8192]{1,0:T(8,128)(2,1)} %finish.2.refs_1_), custom_call_target="tpu_custom_call", output_to_operand_aliasing={{}: (3, {})} | custom-call | flops 1572864 | bytes 1572864 | tf_op jit(solution)/shard_map/finish/pallas_call | solution.py:348
  (10 shorter events, 0.1 us)
Async XLA Ops:
  0.9 6.7 %collective-permute-start = (bf16[192,512]{1,0:T(8,128)(2,1)S(1)}, bf16[192,512]{1,0:T(8,128)(2,1)S(1)}, u32[]{:S(2)}, u32[]{:S(2)}) collective-permute-start(bf16[192,512]{1,0:T(8,128)(2,1)S(1)} %join.1.refs_2_), channel_id=1, source_target_pairs={{0,8},{1,9},{2,10},{3,11},{4,12},{5,13},{6,14},{7,15},{8,0},{9,1},... | collective-permute-start | bytes 589832 | tf_op jit(solution)/shard_map/ppermute | solution.py:379
  2.6 6.4 %collective-permute-start.1 = (bf16[192,512]{1,0:T(8,128)(2,1)S(1)}, bf16[192,512]{1,0:T(8,128)(2,1)S(1)}, u32[]{:S(2)}, u32[]{:S(2)}) collective-permute-start(bf16[192,512]{1,0:T(8,128)(2,1)S(1)} %join.1.refs_2_), channel_id=1, source_target_pairs={{0,1},{1,0},{2,3},{3,2},{4,5},{5,4},{6,7},{7,6},{8,16},{9,17},{10,... | collective-permute-start | bytes 589832 | tf_op jit(solution)/shard_map/ppermute | solution.py:379
  2.6 22.5 %collective-permute-start.5 = (bf16[192,512]{1,0:T(8,128)(2,1)S(1)}, bf16[192,512]{1,0:T(8,128)(2,1)S(1)}, u32[]{:S(2)}, u32[]{:S(2)}) collective-permute-start(bf16[192,512]{1,0:T(8,128)(2,1)S(1)} %join.1.refs_2_), channel_id=1, source_target_pairs={{0,4},{1,5},{2,6},{3,7},{4,0},{5,1},{6,2},{7,3},{8,12},{9,13},{10,... | collective-permute-start | bytes 589832 | tf_op jit(solution)/shard_map/ppermute | solution.py:379
  8.9 5.7 %collective-permute-start.2 = (bf16[192,512]{1,0:T(8,128)(2,1)S(1)}, bf16[192,512]{1,0:T(8,128)(2,1)S(1)}, u32[]{:S(2)}, u32[]{:S(2)}) collective-permute-start(bf16[192,512]{1,0:T(8,128)(2,1)S(1)} %collective-permute-done.1), channel_id=1, source_target_pairs={{0,1},{1,0},{2,3},{3,2},{4,5},{5,4},{6,7},{7,6},{8,9},{9,8},{10,11... | collective-permute-start | bytes 589832 | tf_op jit(solution)/shard_map/ppermute | solution.py:379
  9.2 5.7 %collective-permute-start.3 = (bf16[192,512]{1,0:T(8,128)(2,1)S(1)}, bf16[192,512]{1,0:T(8,128)(2,1)S(1)}, u32[]{:S(2)}, u32[]{:S(2)}) collective-permute-start(bf16[192,512]{1,0:T(8,128)(2,1)S(1)} %collective-permute-done), channel_id=1, source_target_pairs={{0,1},{1,0},{2,3},{3,2},{4,5},{5,4},{6,7},{7,6},{8,16},{9,17},{10,... | collective-permute-start | bytes 589832 | tf_op jit(solution)/shard_map/ppermute | solution.py:379
  9.2 15.8 %collective-permute-start.6 = (bf16[192,512]{1,0:T(8,128)(2,1)S(1)}, bf16[192,512]{1,0:T(8,128)(2,1)S(1)}, u32[]{:S(2)}, u32[]{:S(2)}) collective-permute-start(bf16[192,512]{1,0:T(8,128)(2,1)S(1)} %broadcast_select_fusion.refs_4_), channel_id=1, source_target_pairs={{0,1},{1,0},{2,3},{3,2},{4,5},{5,4},{6,7},{7,6},{8,12},{9,13},{10,... | collective-permute-start | bytes 589832 | tf_op jit(solution)/shard_map/ppermute | solution.py:379
  14.9 12.7 %collective-permute-start.7 = (bf16[192,256]{1,0:T(8,128)(2,1)S(1)}, bf16[192,256]{1,0:T(8,128)(2,1)S(1)}, u32[]{:S(2)}, u32[]{:S(2)}) collective-permute-start(bf16[192,256]{1,0:T(8,128)(2,1)S(1)} %get-tuple-element.51), channel_id=1, source_target_pairs={{0,1},{1,0},{2,3},{3,2},{4,5},{5,4},{6,7},{7,6},{8,9},{9,8},{10,11... | collective-permute-start | bytes 294920 | tf_op jit(solution)/shard_map/ppermute | solution.py:413
  16.5 12.6 %collective-permute-start.4 = (bf16[192,256]{1,0:T(8,128)(2,1)S(1)}, bf16[192,256]{1,0:T(8,128)(2,1)S(1)}, u32[]{:S(2)}, u32[]{:S(2)}) collective-permute-start(bf16[192,256]{1,0:T(8,128)(2,1)S(1)} %get-tuple-element.52), channel_id=1, source_target_pairs={{0,1},{1,0},{2,3},{3,2},{4,5},{5,4},{6,7},{7,6},{8,9},{9,8},{10,11... | collective-permute-start | bytes 294920 | tf_op jit(solution)/shard_map/ppermute | solution.py:413
  22.9 2.1 %copy-start = (bf16[192,1024]{1,0:T(8,128)(2,1)S(1)}, bf16[192,1024]{1,0:T(8,128)(2,1)}, u32[]{:S(2)}) copy-start(bf16[192,1024]{1,0:T(8,128)(2,1)} %refs_0_.5) | copy-start | bytes 1179652
  31.1 6.3 %collective-permute-start.9 = (bf16[48,1792]{1,0:T(8,128)(2,1)S(1)}, bf16[48,1792]{1,0:T(8,128)(2,1)S(1)}, u32[]{:S(2)}, u32[]{:S(2)}) collective-permute-start(bf16[48,1792]{1,0:T(8,128)(2,1)S(1)} %get-tuple-element.44), channel_id=1, source_target_pairs={{0,1},{1,0},{2,3},{3,2},{4,5},{5,4},{6,7},{7,6},{8,9},{9,8},{10,11... | collective-permute-start | bytes 516104 | tf_op jit(solution)/shard_map/ppermute | solution.py:379
  34.1 23.3 %collective-permute-start.8 = (bf16[48,8192]{1,0:T(8,128)(2,1)S(1)}, bf16[48,8192]{1,0:T(8,128)(2,1)S(1)}, u32[]{:S(2)}, u32[]{:S(2)}) collective-permute-start(bf16[48,8192]{1,0:T(8,128)(2,1)S(1)} %get-tuple-element.42), channel_id=1, source_target_pairs={{0,1},{1,0},{2,3},{3,2},{4,5},{5,4},{6,7},{7,6},{8,9},{9,8},{10,11... | collective-permute-start | bytes 2359304 | tf_op jit(solution)/shard_map/ppermute | solution.py:379
  34.7 6.6 %collective-permute-start.11 = (bf16[48,1280]{1,0:T(8,128)(2,1)S(1)}, bf16[48,1280]{1,0:T(8,128)(2,1)S(1)}, u32[]{:S(2)}, u32[]{:S(2)}) collective-permute-start(bf16[48,1280]{1,0:T(8,128)(2,1)S(1)} %get-tuple-element.46), channel_id=1, source_target_pairs={{0,1},{1,0},{2,3},{3,2},{4,5},{5,4},{6,7},{7,6},{8,9},{9,8},{10,11... | collective-permute-start | bytes 368648 | tf_op jit(solution)/shard_map/ppermute | solution.py:379
  35.8 3.2 %collective-permute-start.13 = (bf16[48,2560]{1,0:T(8,128)(2,1)S(1)}, bf16[48,2560]{1,0:T(8,128)(2,1)S(1)}, u32[]{:S(2)}, u32[]{:S(2)}) collective-permute-start(bf16[48,2560]{1,0:T(8,128)(2,1)S(1)} %get-tuple-element.48), channel_id=1, source_target_pairs={{0,1},{1,0},{2,3},{3,2},{4,5},{5,4},{6,7},{7,6},{8,9},{9,8},{10,11... | collective-permute-start | bytes 737288 | tf_op jit(solution)/shard_map/ppermute | solution.py:379
  37.3 2.4 %collective-permute-start.15 = (bf16[48,2560]{1,0:T(8,128)(2,1)S(1)}, bf16[48,2560]{1,0:T(8,128)(2,1)S(1)}, u32[]{:S(2)}, u32[]{:S(2)}) collective-permute-start(bf16[48,2560]{1,0:T(8,128)(2,1)S(1)} %get-tuple-element.50), channel_id=1, source_target_pairs={{0,1},{1,0},{2,3},{3,2},{4,5},{5,4},{6,7},{7,6},{8,9},{9,8},{10,11... | collective-permute-start | bytes 737288 | tf_op jit(solution)/shard_map/ppermute | solution.py:379
  37.5 20.9 %collective-permute-start.10 = (bf16[48,1792]{1,0:T(8,128)(2,1)S(1)}, bf16[48,1792]{1,0:T(8,128)(2,1)S(1)}, u32[]{:S(2)}, u32[]{:S(2)}) collective-permute-start(bf16[48,1792]{1,0:T(8,128)(2,1)S(1)} %add_convert_fusion.2), channel_id=1, source_target_pairs={{0,2},{1,3},{2,0},{3,1},{4,6},{5,7},{6,4},{7,5},{8,10},{9,11},{10,... | collective-permute-start | bytes 516104 | tf_op jit(solution)/shard_map/ppermute | solution.py:482
  39.1 18.3 %collective-permute-start.14 = (bf16[48,2560]{1,0:T(8,128)(2,1)S(1)}, bf16[48,2560]{1,0:T(8,128)(2,1)S(1)}, u32[]{:S(2)}, u32[]{:S(2)}) collective-permute-start(bf16[48,2560]{1,0:T(8,128)(2,1)S(1)} %add_convert_fusion.1), channel_id=1, source_target_pairs={{0,2},{1,3},{2,0},{3,1},{4,6},{5,7},{6,4},{7,5},{8,10},{9,11},{10,... | collective-permute-start | bytes 737288 | tf_op jit(solution)/shard_map/ppermute | solution.py:482
  39.8 17.7 %collective-permute-start.16 = (bf16[48,2560]{1,0:T(8,128)(2,1)S(1)}, bf16[48,2560]{1,0:T(8,128)(2,1)S(1)}, u32[]{:S(2)}, u32[]{:S(2)}) collective-permute-start(bf16[48,2560]{1,0:T(8,128)(2,1)S(1)} %add_convert_fusion), channel_id=1, source_target_pairs={{0,2},{1,3},{2,0},{3,1},{4,6},{5,7},{6,4},{7,5},{8,10},{9,11},{10,... | collective-permute-start | bytes 737288 | tf_op jit(solution)/shard_map/ppermute | solution.py:482
  41.4 16.0 %collective-permute-start.12 = (bf16[48,1280]{1,0:T(8,128)(2,1)S(1)}, bf16[48,1280]{1,0:T(8,128)(2,1)S(1)}, u32[]{:S(2)}, u32[]{:S(2)}) collective-permute-start(bf16[48,1280]{1,0:T(8,128)(2,1)S(1)} %add_convert_fusion.3), channel_id=1, source_target_pairs={{0,2},{1,3},{2,0},{3,1},{4,6},{5,7},{6,4},{7,5},{8,10},{9,11},{10,... | collective-permute-start | bytes 368648 | tf_op jit(solution)/shard_map/ppermute | solution.py:482

commit v9 on v8

--- a/solution.py
+++ b/solution.py
@@ -120,7 +120,6 @@
         docs,
         own.astype(jnp.float32),
         (((0,), (0,)), ((), ())),
-        precision=lax.Precision.HIGHEST,
         preferred_element_type=jnp.float32,
     )
     return column[:, :1]
@@ -144,8 +143,8 @@
 def early_kernel(kv_local, group, count, step, *refs):
     q_ref, docs_ref = refs[:2]
     blocks = refs[2 : 2 + count]
-    acc_ref, top_ref, sum_ref = refs[2 + count : 5 + count]
-    bias_ref, s_ref, p_ref = refs[5 + count :]
+    acc_ref, top_ref, sum_ref, last_bias_ref = refs[2 + count : 6 + count]
+    bias_ref, s_ref, p_ref = refs[6 + count :]
     tokens = q_ref.shape[0]
     me = lax.axis_index("seq")
     row, col = me // 2, me % 2
@@ -153,7 +152,10 @@
     for i in range(count):
         block = me - i if i % 2 == 0 else (row - i // 2) * 2 + 1 - col
         docs.append(key_doc(docs_ref, block, me))
-    allowed = query_doc(docs_ref, me) == jnp.concatenate(docs, axis=1)
+    own_doc = query_doc(docs_ref, me)
+    far = key_doc(docs_ref, (row - count // 2) * 2 + 1 - col, me)
+    last_bias_ref[...] = jnp.where(own_doc == far, 0.0, -jnp.inf)
+    allowed = own_doc == jnp.concatenate(docs, axis=1)
     key_at = lax.broadcasted_iota(jnp.int32, (tokens, count * tokens), 1)
     query_at = lax.broadcasted_iota(jnp.int32, (tokens, count * tokens), 0)
     allowed = allowed & ((key_at <= query_at) | (key_at >= tokens))
@@ -215,17 +217,12 @@
             send_ref[into, at] = rows[(2 * i + 1) * part : (2 * i + 2) * part]
 
 
-def late_kernel(h, kv_local, group, part, depth, step, *refs):
-    q_ref, docs_ref, block, acc_ref, top_ref, sum_ref, w_ref = refs[:7]
-    context_ref, here_ref, bias_ref, s_ref, p_ref, rescale_ref = refs[-6:]
-    refs = refs[7:-6]
+def late_kernel(h, kv_local, group, part, step, *refs):
+    q_ref, bias_ref, block, acc_ref, top_ref, sum_ref, w_ref = refs[:7]
+    context_ref, here_ref, s_ref, p_ref, rescale_ref = refs[-5:]
+    refs = refs[7:-5]
     tokens = q_ref.shape[0]
-    me, rank = lax.axis_index("seq"), lax.axis_index("tp")
-    chips = lax.axis_size("tp") // 2
-    far = (me // 2 - depth) * 2 + 1 - me % 2
-    bias_ref[...] = jnp.where(
-        query_doc(docs_ref, me) == key_doc(docs_ref, far, me), 0.0, -jnp.inf
-    )
+    rank, chips = lax.axis_index("tp"), lax.axis_size("tp") // 2
     keys, values = block[:, pl.ds(0, HD)], with_ones(block[:, pl.ds(HD, HD)])
 
     def score(g):
@@ -417,9 +414,14 @@
     state = jax.ShapeDtypeStruct((kv_local * stacked, HD), jnp.float32)
     early = pl.pallas_call(
         functools.partial(early_kernel, kv_local, group, count, 64),
-        out_shape=(state, state, state),
+        out_shape=(
+            state,
+            state,
+            state,
+            jax.ShapeDtypeStruct((tokens, tokens), jnp.float32),
+        ),
         in_specs=[VMEM] * (2 + count),
-        out_specs=(VMEM,) * 3,
+        out_specs=(VMEM,) * 4,
         scratch_shapes=[
             pltpu.VMEM((tokens, count * tokens), jnp.float32),
             pltpu.VMEM((kv_local * group, tokens, count * tokens), jnp.float32),
@@ -433,7 +435,7 @@
         compiler_params=pltpu.CompilerParams(vmem_limit_bytes=EARLY * MIB),
         name="attend_early",
     )
-    acc, top, total = early(query_rows, docs, *blocks)
+    acc, top, total, bias = early(query_rows, docs, *blocks)
 
     remote = (chips - 1) * part
     out = jax.ShapeDtypeStruct((remote, cuts[1]), jnp.bfloat16)
@@ -447,14 +449,13 @@
         else:
             shapes = (out, out, context_shape)
         so_far = pl.pallas_call(
-            functools.partial(late_kernel, h, kv_local, group, part, depth, 64),
+            functools.partial(late_kernel, h, kv_local, group, part, 64),
             out_shape=shapes,
             in_specs=[VMEM] * (7 + len(so_far)),
             out_specs=(VMEM,) * len(shapes),
             scratch_shapes=[
                 pltpu.VMEM((tokens, share), jnp.bfloat16),
                 pltpu.VMEM((tokens, share), jnp.bfloat16),
-                pltpu.VMEM((tokens, tokens), jnp.float32),
                 pltpu.VMEM((group, tokens, tokens), jnp.float32),
                 pltpu.VMEM((group, tokens, tokens), jnp.bfloat16),
                 pltpu.VMEM((group, tokens, HD), jnp.float32),
@@ -466,7 +467,7 @@
             ),
             compiler_params=pltpu.CompilerParams(vmem_limit_bytes=LATE * MIB),
             name="attend_late",
-        )(query_rows, docs, last_block, acc, top, total, first, *so_far)
+        )(query_rows, bias, last_block, acc, top, total, first, *so_far)
     sent, kept, context = so_far
 
     arrived = []

time: 59.4 us -> 58.9 us (level)
  no operation moved by 1% of the time
where the time goes in v9:
time: 58.9 us; the launch traced here: 58.7 us
  waiting for transfers between devices  23.7 us (40%)
  Pallas kernels  21.1 us (36%)
  starting transfers between devices  12.7 us (22%)
  other arithmetic  0.94 us (2%)
    ppermute x4, waiting for transfers between devices, layer(): block = lax.ppermute(moved[at:at + part], AXES, y_route(seq, tp, distance))  15.5 us
    ppermute x11, waiting for transfers between devices, send(): return lax.ppermute(x, AXES, route[name, step])  8.19 us
    pallas_call x3, Pallas kernels, load_call(): pl.pallas_call(functools.partial(load_kernel, cuts[0]), out_shape=[pltpu....  7.96 us
    ppermute x11, starting transfers between devices, send(): return lax.ppermute(x, AXES, route[name, step])  6.33 us
    pallas_call x4, Pallas kernels, project_call(): pl.pallas_call(functools.partial(project_kernel, part, first), out_shape=...  5.66 us
    ppermute x4, starting transfers between devices, layer(): block = lax.ppermute(moved[at:at + part], AXES, y_route(seq, tp, distance))  4.31 us
    pallas_call x1, Pallas kernels, layer(): acc, top, total, bias = early(query_rows, docs, *blocks)  2.67 us
    pallas_call x2, Pallas kernels, layer(): pl.pallas_call(functools.partial(late_kernel, h, kv_local, group, part, 6...  2.24 us
  transfers between devices with their start and end apart: 17, of which 5 were waited for; matrix products, arithmetic and copies ran while one was open for 2% of the time, Pallas kernels for 30%

profile of v9, /device:TPU:16, one launch (start us, length us, event | category | flops | bytes accessed | tf_op | source)
XLA Modules:
  0.0 58.7 jit_solution(15184556322351465933)
XLA Ops:
  0.0 0.9 %join.1.refs_2_ = bf16[192,512]{1,0:T(8,128)(2,1)S(1)} custom-call(bf16[192,256]{1,0:T(8,128)(2,1)} %k_ref.1, bf16[192,256]{1,0:T(8,128)(2,1)} %v_ref.1), custom_call_target="tpu_custom_call" | custom-call | tf_op jit(solution)/shard_map/join/pallas_call | solution.py:378
  0.9 1.6 %collective-permute-start = (bf16[192,512]{1,0:T(8,128)(2,1)S(1)}, bf16[192,512]{1,0:T(8,128)(2,1)S(1)}, u32[]{:S(2)}, u32[]{:S(2)}) collective-permute-start(bf16[192,512]{1,0:T(8,128)(2,1)S(1)} %join.1.refs_2_), channel_id=1, source_target_pairs={{0,8},{1,9},{2,10},{3,11},{4,12},{5,13},{6,14},{7,15},{8,0},{9,1},... | collective-permute-start | bytes 589832 | tf_op jit(solution)/shard_map/ppermute | solution.py:376
  2.6 0.0 collective-permute-start.1
  2.6 1.5 %collective-permute-start.2 = (bf16[192,512]{1,0:T(8,128)(2,1)S(1)}, bf16[192,512]{1,0:T(8,128)(2,1)S(1)}, u32[]{:S(2)}, u32[]{:S(2)}) collective-permute-start(bf16[192,512]{1,0:T(8,128)(2,1)S(1)} %join.1.refs_2_), channel_id=1, source_target_pairs={{0,4},{1,5},{2,6},{3,7},{4,0},{5,1},{6,2},{7,3},{8,12},{9,13},{10,... | collective-permute-start | bytes 589832 | tf_op jit(solution)/shard_map/ppermute | solution.py:376
  4.0 0.7 %convert_element_type.39 = f32[1536]{0:T(1024)S(1)} convert(s32[1536]{0:T(1024)} %param.8) | non-fusion elementwise | flops 1536 | bytes 12288 | tf_op jit(solution)/shard_map/convert_element_type | solution.py:387
  4.7 0.1 reshape.3.refs_1_
  4.8 2.8 %collective-permute-done = bf16[192,512]{1,0:T(8,128)(2,1)S(1)} collective-permute-done((bf16[192,512]{1,0:T(8,128)(2,1)S(1)}, bf16[192,512]{1,0:T(8,128)(2,1)S(1)}, u32[]{:S(2)}, u32[]{:S(2)}) %collective-permute-start) | collective-permute-done | bytes 196640 | tf_op jit(solution)/shard_map/ppermute | solution.py:376
  7.6 1.3 %collective-permute-done.1 = bf16[192,512]{1,0:T(8,128)(2,1)S(1)} collective-permute-done((bf16[192,512]{1,0:T(8,128)(2,1)S(1)}, bf16[192,512]{1,0:T(8,128)(2,1)S(1)}, u32[]{:S(2)}, u32[]{:S(2)}) %collective-permute-start.1) | collective-permute-done | bytes 196640 | tf_op jit(solution)/shard_map/ppermute | solution.py:376
  8.9 0.3 collective-permute-start.4
  9.2 1.6 %collective-permute-start.3 = (bf16[192,512]{1,0:T(8,128)(2,1)S(1)}, bf16[192,512]{1,0:T(8,128)(2,1)S(1)}, u32[]{:S(2)}, u32[]{:S(2)}) collective-permute-start(bf16[192,512]{1,0:T(8,128)(2,1)S(1)} %broadcast_select_fusion.1.refs_4_), channel_id=1, source_target_pairs={{0,1},{1,0},{2,3},{3,2},{4,5},{5,4},{6,7},{7,6},{8,12},{9,13},{10,... | collective-permute-start | bytes 589832 | tf_op jit(solution)/shard_map/ppermute | solution.py:376
  10.8 3.8 %collective-permute-done.4 = bf16[192,512]{1,0:T(8,128)(2,1)S(1)} collective-permute-done((bf16[192,512]{1,0:T(8,128)(2,1)S(1)}, bf16[192,512]{1,0:T(8,128)(2,1)S(1)}, u32[]{:S(2)}, u32[]{:S(2)}) %collective-permute-start.4) | collective-permute-done | bytes 196640 | tf_op jit(solution)/shard_map/ppermute | solution.py:376
  14.6 0.3 collective-permute-done.5
  14.9 1.6 %collective-permute-start.7 = (bf16[192,256]{1,0:T(8,128)(2,1)S(1)}, bf16[192,256]{1,0:T(8,128)(2,1)S(1)}, u32[]{:S(2)}, u32[]{:S(2)}) collective-permute-start(bf16[192,256]{1,0:T(8,128)(2,1)S(1)} %get-tuple-element.53), channel_id=1, source_target_pairs={{0,1},{1,0},{2,3},{3,2},{4,5},{5,4},{6,7},{7,6},{8,9},{9,8},{10,11... | collective-permute-start | bytes 294920 | tf_op jit(solution)/shard_map/ppermute | solution.py:410
  16.5 0.5 collective-permute-start.6
  17.0 2.9 %load.3 = (bf16[1024,1280]{1,0:T(8,128)(2,1)S(1)}, bf16[1024,1792]{1,0:T(8,128)(2,1)S(1)}) custom-call(bf16[1024,8192]{1,0:T(8,128)(2,1)} %w_hbm.5), custom_call_target="tpu_custom_call" | custom-call | bytes 6291456 | tf_op jit(solution)/shard_map/load/pallas_call | solution.py:96
  19.9 3.0 %load.4 = (bf16[1024,768]{1,0:T(8,128)(2,1)S(1)}, bf16[1024,2560]{1,0:T(8,128)(2,1)S(1)}) custom-call(bf16[1024,8192]{1,0:T(8,128)(2,1)} %w_hbm.5), custom_call_target="tpu_custom_call" | custom-call | bytes 6815744 | tf_op jit(solution)/shard_map/load/pallas_call | solution.py:96
  22.9 0.0 copy-start
  22.9 2.1 %load.5.refs_4_.refs_0_ = bf16[1024,1792]{1,0:T(8,128)(2,1)S(1)} custom-call(bf16[1024,8192]{1,0:T(8,128)(2,1)} %w_hbm.5), custom_call_target="tpu_custom_call" | custom-call | bytes 3670016 | tf_op jit(solution)/shard_map/load/pallas_call | solution.py:96
  25.0 0.0 collective-permute-done.3.refs_5_
  25.0 2.7 %attend_early.1 = (f32[1536,128]{1,0:T(8,128)S(1)}, f32[1536,128]{1,0:T(8,128)S(1)}, f32[1536,128]{1,0:T(8,128)S(1)}, f32[192,192]{1,0:T(8,128)S(1)}) custom-call(bf16[192,1024]{1,0:T(8,128)(2,1)S(1)} %copy-done, f32[8,192]{1,0:T(8,128)S(1)} %reshape.3.refs_1_, bf16[192,512]{1,0:T(8,128)(2,1)S(1)} %join.1.refs_2_, ...), custom_call_target="tpu_custom_call" | custom-call | flops 754974720 | bytes 786432 | tf_op jit(solution)/shard_map/attend_early/pallas_call | solution.py:438
  27.7 1.1 %attend_late.2 = (f32[96,1280]{1,0:T(8,128)S(1)}, bf16[192,512]{1,0:T(8,128)(2,1)S(1)}) custom-call(bf16[192,1024]{1,0:T(8,128)(2,1)S(1)} %copy-done, f32[192,192]{1,0:T(8,128)S(1)} %get-tuple-element.32.refs_1_, bf16[192,256]{1,0:T(8,128)(2,1)S(1)} %collective-permute-done.7.refs_2_, f32[1536,128]{1,0:T(8,128)S(1)} %get-tuple-element.33.refs_3_, ...), custom_call_target="tpu_custom_call" | custom-call | flops 201326592 | bytes 1703936 | tf_op jit(solution)/shard_map/attend_late/pallas_call | solution.py:451
  28.8 0.0 collective-permute-done.6.refs_2_
  28.9 1.1 %attend_late.3 = (bf16[48,1280]{1,0:T(8,128)(2,1)S(1)}, bf16[48,1280]{1,0:T(8,128)(2,1)S(1)}, bf16[192,1024]{1,0:T(8,128)(2,1)S(1)}) custom-call(bf16[192,1024]{1,0:T(8,128)(2,1)S(1)} %copy-done, f32[192,192]{1,0:T(8,128)S(1)} %get-tuple-element.32.refs_1_, bf16[192,256]{1,0:T(8,128)(2,1)S(1)} %collective-permute-done.6.refs_2_, ...), custom_call_target="tpu_custom_call" | custom-call | flops 201326592 | bytes 1703936 | tf_op jit(solution)/shard_map/attend_late/pallas_call | solution.py:451
  30.0 0.8 %project_rest.5 = (bf16[48,1792]{1,0:T(8,128)(2,1)S(1)}, bf16[48,1792]{1,0:T(8,128)(2,1)S(1)}) custom-call(bf16[192,1024]{1,0:T(8,128)(2,1)S(1)} %get-tuple-element.39.context_ref, bf16[1024,1792]{1,0:T(8,128)(2,1)S(1)} %load.5.refs_4_.refs_0_), custom_call_target="tpu_custom_call" | custom-call | flops 352321536 | bytes 3670016 | tf_op jit(solution)/shard_map/project_rest/pallas_call | solution.py:301
  30.7 0.1 collective-permute-start.9
  30.8 2.9 %project_rest.4 = (bf16[48,8192]{1,0:T(8,128)(2,1)S(1)}, bf16[48,8192]{1,0:T(8,128)(2,1)S(1)}) custom-call(bf16[192,1024]{1,0:T(8,128)(2,1)S(1)} %get-tuple-element.39.context_ref, bf16[1024,1280]{1,0:T(8,128)(2,1)S(1)} %get-tuple-element.36.refs_6_.refs_0_, bf16[1024,1792]{1,0:T(8,128)(2,1)S(1)} %get-tuple-element.40.refs_1_.refs_0_, ...), custom_call_target="tpu_custom_call" | custom-call | flops 1610612736 | bytes 16777216 | tf_op jit(solution)/shard_map/project_rest/pallas_call | solution.py:301
  33.7 0.6 collective-permute-start.8
  34.3 0.1 collective-permute-start.11
  34.4 1.0 %project_rest.6 = (bf16[48,2560]{1,0:T(8,128)(2,1)S(1)}, bf16[48,2560]{1,0:T(8,128)(2,1)S(1)}) custom-call(bf16[192,1024]{1,0:T(8,128)(2,1)S(1)} %get-tuple-element.39.context_ref, bf16[1024,1792]{1,0:T(8,128)(2,1)S(1)} %get-tuple-element.40.refs_1_.refs_0_, bf16[1024,768]{1,0:T(8,128)(2,1)S(1)} %get-tuple-element.41.refs_2_.refs_1_), custom_call_target="tpu_custom_call" | custom-call | flops 503316480 | bytes 5242880 | tf_op jit(solution)/shard_map/project_rest/pallas_call | solution.py:301
  35.4 0.5 collective-permute-start.13
  35.9 1.0 %project_rest.7 = (bf16[48,2560]{1,0:T(8,128)(2,1)S(1)}, bf16[48,2560]{1,0:T(8,128)(2,1)S(1)}) custom-call(bf16[192,1024]{1,0:T(8,128)(2,1)S(1)} %get-tuple-element.39.context_ref, bf16[1024,2560]{1,0:T(8,128)(2,1)S(1)} %get-tuple-element.42.refs_3_.refs_0_), custom_call_target="tpu_custom_call" | custom-call | flops 503316480 | bytes 5242880 | tf_op jit(solution)/shard_map/project_rest/pallas_call | solution.py:301
  36.9 0.1 collective-permute-start.15
  37.0 0.0 collective-permute-done.9
  37.1 1.6 %collective-permute-start.10 = (bf16[48,1792]{1,0:T(8,128)(2,1)S(1)}, bf16[48,1792]{1,0:T(8,128)(2,1)S(1)}, u32[]{:S(2)}, u32[]{:S(2)}) collective-permute-start(bf16[48,1792]{1,0:T(8,128)(2,1)S(1)} %add_convert_fusion.2), channel_id=1, source_target_pairs={{0,2},{1,3},{2,0},{3,1},{4,6},{5,7},{6,4},{7,5},{8,10},{9,11},{10,... | collective-permute-start | bytes 516104 | tf_op jit(solution)/shard_map/ppermute | solution.py:483
  38.6 0.0 collective-permute-done.13
  38.6 0.1 add_convert_fusion.1
  38.7 0.6 collective-permute-start.14
  39.3 0.1 add_convert_fusion
  39.4 1.6 %collective-permute-start.16 = (bf16[48,2560]{1,0:T(8,128)(2,1)S(1)}, bf16[48,2560]{1,0:T(8,128)(2,1)S(1)}, u32[]{:S(2)}, u32[]{:S(2)}) collective-permute-start(bf16[48,2560]{1,0:T(8,128)(2,1)S(1)} %add_convert_fusion), channel_id=1, source_target_pairs={{0,2},{1,3},{2,0},{3,1},{4,6},{5,7},{6,4},{7,5},{8,10},{9,11},{10,... | collective-permute-start | bytes 737288 | tf_op jit(solution)/shard_map/ppermute | solution.py:483
  40.9 0.0 collective-permute-done.11
  41.0 0.6 collective-permute-start.12
  41.6 15.4 %collective-permute-done.12.refs_0_ = bf16[48,1280]{1,0:T(8,128)(2,1)S(1)} collective-permute-done((bf16[48,1280]{1,0:T(8,128)(2,1)S(1)}, bf16[48,1280]{1,0:T(8,128)(2,1)S(1)}, u32[]{:S(2)}, u32[]{:S(2)}) %collective-permute-start.12) | collective-permute-done | bytes 122912 | tf_op jit(solution)/shard_map/ppermute | solution.py:483
  57.0 0.0 collective-permute-done.14.refs_1_
  57.0 0.0 collective-permute-done.16.refs_2_
  57.0 0.0 collective-permute-done.8.received_ref
  57.0 0.9 %finish.2.refs_1_ = bf16[48,8192]{1,0:T(8,128)(2,1)} custom-call(bf16[48,8192]{1,0:T(8,128)(2,1)S(1)} %get-tuple-element.43.kept_ref, bf16[48,8192]{1,0:T(8,128)(2,1)S(1)} %collective-permute-done.8.received_ref, bf16[48,1280]{1,0:T(8,128)(2,1)S(1)} %collective-permute-done.12.refs_0_, bf16[48,2560]{1,0:T(8,128)(2,1)S(1)} %collective-permute-done.14.refs_1_, ...), custom_call_target="tpu_custom_call" | custom-call | flops 1572864 | bytes 1572864 | tf_op jit(solution)/shard_map/finish/pallas_call | solution.py:345
  58.0 0.0 collective-permute-done.10.refs_0_
  58.0 0.7 %finish.3 = bf16[48,8192]{1,0:T(8,128)(2,1)} custom-call(bf16[48,8192]{1,0:T(8,128)(2,1)S(1)} %get-tuple-element.43.kept_ref, bf16[48,8192]{1,0:T(8,128)(2,1)S(1)} %collective-permute-done.8.received_ref, bf16[48,1792]{1,0:T(8,128)(2,1)S(1)} %collective-permute-done.10.refs_0_, bf16[48,8192]{1,0:T(8,128)(2,1)} %finish.2.refs_1_), custom_call_target="tpu_custom_call", output_to_operand_aliasing={{}: (3, {})} | custom-call | flops 1572864 | bytes 1572864 | tf_op jit(solution)/shard_map/finish/pallas_call | solution.py:345
  (10 shorter events, 0.1 us)
Async XLA Ops:
  0.9 6.7 %collective-permute-start = (bf16[192,512]{1,0:T(8,128)(2,1)S(1)}, bf16[192,512]{1,0:T(8,128)(2,1)S(1)}, u32[]{:S(2)}, u32[]{:S(2)}) collective-permute-start(bf16[192,512]{1,0:T(8,128)(2,1)S(1)} %join.1.refs_2_), channel_id=1, source_target_pairs={{0,8},{1,9},{2,10},{3,11},{4,12},{5,13},{6,14},{7,15},{8,0},{9,1},... | collective-permute-start | bytes 589832 | tf_op jit(solution)/shard_map/ppermute | solution.py:376
  2.6 6.4 %collective-permute-start.1 = (bf16[192,512]{1,0:T(8,128)(2,1)S(1)}, bf16[192,512]{1,0:T(8,128)(2,1)S(1)}, u32[]{:S(2)}, u32[]{:S(2)}) collective-permute-start(bf16[192,512]{1,0:T(8,128)(2,1)S(1)} %join.1.refs_2_), channel_id=1, source_target_pairs={{0,1},{1,0},{2,3},{3,2},{4,5},{5,4},{6,7},{7,6},{8,16},{9,17},{10,... | collective-permute-start | bytes 589832 | tf_op jit(solution)/shard_map/ppermute | solution.py:376
  2.6 22.5 %collective-permute-start.2 = (bf16[192,512]{1,0:T(8,128)(2,1)S(1)}, bf16[192,512]{1,0:T(8,128)(2,1)S(1)}, u32[]{:S(2)}, u32[]{:S(2)}) collective-permute-start(bf16[192,512]{1,0:T(8,128)(2,1)S(1)} %join.1.refs_2_), channel_id=1, source_target_pairs={{0,4},{1,5},{2,6},{3,7},{4,0},{5,1},{6,2},{7,3},{8,12},{9,13},{10,... | collective-permute-start | bytes 589832 | tf_op jit(solution)/shard_map/ppermute | solution.py:376
  8.9 5.7 %collective-permute-start.4 = (bf16[192,512]{1,0:T(8,128)(2,1)S(1)}, bf16[192,512]{1,0:T(8,128)(2,1)S(1)}, u32[]{:S(2)}, u32[]{:S(2)}) collective-permute-start(bf16[192,512]{1,0:T(8,128)(2,1)S(1)} %collective-permute-done.1), channel_id=1, source_target_pairs={{0,1},{1,0},{2,3},{3,2},{4,5},{5,4},{6,7},{7,6},{8,9},{9,8},{10,11... | collective-permute-start | bytes 589832 | tf_op jit(solution)/shard_map/ppermute | solution.py:376
  9.2 5.7 %collective-permute-start.5 = (bf16[192,512]{1,0:T(8,128)(2,1)S(1)}, bf16[192,512]{1,0:T(8,128)(2,1)S(1)}, u32[]{:S(2)}, u32[]{:S(2)}) collective-permute-start(bf16[192,512]{1,0:T(8,128)(2,1)S(1)} %collective-permute-done), channel_id=1, source_target_pairs={{0,1},{1,0},{2,3},{3,2},{4,5},{5,4},{6,7},{7,6},{8,16},{9,17},{10,... | collective-permute-start | bytes 589832 | tf_op jit(solution)/shard_map/ppermute | solution.py:376
  9.2 15.8 %collective-permute-start.3 = (bf16[192,512]{1,0:T(8,128)(2,1)S(1)}, bf16[192,512]{1,0:T(8,128)(2,1)S(1)}, u32[]{:S(2)}, u32[]{:S(2)}) collective-permute-start(bf16[192,512]{1,0:T(8,128)(2,1)S(1)} %broadcast_select_fusion.1.refs_4_), channel_id=1, source_target_pairs={{0,1},{1,0},{2,3},{3,2},{4,5},{5,4},{6,7},{7,6},{8,12},{9,13},{10,... | collective-permute-start | bytes 589832 | tf_op jit(solution)/shard_map/ppermute | solution.py:376
  14.9 12.8 %collective-permute-start.7 = (bf16[192,256]{1,0:T(8,128)(2,1)S(1)}, bf16[192,256]{1,0:T(8,128)(2,1)S(1)}, u32[]{:S(2)}, u32[]{:S(2)}) collective-permute-start(bf16[192,256]{1,0:T(8,128)(2,1)S(1)} %get-tuple-element.53), channel_id=1, source_target_pairs={{0,1},{1,0},{2,3},{3,2},{4,5},{5,4},{6,7},{7,6},{8,9},{9,8},{10,11... | collective-permute-start | bytes 294920 | tf_op jit(solution)/shard_map/ppermute | solution.py:410
  16.5 12.4 %collective-permute-start.6 = (bf16[192,256]{1,0:T(8,128)(2,1)S(1)}, bf16[192,256]{1,0:T(8,128)(2,1)S(1)}, u32[]{:S(2)}, u32[]{:S(2)}) collective-permute-start(bf16[192,256]{1,0:T(8,128)(2,1)S(1)} %get-tuple-element.54), channel_id=1, source_target_pairs={{0,1},{1,0},{2,3},{3,2},{4,5},{5,4},{6,7},{7,6},{8,9},{9,8},{10,11... | collective-permute-start | bytes 294920 | tf_op jit(solution)/shard_map/ppermute | solution.py:410
  22.9 2.1 %copy-start = (bf16[192,1024]{1,0:T(8,128)(2,1)S(1)}, bf16[192,1024]{1,0:T(8,128)(2,1)}, u32[]{:S(2)}) copy-start(bf16[192,1024]{1,0:T(8,128)(2,1)} %refs_0_.5) | copy-start | bytes 1179652
  30.7 6.3 %collective-permute-start.9 = (bf16[48,1792]{1,0:T(8,128)(2,1)S(1)}, bf16[48,1792]{1,0:T(8,128)(2,1)S(1)}, u32[]{:S(2)}, u32[]{:S(2)}) collective-permute-start(bf16[48,1792]{1,0:T(8,128)(2,1)S(1)} %get-tuple-element.46), channel_id=1, source_target_pairs={{0,1},{1,0},{2,3},{3,2},{4,5},{5,4},{6,7},{7,6},{8,9},{9,8},{10,11... | collective-permute-start | bytes 516104 | tf_op jit(solution)/shard_map/ppermute | solution.py:376
  33.7 23.3 %collective-permute-start.8 = (bf16[48,8192]{1,0:T(8,128)(2,1)S(1)}, bf16[48,8192]{1,0:T(8,128)(2,1)S(1)}, u32[]{:S(2)}, u32[]{:S(2)}) collective-permute-start(bf16[48,8192]{1,0:T(8,128)(2,1)S(1)} %get-tuple-element.44), channel_id=1, source_target_pairs={{0,1},{1,0},{2,3},{3,2},{4,5},{5,4},{6,7},{7,6},{8,9},{9,8},{10,11... | collective-permute-start | bytes 2359304 | tf_op jit(solution)/shard_map/ppermute | solution.py:376
  34.3 6.6 %collective-permute-start.11 = (bf16[48,1280]{1,0:T(8,128)(2,1)S(1)}, bf16[48,1280]{1,0:T(8,128)(2,1)S(1)}, u32[]{:S(2)}, u32[]{:S(2)}) collective-permute-start(bf16[48,1280]{1,0:T(8,128)(2,1)S(1)} %get-tuple-element.48), channel_id=1, source_target_pairs={{0,1},{1,0},{2,3},{3,2},{4,5},{5,4},{6,7},{7,6},{8,9},{9,8},{10,11... | collective-permute-start | bytes 368648 | tf_op jit(solution)/shard_map/ppermute | solution.py:376
  35.4 3.2 %collective-permute-start.13 = (bf16[48,2560]{1,0:T(8,128)(2,1)S(1)}, bf16[48,2560]{1,0:T(8,128)(2,1)S(1)}, u32[]{:S(2)}, u32[]{:S(2)}) collective-permute-start(bf16[48,2560]{1,0:T(8,128)(2,1)S(1)} %get-tuple-element.50), channel_id=1, source_target_pairs={{0,1},{1,0},{2,3},{3,2},{4,5},{5,4},{6,7},{7,6},{8,9},{9,8},{10,11... | collective-permute-start | bytes 737288 | tf_op jit(solution)/shard_map/ppermute | solution.py:376
  36.9 2.4 %collective-permute-start.15 = (bf16[48,2560]{1,0:T(8,128)(2,1)S(1)}, bf16[48,2560]{1,0:T(8,128)(2,1)S(1)}, u32[]{:S(2)}, u32[]{:S(2)}) collective-permute-start(bf16[48,2560]{1,0:T(8,128)(2,1)S(1)} %get-tuple-element.52), channel_id=1, source_target_pairs={{0,1},{1,0},{2,3},{3,2},{4,5},{5,4},{6,7},{7,6},{8,9},{9,8},{10,11... | collective-permute-start | bytes 737288 | tf_op jit(solution)/shard_map/ppermute | solution.py:376
  37.1 20.9 %collective-permute-start.10 = (bf16[48,1792]{1,0:T(8,128)(2,1)S(1)}, bf16[48,1792]{1,0:T(8,128)(2,1)S(1)}, u32[]{:S(2)}, u32[]{:S(2)}) collective-permute-start(bf16[48,1792]{1,0:T(8,128)(2,1)S(1)} %add_convert_fusion.2), channel_id=1, source_target_pairs={{0,2},{1,3},{2,0},{3,1},{4,6},{5,7},{6,4},{7,5},{8,10},{9,11},{10,... | collective-permute-start | bytes 516104 | tf_op jit(solution)/shard_map/ppermute | solution.py:483
  38.7 18.3 %collective-permute-start.14 = (bf16[48,2560]{1,0:T(8,128)(2,1)S(1)}, bf16[48,2560]{1,0:T(8,128)(2,1)S(1)}, u32[]{:S(2)}, u32[]{:S(2)}) collective-permute-start(bf16[48,2560]{1,0:T(8,128)(2,1)S(1)} %add_convert_fusion.1), channel_id=1, source_target_pairs={{0,2},{1,3},{2,0},{3,1},{4,6},{5,7},{6,4},{7,5},{8,10},{9,11},{10,... | collective-permute-start | bytes 737288 | tf_op jit(solution)/shard_map/ppermute | solution.py:483
  39.4 17.6 %collective-permute-start.16 = (bf16[48,2560]{1,0:T(8,128)(2,1)S(1)}, bf16[48,2560]{1,0:T(8,128)(2,1)S(1)}, u32[]{:S(2)}, u32[]{:S(2)}) collective-permute-start(bf16[48,2560]{1,0:T(8,128)(2,1)S(1)} %add_convert_fusion), channel_id=1, source_target_pairs={{0,2},{1,3},{2,0},{3,1},{4,6},{5,7},{6,4},{7,5},{8,10},{9,11},{10,... | collective-permute-start | bytes 737288 | tf_op jit(solution)/shard_map/ppermute | solution.py:483
  41.0 16.0 %collective-permute-start.12 = (bf16[48,1280]{1,0:T(8,128)(2,1)S(1)}, bf16[48,1280]{1,0:T(8,128)(2,1)S(1)}, u32[]{:S(2)}, u32[]{:S(2)}) collective-permute-start(bf16[48,1280]{1,0:T(8,128)(2,1)S(1)} %add_convert_fusion.3), channel_id=1, source_target_pairs={{0,2},{1,3},{2,0},{3,1},{4,6},{5,7},{6,4},{7,5},{8,10},{9,11},{10,... | collective-permute-start | bytes 368648 | tf_op jit(solution)/shard_map/ppermute | solution.py:483
